TPU v7x, 768 devices: a whole 4x8x12 slice. The times are simulated.
768 devices in a mesh: face: 12 (over z), tile: 64 (over x, y, core).
Axes of the slice: x: 4, y: 8, z: 12, core: 2. Of those that a mesh axis runs over, the one named last changes fastest.
Arguments:
- tracers: float32 [48, 256, 16, 1280], P('face', 'tile'), may hold values from -6 to 6
- basis_weights: float32 [2, 48, 256, 16, 16], P(None, 'face', 'tile'), may hold values from -1 to 1
- up_owner: int32 [2, 48, 256], P(None, 'face', 'tile'), may hold values from 0 to 4, as said below
- up_slot: int32 [2, 48, 256], P(None, 'face', 'tile'), may hold values from 0 to 15, as said below
- send_list: int32 [2, 48, 256], replicated, may hold values from 0 to 15, as said below
Outputs:
- transported: float32 [48, 256, 16, 1280], P('face', 'tile')
Inputs may be any that keep to these rules, and one draw needn't show every extreme that they name: `up_owner`: 0: the upstream element is on the same device; 1 and 2: on the device before or after along face, cyclically; 3 and 4: before or after along tile. On one device in one step, each position of each neighbour's list toward it is named by at most one target element, and a device names positions 0 to k - 1 of a list, k between 1 and 4, with 4 reached in every draw. `up_slot`: below 4 where up_owner is not 0. `send_list`: entry [s, 4 f + j, 4 t + c] is the c-th local element that device (f, t) lists in step s for direction j (j = 0: toward face + 1, 1: toward face - 1, 2: toward tile + 1, 3: toward tile - 1); the entries of one list are distinct.
All inputs are finite; a program needn't handle non-finite values.
Results may differ from a plain program's by a relative error of at most 0.0001.
Values sent between devices are 32-bit elements; how exact they have to be, the bound alone decides.
No kernel may reach another device: no remote copies, remote signals or barrier semaphores. Data moves between devices by JAX's collectives and lax.ppermute only.
A program may use at most 64 MiB of HBM per device.

v0:
```python
import jax
import jax.numpy as jnp
from jax import lax
from jax.sharding import PartitionSpec as P


def with_halo(block, sides, width):
    for axis, dim in sides:
        count = lax.axis_size(axis)
        forward = [(i, i + 1) for i in range(count - 1)]
        forward.append((count - 1, 0))
        backward = [(target, source) for source, target in forward]
        low = lax.ppermute(
            lax.slice_in_dim(block, block.shape[dim] - width, None, axis=dim), axis, forward
        )
        high = lax.ppermute(lax.slice_in_dim(block, 0, width, axis=dim), axis, backward)
        block = jnp.concatenate([low, block, high], axis=dim)
    return block


def interpolate(weights, source):
    interpolated = jnp.einsum("eij,ejc->eic", weights, source, precision=lax.Precision.HIGHEST)
    return jnp.clip(
        interpolated, jnp.min(source, axis=1, keepdims=True), jnp.max(source, axis=1, keepdims=True)
    )


def average_edges(interpolated):
    elem_side = interpolated.shape[0]
    columns = interpolated.shape[3]
    node_side = 4 * elem_side
    node_grid = interpolated.reshape(elem_side, elem_side, 4, 4, columns).transpose(0, 2, 1, 3, 4)
    node_grid = node_grid.reshape(node_side, node_side, columns)
    padded = with_halo(node_grid, (("face", 0), ("tile", 1)), 1)
    node_pos = jnp.arange(node_side, dtype=jnp.int32) % 4
    at_first = (node_pos == 0)[:, None, None]
    at_last = (node_pos == 3)[:, None, None]
    center = padded[1:-1]
    row_pass = jnp.where(
        at_first,
        0.5 * (center + padded[:-2]),
        jnp.where(at_last, 0.5 * (center + padded[2:]), center),
    )
    col_first = (node_pos == 0)[None, :, None]
    col_last = (node_pos == 3)[None, :, None]
    middle = row_pass[:, 1:-1]
    col_pass = jnp.where(
        col_first,
        0.5 * (middle + row_pass[:, :-2]),
        jnp.where(col_last, 0.5 * (middle + row_pass[:, 2:]), middle),
    )
    col_pass = col_pass.reshape(elem_side, 4, elem_side, 4, columns).transpose(0, 2, 1, 3, 4)
    return col_pass.reshape(elem_side, elem_side, 16, columns)


def local(tracers, basis_weights, up_owner, up_slot, send_list):
    elem_side = tracers.shape[0]
    elem_count = elem_side * elem_side
    columns = tracers.shape[3]
    tile_count = lax.axis_size("tile")
    list_cap = send_list.shape[2] // tile_count
    face_index = lax.axis_index("face")
    tile_index = lax.axis_index("tile")
    tracer_field = tracers
    for sweep_index in range(basis_weights.shape[0]):
        owners = up_owner[sweep_index].reshape(elem_count)
        slot_index = up_slot[sweep_index].reshape(elem_count)
        sender_lists = send_list[sweep_index]
        flat_blocks = tracer_field.reshape(elem_count, 16, columns)
        own_list = lax.dynamic_slice(
            sender_lists, (face_index * 4, tile_index * list_cap), (4, list_cap)
        )
        picked = flat_blocks[own_list.reshape(4 * list_cap)].reshape(4, list_cap, 16, columns)
        face_pair = jnp.stack([picked[1], picked[0]])
        tile_pair = jnp.stack([picked[3], picked[2]])
        from_face = with_halo(face_pair, (("face", 0),), 1)
        from_tile = with_halo(tile_pair, (("tile", 0),), 1)
        gathered = jnp.concatenate(
            [flat_blocks, from_face[0], from_face[3], from_tile[0], from_tile[3]], axis=0
        )
        source_index = jnp.where(
            owners == 0, slot_index, elem_count + (owners - 1) * list_cap + slot_index
        )
        source = gathered[source_index]
        weights = basis_weights[sweep_index].reshape(elem_count, 16, 16)
        interpolated = interpolate(weights, source)
        tracer_field = average_edges(interpolated.reshape(elem_side, elem_side, 16, columns))
    return tracer_field


def solution(mesh):
    return jax.shard_map(
        local,
        mesh=mesh,
        in_specs=(
            P("face", "tile", None, None),
            P(None, "face", "tile", None, None),
            P(None, "face", "tile"),
            P(None, "face", "tile"),
            P(),
        ),
        out_specs=P("face", "tile", None, None),
        check_vma=False,
    )
```

profile of v0, /device:TPU:63, one launch (start us, length us, event | category | flops | bytes accessed | tf_op | source)
XLA Modules:
  0.0 118.7 jit_solution(15797868156317487892)
XLA Ops:
  1.0 1.9 %gather_fusion = f32[16,16,1280]{2,1,0:T(8,128)S(1)} fusion(f32[16,16,1280]{2,1,0:T(8,128)} %bitcast.62, s32[1024]{0:T(1024)S(1)} %pad_clamp_fusion.3), kind=kCustom, calls=%fused_computation | custom fusion | bytes 2621504 | tf_op jit(solution)/shard_map/gather | solution.py:73
  3.9 4.0 %collective-permute-start = (f32[1,4,16,1280]{3,2,1,0:T(8,128)}, f32[1,4,16,1280]{3,2,1,0:T(8,128)S(1)}, u32[]{:S(2)}, u32[]{:S(2)}) collective-permute-start(f32[1,4,16,1280]{3,2,1,0:T(8,128)} %get-tuple-element.24), channel_id=1, source_target_pairs={{0,64},{64,128},{128,192},{192,256},{256,320},{320,384},{384,448},... | collective-permute-start | bytes 983048 | tf_op jit(solution)/shard_map/ppermute | solution.py:13
  7.9 12.2 %collective-permute-start.1 = (f32[1,4,16,1280]{3,2,1,0:T(8,128)}, f32[1,4,16,1280]{3,2,1,0:T(8,128)S(1)}, u32[]{:S(2)}, u32[]{:S(2)}) collective-permute-start(f32[1,4,16,1280]{3,2,1,0:T(8,128)} %get-tuple-element.23), channel_id=1, source_target_pairs={{64,0},{128,64},{192,128},{256,192},{320,256},{384,320},{448,384},... | collective-permute-start | bytes 983048 | tf_op jit(solution)/shard_map/ppermute | solution.py:16
  20.2 2.2 %collective-permute-start.2 = (f32[1,4,16,1280]{3,2,1,0:T(8,128)S(1)}, f32[1,4,16,1280]{3,2,1,0:T(8,128)S(1)}, u32[]{:S(2)}, u32[]{:S(2)}) collective-permute-start(f32[1,4,16,1280]{3,2,1,0:T(8,128)S(1)} %get-tuple-element.22), channel_id=1, source_target_pairs={{0,1},{1,2},{2,3},{3,4},{4,5},{5,6},{6,7},{7,8},{8,9},{9,10},{10,1... | collective-permute-start | bytes 983048 | tf_op jit(solution)/shard_map/ppermute | solution.py:13
  22.3 2.6 %collective-permute-start.3 = (f32[1,4,16,1280]{3,2,1,0:T(8,128)S(1)}, f32[1,4,16,1280]{3,2,1,0:T(8,128)S(1)}, u32[]{:S(2)}, u32[]{:S(2)}) collective-permute-start(f32[1,4,16,1280]{3,2,1,0:T(8,128)S(1)} %get-tuple-element.21), channel_id=1, source_target_pairs={{1,0},{2,1},{3,2},{4,3},{5,4},{6,5},{7,6},{8,7},{9,8},{10,9},{11,1... | collective-permute-start | bytes 983048 | tf_op jit(solution)/shard_map/ppermute | solution.py:16
  35.6 2.4 %gather_fusion.1 = f32[16,16,1280]{2,1,0:T(8,128)S(1)} fusion(f32[32,16,1280]{2,1,0:T(8,128)} %bitcast_dynamic-update-slice_fusion.4, s32[1024]{0:T(1024)S(1)} %pad_clamp_fusion.2), kind=kCustom, calls=%fused_computation.1 | custom fusion | bytes 2621504 | tf_op jit(solution)/shard_map/gather | solution.py:84
  40.7 1.9 %collective-permute-start.4 = (f32[1,16,1280]{2,1,0:T(8,128)S(1)}, f32[1,16,1280]{2,1,0:T(8,128)S(1)}, u32[]{:S(2)}, u32[]{:S(2)}) collective-permute-start(f32[1,16,1280]{2,1,0:T(8,128)S(1)} %get-tuple-element.20), channel_id=1, source_target_pairs={{0,64},{64,128},{128,192},{192,256},{256,320},{320,384},{384,448},... | collective-permute-start | bytes 245768 | tf_op jit(solution)/shard_map/ppermute | solution.py:13
  42.6 4.6 %collective-permute-start.5 = (f32[1,16,1280]{2,1,0:T(8,128)S(1)}, f32[1,16,1280]{2,1,0:T(8,128)S(1)}, u32[]{:S(2)}, u32[]{:S(2)}) collective-permute-start(f32[1,16,1280]{2,1,0:T(8,128)S(1)} %get-tuple-element.19), channel_id=1, source_target_pairs={{64,0},{128,64},{192,128},{256,192},{320,256},{384,320},{448,384},... | collective-permute-start | bytes 245768 | tf_op jit(solution)/shard_map/ppermute | solution.py:16
  47.3 1.3 %collective-permute-done.5 = f32[1,16,1280]{2,1,0:T(8,128)S(1)} collective-permute-done((f32[1,16,1280]{2,1,0:T(8,128)S(1)}, f32[1,16,1280]{2,1,0:T(8,128)S(1)}, u32[]{:S(2)}, u32[]{:S(2)}) %collective-permute-start.5) | collective-permute-done | bytes 81952 | tf_op jit(solution)/shard_map/ppermute | solution.py:16
  48.8 7.4 %collective-permute-start.6 = (f32[18,1,1280]{2,1,0:T(1,128)S(1)}, f32[18,1,1280]{2,1,0:T(1,128)S(1)}, u32[]{:S(2)}, u32[]{:S(2)}) collective-permute-start(f32[18,1,1280]{2,1,0:T(1,128)S(1)} %get-tuple-element.11), channel_id=1, source_target_pairs={{0,1},{1,2},{2,3},{3,4},{4,5},{5,6},{6,7},{7,8},{8,9},{9,10},{10,1... | collective-permute-start | bytes 276488 | tf_op jit(solution)/shard_map/ppermute | solution.py:13
  56.2 1.9 %collective-permute-start.7 = (f32[18,1,1280]{2,1,0:T(1,128)S(1)}, f32[18,1,1280]{2,1,0:T(1,128)S(1)}, u32[]{:S(2)}, u32[]{:S(2)}) collective-permute-start(f32[18,1,1280]{2,1,0:T(1,128)S(1)} %get-tuple-element.12), channel_id=1, source_target_pairs={{1,0},{2,1},{3,2},{4,3},{5,4},{6,5},{7,6},{8,7},{9,8},{10,9},{11,1... | collective-permute-start | bytes 276488 | tf_op jit(solution)/shard_map/ppermute | solution.py:16
  58.1 7.2 %collective-permute-done.7 = f32[18,1,1280]{2,1,0:T(1,128)S(1)} collective-permute-done((f32[18,1,1280]{2,1,0:T(1,128)S(1)}, f32[18,1,1280]{2,1,0:T(1,128)S(1)}, u32[]{:S(2)}, u32[]{:S(2)}) %collective-permute-start.7) | collective-permute-done | bytes 92192 | tf_op jit(solution)/shard_map/ppermute | solution.py:16
  68.3 1.9 %collective-permute-start.8 = (f32[1,4,16,1280]{3,2,1,0:T(8,128)S(1)}, f32[1,4,16,1280]{3,2,1,0:T(8,128)S(1)}, u32[]{:S(2)}, u32[]{:S(2)}) collective-permute-start(f32[1,4,16,1280]{3,2,1,0:T(8,128)S(1)} %get-tuple-element.18), channel_id=1, source_target_pairs={{0,64},{64,128},{128,192},{192,256},{256,320},{320,384},{384,448},... | collective-permute-start | bytes 983048 | tf_op jit(solution)/shard_map/ppermute | solution.py:13
  70.3 5.2 %collective-permute-start.9 = (f32[1,4,16,1280]{3,2,1,0:T(8,128)S(1)}, f32[1,4,16,1280]{3,2,1,0:T(8,128)S(1)}, u32[]{:S(2)}, u32[]{:S(2)}) collective-permute-start(f32[1,4,16,1280]{3,2,1,0:T(8,128)S(1)} %get-tuple-element.17), channel_id=1, source_target_pairs={{64,0},{128,64},{192,128},{256,192},{320,256},{384,320},{448,384},... | collective-permute-start | bytes 983048 | tf_op jit(solution)/shard_map/ppermute | solution.py:16
  75.5 2.1 %collective-permute-start.10 = (f32[1,4,16,1280]{3,2,1,0:T(8,128)S(1)}, f32[1,4,16,1280]{3,2,1,0:T(8,128)S(1)}, u32[]{:S(2)}, u32[]{:S(2)}) collective-permute-start(f32[1,4,16,1280]{3,2,1,0:T(8,128)S(1)} %get-tuple-element.16), channel_id=1, source_target_pairs={{0,1},{1,2},{2,3},{3,4},{4,5},{5,6},{6,7},{7,8},{8,9},{9,10},{10,1... | collective-permute-start | bytes 983048 | tf_op jit(solution)/shard_map/ppermute | solution.py:13
  77.6 2.2 %collective-permute-start.11 = (f32[1,4,16,1280]{3,2,1,0:T(8,128)S(1)}, f32[1,4,16,1280]{3,2,1,0:T(8,128)S(1)}, u32[]{:S(2)}, u32[]{:S(2)}) collective-permute-start(f32[1,4,16,1280]{3,2,1,0:T(8,128)S(1)} %get-tuple-element.15), channel_id=1, source_target_pairs={{1,0},{2,1},{3,2},{4,3},{5,4},{6,5},{7,6},{8,7},{9,8},{10,9},{11,1... | collective-permute-start | bytes 983048 | tf_op jit(solution)/shard_map/ppermute | solution.py:16
  83.3 6.1 %collective-permute-done.11 = f32[1,4,16,1280]{3,2,1,0:T(8,128)S(1)} collective-permute-done((f32[1,4,16,1280]{3,2,1,0:T(8,128)S(1)}, f32[1,4,16,1280]{3,2,1,0:T(8,128)S(1)}, u32[]{:S(2)}, u32[]{:S(2)}) %collective-permute-start.11) | collective-permute-done | bytes 327712 | tf_op jit(solution)/shard_map/ppermute | solution.py:16
  90.1 2.4 %gather_fusion.3 = f32[16,16,1280]{2,1,0:T(8,128)S(1)} fusion(f32[32,16,1280]{2,1,0:T(8,128)} %bitcast_dynamic-update-slice_fusion, s32[1024]{0:T(1024)S(1)} %pad_clamp_fusion), kind=kCustom, calls=%fused_computation.3 | custom fusion | bytes 2621504 | tf_op jit(solution)/shard_map/gather | solution.py:84
  95.2 1.9 %collective-permute-start.12 = (f32[1,16,1280]{2,1,0:T(8,128)S(1)}, f32[1,16,1280]{2,1,0:T(8,128)S(1)}, u32[]{:S(2)}, u32[]{:S(2)}) collective-permute-start(f32[1,16,1280]{2,1,0:T(8,128)S(1)} %get-tuple-element.14), channel_id=1, source_target_pairs={{0,64},{64,128},{128,192},{192,256},{256,320},{320,384},{384,448},... | collective-permute-start | bytes 245768 | tf_op jit(solution)/shard_map/ppermute | solution.py:13
  97.1 4.6 %collective-permute-start.13 = (f32[1,16,1280]{2,1,0:T(8,128)S(1)}, f32[1,16,1280]{2,1,0:T(8,128)S(1)}, u32[]{:S(2)}, u32[]{:S(2)}) collective-permute-start(f32[1,16,1280]{2,1,0:T(8,128)S(1)} %get-tuple-element.13), channel_id=1, source_target_pairs={{64,0},{128,64},{192,128},{256,192},{320,256},{384,320},{448,384},... | collective-permute-start | bytes 245768 | tf_op jit(solution)/shard_map/ppermute | solution.py:16
  101.9 1.3 %collective-permute-done.13 = f32[1,16,1280]{2,1,0:T(8,128)S(1)} collective-permute-done((f32[1,16,1280]{2,1,0:T(8,128)S(1)}, f32[1,16,1280]{2,1,0:T(8,128)S(1)}, u32[]{:S(2)}, u32[]{:S(2)}) %collective-permute-start.13) | collective-permute-done | bytes 81952 | tf_op jit(solution)/shard_map/ppermute | solution.py:16
  103.3 2.9 %collective-permute-start.14 = (f32[18,1,1280]{2,1,0:T(1,128)S(1)}, f32[18,1,1280]{2,1,0:T(1,128)S(1)}, u32[]{:S(2)}, u32[]{:S(2)}) collective-permute-start(f32[18,1,1280]{2,1,0:T(1,128)S(1)} %get-tuple-element.9), channel_id=1, source_target_pairs={{0,1},{1,2},{2,3},{3,4},{4,5},{5,6},{6,7},{7,8},{8,9},{9,10},{10,1... | collective-permute-start | bytes 276488 | tf_op jit(solution)/shard_map/ppermute | solution.py:13
  106.2 1.9 %collective-permute-start.15 = (f32[18,1,1280]{2,1,0:T(1,128)S(1)}, f32[18,1,1280]{2,1,0:T(1,128)S(1)}, u32[]{:S(2)}, u32[]{:S(2)}) collective-permute-start(f32[18,1,1280]{2,1,0:T(1,128)S(1)} %get-tuple-element.10), channel_id=1, source_target_pairs={{1,0},{2,1},{3,2},{4,3},{5,4},{6,5},{7,6},{8,7},{9,8},{10,9},{11,1... | collective-permute-start | bytes 276488 | tf_op jit(solution)/shard_map/ppermute | solution.py:16
  108.2 7.3 %collective-permute-done.15 = f32[18,1,1280]{2,1,0:T(1,128)S(1)} collective-permute-done((f32[18,1,1280]{2,1,0:T(1,128)S(1)}, f32[18,1,1280]{2,1,0:T(1,128)S(1)}, u32[]{:S(2)}, u32[]{:S(2)}) %collective-permute-start.15) | collective-permute-done | bytes 92192 | tf_op jit(solution)/shard_map/ppermute | solution.py:16
  (86 shorter events, 28.8 us)
Async XLA Ops:
  3.0 22.0 %copy-start.1 = (s32[2,4,4]{2,1,0:T(4,128)S(1)}, s32[2,4,4]{2,1,0:T(4,128)}, u32[]{:S(2)}) copy-start(s32[2,4,4]{2,1,0:T(4,128)} %param.7) | copy-start | bytes 388
  3.0 22.6 %copy-start.2 = (s32[2,4,4]{2,1,0:T(4,128)S(1)}, s32[2,4,4]{2,1,0:T(4,128)}, u32[]{:S(2)}) copy-start(s32[2,4,4]{2,1,0:T(4,128)} %param.8) | copy-start | bytes 388
  3.0 28.4 %copy-start = (f32[4,4,16,1280]{3,2,1,0:T(8,128)S(1)}, f32[4,4,16,1280]{3,2,1,0:T(8,128)}, u32[]{:S(2)}) copy-start(f32[4,4,16,1280]{3,2,1,0:T(8,128)} %param.5) | copy-start | bytes 3932164
  3.9 28.6 %collective-permute-start = (f32[1,4,16,1280]{3,2,1,0:T(8,128)}, f32[1,4,16,1280]{3,2,1,0:T(8,128)S(1)}, u32[]{:S(2)}, u32[]{:S(2)}) collective-permute-start(f32[1,4,16,1280]{3,2,1,0:T(8,128)} %get-tuple-element.24), channel_id=1, source_target_pairs={{0,64},{64,128},{128,192},{192,256},{256,320},{320,384},{384,448},... | collective-permute-start | bytes 983048 | tf_op jit(solution)/shard_map/ppermute | solution.py:13
  7.9 25.4 %collective-permute-start.1 = (f32[1,4,16,1280]{3,2,1,0:T(8,128)}, f32[1,4,16,1280]{3,2,1,0:T(8,128)S(1)}, u32[]{:S(2)}, u32[]{:S(2)}) collective-permute-start(f32[1,4,16,1280]{3,2,1,0:T(8,128)} %get-tuple-element.23), channel_id=1, source_target_pairs={{64,0},{128,64},{192,128},{256,192},{320,256},{384,320},{448,384},... | collective-permute-start | bytes 983048 | tf_op jit(solution)/shard_map/ppermute | solution.py:16
  20.2 13.9 %collective-permute-start.2 = (f32[1,4,16,1280]{3,2,1,0:T(8,128)S(1)}, f32[1,4,16,1280]{3,2,1,0:T(8,128)S(1)}, u32[]{:S(2)}, u32[]{:S(2)}) collective-permute-start(f32[1,4,16,1280]{3,2,1,0:T(8,128)S(1)} %get-tuple-element.22), channel_id=1, source_target_pairs={{0,1},{1,2},{2,3},{3,4},{4,5},{5,6},{6,7},{7,8},{8,9},{9,10},{10,1... | collective-permute-start | bytes 983048 | tf_op jit(solution)/shard_map/ppermute | solution.py:13
  22.3 12.5 %collective-permute-start.3 = (f32[1,4,16,1280]{3,2,1,0:T(8,128)S(1)}, f32[1,4,16,1280]{3,2,1,0:T(8,128)S(1)}, u32[]{:S(2)}, u32[]{:S(2)}) collective-permute-start(f32[1,4,16,1280]{3,2,1,0:T(8,128)S(1)} %get-tuple-element.21), channel_id=1, source_target_pairs={{1,0},{2,1},{3,2},{4,3},{5,4},{6,5},{7,6},{8,7},{9,8},{10,9},{11,1... | collective-permute-start | bytes 983048 | tf_op jit(solution)/shard_map/ppermute | solution.py:16
  40.7 6.5 %collective-permute-start.4 = (f32[1,16,1280]{2,1,0:T(8,128)S(1)}, f32[1,16,1280]{2,1,0:T(8,128)S(1)}, u32[]{:S(2)}, u32[]{:S(2)}) collective-permute-start(f32[1,16,1280]{2,1,0:T(8,128)S(1)} %get-tuple-element.20), channel_id=1, source_target_pairs={{0,64},{64,128},{128,192},{192,256},{256,320},{320,384},{384,448},... | collective-permute-start | bytes 245768 | tf_op jit(solution)/shard_map/ppermute | solution.py:13
  42.6 6.0 %collective-permute-start.5 = (f32[1,16,1280]{2,1,0:T(8,128)S(1)}, f32[1,16,1280]{2,1,0:T(8,128)S(1)}, u32[]{:S(2)}, u32[]{:S(2)}) collective-permute-start(f32[1,16,1280]{2,1,0:T(8,128)S(1)} %get-tuple-element.19), channel_id=1, source_target_pairs={{64,0},{128,64},{192,128},{256,192},{320,256},{384,320},{448,384},... | collective-permute-start | bytes 245768 | tf_op jit(solution)/shard_map/ppermute | solution.py:16
  48.8 9.3 %collective-permute-start.6 = (f32[18,1,1280]{2,1,0:T(1,128)S(1)}, f32[18,1,1280]{2,1,0:T(1,128)S(1)}, u32[]{:S(2)}, u32[]{:S(2)}) collective-permute-start(f32[18,1,1280]{2,1,0:T(1,128)S(1)} %get-tuple-element.11), channel_id=1, source_target_pairs={{0,1},{1,2},{2,3},{3,4},{4,5},{5,6},{6,7},{7,8},{8,9},{9,10},{10,1... | collective-permute-start | bytes 276488 | tf_op jit(solution)/shard_map/ppermute | solution.py:13
  56.2 9.2 %collective-permute-start.7 = (f32[18,1,1280]{2,1,0:T(1,128)S(1)}, f32[18,1,1280]{2,1,0:T(1,128)S(1)}, u32[]{:S(2)}, u32[]{:S(2)}) collective-permute-start(f32[18,1,1280]{2,1,0:T(1,128)S(1)} %get-tuple-element.12), channel_id=1, source_target_pairs={{1,0},{2,1},{3,2},{4,3},{5,4},{6,5},{7,6},{8,7},{9,8},{10,9},{11,1... | collective-permute-start | bytes 276488 | tf_op jit(solution)/shard_map/ppermute | solution.py:16
  68.3 12.7 %collective-permute-start.8 = (f32[1,4,16,1280]{3,2,1,0:T(8,128)S(1)}, f32[1,4,16,1280]{3,2,1,0:T(8,128)S(1)}, u32[]{:S(2)}, u32[]{:S(2)}) collective-permute-start(f32[1,4,16,1280]{3,2,1,0:T(8,128)S(1)} %get-tuple-element.18), channel_id=1, source_target_pairs={{0,64},{64,128},{128,192},{192,256},{256,320},{320,384},{384,448},... | collective-permute-start | bytes 983048 | tf_op jit(solution)/shard_map/ppermute | solution.py:13
  70.3 11.5 %collective-permute-start.9 = (f32[1,4,16,1280]{3,2,1,0:T(8,128)S(1)}, f32[1,4,16,1280]{3,2,1,0:T(8,128)S(1)}, u32[]{:S(2)}, u32[]{:S(2)}) collective-permute-start(f32[1,4,16,1280]{3,2,1,0:T(8,128)S(1)} %get-tuple-element.17), channel_id=1, source_target_pairs={{64,0},{128,64},{192,128},{256,192},{320,256},{384,320},{448,384},... | collective-permute-start | bytes 983048 | tf_op jit(solution)/shard_map/ppermute | solution.py:16
  75.5 7.0 %collective-permute-start.10 = (f32[1,4,16,1280]{3,2,1,0:T(8,128)S(1)}, f32[1,4,16,1280]{3,2,1,0:T(8,128)S(1)}, u32[]{:S(2)}, u32[]{:S(2)}) collective-permute-start(f32[1,4,16,1280]{3,2,1,0:T(8,128)S(1)} %get-tuple-element.16), channel_id=1, source_target_pairs={{0,1},{1,2},{2,3},{3,4},{4,5},{5,6},{6,7},{7,8},{8,9},{9,10},{10,1... | collective-permute-start | bytes 983048 | tf_op jit(solution)/shard_map/ppermute | solution.py:13
  77.6 11.7 %collective-permute-start.11 = (f32[1,4,16,1280]{3,2,1,0:T(8,128)S(1)}, f32[1,4,16,1280]{3,2,1,0:T(8,128)S(1)}, u32[]{:S(2)}, u32[]{:S(2)}) collective-permute-start(f32[1,4,16,1280]{3,2,1,0:T(8,128)S(1)} %get-tuple-element.15), channel_id=1, source_target_pairs={{1,0},{2,1},{3,2},{4,3},{5,4},{6,5},{7,6},{8,7},{9,8},{10,9},{11,1... | collective-permute-start | bytes 983048 | tf_op jit(solution)/shard_map/ppermute | solution.py:16
  95.2 6.5 %collective-permute-start.12 = (f32[1,16,1280]{2,1,0:T(8,128)S(1)}, f32[1,16,1280]{2,1,0:T(8,128)S(1)}, u32[]{:S(2)}, u32[]{:S(2)}) collective-permute-start(f32[1,16,1280]{2,1,0:T(8,128)S(1)} %get-tuple-element.14), channel_id=1, source_target_pairs={{0,64},{64,128},{128,192},{192,256},{256,320},{320,384},{384,448},... | collective-permute-start | bytes 245768 | tf_op jit(solution)/shard_map/ppermute | solution.py:13
  97.1 6.0 %collective-permute-start.13 = (f32[1,16,1280]{2,1,0:T(8,128)S(1)}, f32[1,16,1280]{2,1,0:T(8,128)S(1)}, u32[]{:S(2)}, u32[]{:S(2)}) collective-permute-start(f32[1,16,1280]{2,1,0:T(8,128)S(1)} %get-tuple-element.13), channel_id=1, source_target_pairs={{64,0},{128,64},{192,128},{256,192},{320,256},{384,320},{448,384},... | collective-permute-start | bytes 245768 | tf_op jit(solution)/shard_map/ppermute | solution.py:16
  103.3 4.8 %collective-permute-start.14 = (f32[18,1,1280]{2,1,0:T(1,128)S(1)}, f32[18,1,1280]{2,1,0:T(1,128)S(1)}, u32[]{:S(2)}, u32[]{:S(2)}) collective-permute-start(f32[18,1,1280]{2,1,0:T(1,128)S(1)} %get-tuple-element.9), channel_id=1, source_target_pairs={{0,1},{1,2},{2,3},{3,4},{4,5},{5,6},{6,7},{7,8},{8,9},{9,10},{10,1... | collective-permute-start | bytes 276488 | tf_op jit(solution)/shard_map/ppermute | solution.py:13
  106.2 9.2 %collective-permute-start.15 = (f32[18,1,1280]{2,1,0:T(1,128)S(1)}, f32[18,1,1280]{2,1,0:T(1,128)S(1)}, u32[]{:S(2)}, u32[]{:S(2)}) collective-permute-start(f32[18,1,1280]{2,1,0:T(1,128)S(1)} %get-tuple-element.10), channel_id=1, source_target_pairs={{1,0},{2,1},{3,2},{4,3},{5,4},{6,5},{7,6},{8,7},{9,8},{10,9},{11,1... | collective-permute-start | bytes 276488 | tf_op jit(solution)/shard_map/ppermute | solution.py:16
where the time goes:
time: 119 us
  starting transfers between devices  59.6 us (50%)
  local copies, waits for them, and re-layouts  26.4 us (22%)
  waiting for transfers between devices  23.3 us (20%)
  other arithmetic  6.41 us (5%)
  matrix products  2.58 us (2%)
    ppermute x8, starting transfers between devices, with_halo(): lax.ppermute(lax.slice_in_dim(block, 0, width, axis=dim), axis, backward)  35.3 us
    ppermute x8, starting transfers between devices, with_halo(): lax.ppermute(lax.slice_in_dim(block, block.shape[dim] - width, None, axis...  24.3 us
    ppermute x8, waiting for transfers between devices, with_halo(): lax.ppermute(lax.slice_in_dim(block, 0, width, axis=dim), axis, backward)  23.2 us
    unnamed x18, local copies, waits for them, and re-layouts  7.06 us
    gather x2, local copies, waits for them, and re-layouts, local(): source = gathered[source_index]  4.74 us
    gather x2, local copies, waits for them, and re-layouts, local(): flat_blocks[own_list.reshape(4 * list_cap)]  2.58 us
    dot_general x2, matrix products, interpolate(): jnp.einsum('eij,ejc->eic', weights, source, precision=lax.Precision.HIGHEST)  2.58 us
  transfers between devices with their start and end apart: 16, of which 5 were waited for; matrix products, arithmetic and copies ran while one was open for 11% of the time, Pallas kernels for 0%

commit v1 on v0

v1 whole, which is shorter than its diff:
```python
import functools

import jax
import jax.numpy as jnp
from jax import lax
from jax.experimental import pallas as pl
from jax.experimental.pallas import tpu as pltpu
from jax.sharding import PartitionSpec as P

F32 = jnp.float32
BF16 = jnp.bfloat16
VMEM = pl.BlockSpec(memory_space=pltpu.VMEM)
SMEM = pl.BlockSpec(memory_space=pltpu.SMEM)
HBM = pl.BlockSpec(memory_space=pltpu.HBM)
ELEMS = 16
NODES = 16
CAP = 4


def cost(cycles_bytes):
    return pl.CostEstimate(flops=0, transcendentals=0, bytes_accessed=cycles_bytes)


def grant(mib):
    return pltpu.CompilerParams(vmem_limit_bytes=mib << 20)


def list_copy(step, lists, table, sem):
    rows, cols = table.shape
    row = lax.axis_index("face") * 4
    col = lax.axis_index("tile") * CAP
    row0, col0 = lax.div(row, rows) * rows, lax.div(col, cols) * cols
    copy = pltpu.make_async_copy(
        lists.at[step, pl.ds(pl.multiple_of(row0, rows), rows), pl.ds(pl.multiple_of(col0, cols), cols)],
        table,
        sem,
    )
    return copy, row - row0, col - col0


def directions():
    return odd("face"), 1 - odd("face"), 2 + odd("tile"), 3 - odd("tile")


def first_gather(lists, field, *rest):
    sends, (table, list_sem, sems) = rest[:4], rest[4:]
    copy, row, col = list_copy(0, lists, table, list_sem)
    copy.start()
    copy.wait()
    copies = []
    for k, j in enumerate(directions()):
        for c in range(CAP):
            copies.append(
                pltpu.make_async_copy(
                    field.at[table[row + j, col + c]], sends[k].at[c], sems.at[k * CAP + c]
                )
            )
            copies[-1].start()
    for copy in copies:
        copy.wait()


def spread_weights(weights, high, low):
    lane = lax.broadcasted_iota(jnp.int32, (16, 256), 1)
    row = lax.broadcasted_iota(jnp.int32, (16, 256), 0)
    spread = jnp.where(lane % 16 == row, 1.0, 0.0).astype(BF16)
    out_row = lax.broadcasted_iota(jnp.int32, (256, 256), 0)
    out_col = lax.broadcasted_iota(jnp.int32, (256, 256), 1)
    own = out_row // 16 == out_col // 16
    for step in range(weights.shape[0]):
        w = weights[step]
        w_high = w.astype(BF16)
        w_low = (w - w_high.astype(F32)).astype(BF16)
        for part, out in ((w_high, high), (w_low, low)):
            wide = jnp.dot(part, spread, preferred_element_type=F32)
            out[step] = jnp.where(own, wide, 0.0).astype(BF16)


def sublane(shape=(8, 1)):
    return lax.broadcasted_iota(jnp.int32, shape, 0)


def roll(x, by):
    return x if by % 8 == 0 else pltpu.roll(x, by % 8, 0)


def move(step, owner, slot, field, face_first, face_second, tile_first, tile_second, high, low,
         moved, row_first, row_second, source, split_high, split_low):
    owners = (2 - odd("face"), 1 + odd("face"), 4 - odd("tile"), 3 + odd("tile"))
    for e in range(ELEMS):
        o = owner[step, e // 4, e % 4]
        p = slot[step, e // 4, e % 4]
        c = jnp.minimum(p, CAP - 1)
        block = field[p]
        for code, arrived in zip(owners, (face_first, face_second, tile_first, tile_second)):
            block = jnp.where(o == code, arrived[c], block)
        source[e] = block
        part = block.astype(BF16)
        split_high[pl.ds(e * 16, 16), :] = part
        split_low[pl.ds(e * 16, 16), :] = (block - part.astype(F32)).astype(BF16)
    wide = 256
    for n in range(0, field.shape[2], wide):
        cols = pl.ds(n, wide)
        s_high, s_low = split_high[:, cols], split_low[:, cols]
        w_high, w_low = high[step], low[step]
        total = jnp.dot(w_high, s_high, preferred_element_type=F32)
        total += jnp.dot(w_high, s_low, preferred_element_type=F32)
        total += jnp.dot(w_low, s_high, preferred_element_type=F32)
        for e in range(ELEMS):
            src = source[e, :, cols]
            least = jnp.min(src, axis=0, keepdims=True)
            most = jnp.max(src, axis=0, keepdims=True)
            moved[e, :, cols] = jnp.clip(total[e * 16 : e * 16 + 16], least, most)
    sub = sublane()
    packed = []
    for x, tile in ((0, 0), (3, 1)):
        rows = []
        for pair in range(2):
            even = moved[4 * x + 2 * pair, 8 * tile : 8 * tile + 8, :]
            after = moved[4 * x + 2 * pair + 1, 8 * tile : 8 * tile + 8, :]
            if tile == 0:
                rows.append(jnp.where(sub < 4, even, roll(after, 4)))
            else:
                rows.append(jnp.where(sub < 4, roll(even, 4), after))
        left, right = rows
        inner = []
        for t in rows:
            t2 = jnp.where(sub == 3, 0.5 * (t + roll(t, 7)), t)
            inner.append(jnp.where(sub == 4, 0.5 * (t + roll(t, 1)), t2))
        inner[0] = jnp.where(sub == 7, 0.5 * (left + roll(right, 7)), inner[0])
        inner[1] = jnp.where(sub == 0, 0.5 * (right + roll(left, 1)), inner[1])
        packed.append(inner)
    flip = odd("face") == 1
    for k in range(2):
        rows = slice(8 * k, 8 * k + 8)
        top, bottom = packed[0][k], packed[1][k]
        row_first[rows, :] = jnp.where(flip, top, bottom)
        row_second[rows, :] = jnp.where(flip, bottom, top)


def average_inside(moved, inside, left, right, draft):
    sub = sublane()
    first, last = sub % 4 == 0, sub % 4 == 3
    for e in range(ELEMS):
        y = e % 4
        for k in range(2):
            rows = slice(8 * k, 8 * k + 8)
            m = moved[e, rows, :]
            c = m
            if y < 3:
                c = jnp.where(last, 0.5 * (m + roll(moved[e + 1, rows, :], 3)), c)
            if y > 0:
                c = jnp.where(first, 0.5 * (m + roll(moved[e - 1, rows, :], 5)), c)
            draft[e, rows, :] = c
    for e in range(ELEMS):
        x = e // 4
        t0, t1 = draft[e, 0:8, :], draft[e, 8:16, :]
        if x > 0:
            t0 = jnp.where(sub < 4, 0.5 * (t0 + roll(draft[e - 4, 8:16, :], 4)), t0)
        if x < 3:
            t1 = jnp.where(sub >= 4, 0.5 * (t1 + roll(draft[e + 4, 0:8, :], 4)), t1)
        inside[e, 0:8, :] = t0
        inside[e, 8:16, :] = t1
    for out, y, at in ((left, 0, 0), (right, 3, 3)):
        for pair in range(2):
            packed = None
            for place in range(4):
                e = 4 * (2 * pair + place // 2) + y
                k = place % 2
                t = roll(inside[e, 8 * k : 8 * k + 8, :], place - at)
                packed = t if packed is None else jnp.where(sub % 4 == place, t, packed)
            out[8 * pair : 8 * pair + 8, :] = packed


def finish_columns(left, right, face_first, face_second, column_first, column_second):
    sub = sublane()
    flip = odd("face") == 1
    lo, hi = slice(0, 8), slice(8, 16)
    a0, a1, b0, b1 = (
        jnp.where(flip == from_first, face_first[rows, :], face_second[rows, :])
        for from_first in (True, False)
        for rows in (lo, hi)
    )
    l0 = jnp.where(sub == 0, 0.5 * (left[lo, :] + a0), left[lo, :])
    l1 = jnp.where(sub == 7, 0.5 * (left[hi, :] + roll(b0, 7)), left[hi, :])
    r0 = jnp.where(sub == 0, 0.5 * (right[lo, :] + roll(a1, 1)), right[lo, :])
    r1 = jnp.where(sub == 7, 0.5 * (right[hi, :] + b1), right[hi, :])
    flip = odd("tile") == 1
    for rows, l, r in ((lo, l0, r0), (hi, l1, r1)):
        column_first[rows, :] = jnp.where(flip, l, r)
        column_second[rows, :] = jnp.where(flip, r, l)


def finish_rows(inside, face_first, face_second, out):
    sub = sublane()
    flip = odd("face") == 1
    out[4:12] = inside[4:12]
    for y in range(4):
        first = face_first[8 * (y // 2) : 8 * (y // 2) + 8, :]
        second = face_second[8 * (y // 2) : 8 * (y // 2) + 8, :]
        a, b = jnp.where(flip, first, second), jnp.where(flip, second, first)
        t = inside[y, 0:8, :]
        out[y, 0:8, :] = jnp.where(sub < 4, 0.5 * (t + roll(a, 4 * (y % 2))), t)
        out[y, 8:16, :] = inside[y, 8:16, :]
        out[12 + y, 0:8, :] = inside[12 + y, 0:8, :]
        t = inside[12 + y, 8:16, :]
        out[12 + y, 8:16, :] = jnp.where(sub >= 4, 0.5 * (t + roll(b, 4 - 4 * (y % 2))), t)


def fix_edges(inside, tile_first, tile_second, out):
    sub = sublane()
    first, last = sub % 4 == 0, sub % 4 == 3
    flip = odd("tile") == 1
    for x in range(4):
        one = tile_first[8 * (x // 2) : 8 * (x // 2) + 8, :]
        two = tile_second[8 * (x // 2) : 8 * (x // 2) + 8, :]
        before, after = jnp.where(flip, one, two), jnp.where(flip, two, one)
        out[4 * x + 1 : 4 * x + 3] = inside[4 * x + 1 : 4 * x + 3]
        for k in range(2):
            place = 2 * (x % 2) + k
            rows = slice(8 * k, 8 * k + 8)
            t = inside[4 * x, rows, :]
            out[4 * x, rows, :] = jnp.where(first, 0.5 * (t + roll(before, -place)), t)
            t = inside[4 * x + 3, rows, :]
            out[4 * x + 3, rows, :] = jnp.where(last, 0.5 * (t + roll(after, 3 - place)), t)


def finish_field(step, lists, inside, tile_first, tile_second, field, *rest):
    sends, (table, list_sem) = rest[:4], rest[4:]
    copy, row, col = list_copy(step + 1, lists, table, list_sem)
    copy.start()
    fix_edges(inside, tile_first, tile_second, field)
    copy.wait()
    for k, j in enumerate(directions()):
        for c in range(CAP):
            sends[k][c] = field[table[row + j, col + c]]


def finish_last(inside, tile_first, tile_second, field):
    fix_edges(inside, tile_first, tile_second, field)


def swap(axis, offset, x):
    count = lax.axis_size(axis)
    pairs = []
    for i in range(offset, count + offset, 2):
        pairs += [(i % count, (i + 1) % count), ((i + 1) % count, i % count)]
    return lax.ppermute(x, axis, sorted(pairs))


def swaps(axis, first, second):
    return swap(axis, 0, first), swap(axis, 1, second)


def odd(axis):
    return lax.rem(lax.axis_index(axis), 2)


def local(tracers, basis_weights, up_owner, up_slot, send_list):
    columns = tracers.shape[3]
    steps = basis_weights.shape[0]
    block = jax.ShapeDtypeStruct((ELEMS, NODES, columns), F32)
    edge = jax.ShapeDtypeStruct((16, columns), F32)
    listed = jax.ShapeDtypeStruct((CAP, NODES, columns), F32)
    mats = jax.ShapeDtypeStruct((steps, 256, 256), BF16)
    table = pltpu.SMEM(
        (min(8, send_list.shape[1]), 128 if send_list.shape[2] % 128 == 0 else send_list.shape[2]), jnp.int32
    )
    field = tracers.reshape(ELEMS, NODES, columns)
    weights = basis_weights.reshape(steps, 256, 16)

    sends = pl.pallas_call(
        first_gather, name="first_gather", out_shape=[listed] * 4, in_specs=[HBM, HBM], out_specs=[VMEM] * 4,
        scratch_shapes=[table, pltpu.SemaphoreType.DMA, pltpu.SemaphoreType.DMA((16,))],
        cost_estimate=cost(3 << 20), compiler_params=grant(12),
    )(pltpu.with_memory_space_constraint(send_list, pltpu.HBM), pltpu.with_memory_space_constraint(field, pltpu.HBM))
    high, low = pl.pallas_call(
        spread_weights, name="spread_weights", out_shape=[mats] * 2, in_specs=[VMEM], out_specs=[VMEM] * 2,
        cost_estimate=cost(2 << 20), compiler_params=grant(12),
    )(weights)
    for step in range(steps):
        face = swaps("face", sends[0], sends[1])
        tile = swaps("tile", sends[2], sends[3])
        moved, *rows = pl.pallas_call(
            functools.partial(move, step), name="move", out_shape=[block, edge, edge],
            in_specs=[SMEM, SMEM] + [VMEM] * 7, out_specs=[VMEM] * 3,
            scratch_shapes=[
                pltpu.VMEM((ELEMS, NODES, columns), F32),
                pltpu.VMEM((256, columns), BF16),
                pltpu.VMEM((256, columns), BF16),
            ],
            cost_estimate=cost(6 << 20), compiler_params=grant(12),
        )(up_owner, up_slot, field, *face, *tile, high, low)
        face = swaps("face", *rows)
        inside, left, right = pl.pallas_call(
            average_inside, name="average_inside", out_shape=[block, edge, edge], in_specs=[VMEM],
            out_specs=[VMEM] * 3, scratch_shapes=[pltpu.VMEM((ELEMS, NODES, columns), F32)],
            cost_estimate=cost(3 << 20), compiler_params=grant(12),
        )(moved)
        columns_out = pl.pallas_call(
            finish_columns, name="finish_columns", out_shape=[edge] * 2, in_specs=[VMEM] * 4, out_specs=[VMEM] * 2,
            cost_estimate=cost(1 << 19), compiler_params=grant(12),
        )(left, right, *face)
        tile = swaps("tile", *columns_out)
        inside = pl.pallas_call(
            finish_rows, name="finish_rows", out_shape=block, in_specs=[VMEM] * 3, out_specs=VMEM,
            cost_estimate=cost(1 << 20), compiler_params=grant(12),
        )(inside, *face)
        if step < steps - 1:
            field, *sends = pl.pallas_call(
                functools.partial(finish_field, step), name="finish_field", out_shape=[block] + [listed] * 4,
                in_specs=[HBM] + [VMEM] * 3, out_specs=[VMEM] * 5,
                scratch_shapes=[table, pltpu.SemaphoreType.DMA], cost_estimate=cost(3 << 20), compiler_params=grant(12),
            )(send_list, inside, *tile)
        else:
            field = pl.pallas_call(
                finish_last, name="finish_last", out_shape=block, in_specs=[VMEM] * 3, out_specs=VMEM,
                cost_estimate=cost(3 << 20), compiler_params=grant(12),
            )(inside, *tile)
    return field.reshape(tracers.shape)


def solution(mesh):
    return jax.shard_map(
        local,
        mesh=mesh,
        in_specs=(
            P("face", "tile", None, None),
            P(None, "face", "tile", None, None),
            P(None, "face", "tile"),
            P(None, "face", "tile"),
            P(),
        ),
        out_specs=P("face", "tile", None, None),
        check_vma=False,
    )
```

time: 119 us -> 98.9 us (0.83)
  the two profiles are of different devices: /device:TPU:63 before, /device:TPU:1 now
where the time goes in v1:
time: 98.9 us; the launch traced here: 98.2 us
  starting transfers between devices  64.8 us (66%)
  waiting for transfers between devices  23 us (23%)
  Pallas kernels  9.19 us (9%)
    ppermute x16, starting transfers between devices, swap(): return lax.ppermute(x, axis, sorted(pairs))  64.8 us
    ppermute x16, waiting for transfers between devices, swap(): return lax.ppermute(x, axis, sorted(pairs))  23 us
    pallas_call x2, Pallas kernels, local(): pl.pallas_call(functools.partial(move, step), name='move', out_shape=[blo...  3.49 us
    pallas_call x1, Pallas kernels, local(): pl.pallas_call(first_gather, name='first_gather', out_shape=[listed] * 4,...  2.4 us
  transfers between devices with their start and end apart: 16, of which 6 were waited for; matrix products, arithmetic and copies ran while one was open for 0% of the time, Pallas kernels for 1%

profile of v1, /device:TPU:1, one launch (start us, length us, event | category | flops | bytes accessed | tf_op | source)
XLA Modules:
  0.0 98.2 jit_solution(10492569850820425362)
XLA Ops:
  0.0 2.4 %first_gather.1 = (f32[4,16,1280]{2,1,0:T(8,128)S(1)}, f32[4,16,1280]{2,1,0:T(8,128)S(1)}, f32[4,16,1280]{2,1,0:T(8,128)S(1)}, f32[4,16,1280]{2,1,0:T(8,128)S(1)}) custom-call(s32[2,48,256]{2,1,0:T(8,128)} %lists.3, f32[16,16,1280]{2,1,0:T(8,128)} %bitcast.3), custom_call_target="tpu_custom_call" | custom-call | bytes 3145728 | tf_op jit(solution)/shard_map/first_gather/pallas_call | solution.py:272
  2.4 4.8 %collective-permute-start = (f32[4,16,1280]{2,1,0:T(8,128)S(1)}, f32[4,16,1280]{2,1,0:T(8,128)S(1)}, u32[]{:S(2)}, u32[]{:S(2)}) collective-permute-start(f32[4,16,1280]{2,1,0:T(8,128)S(1)} %get-tuple-element.32), channel_id=1, source_target_pairs={{0,64},{64,0},{128,192},{192,128},{256,320},{320,256},{384,448},{4... | collective-permute-start | bytes 983048 | tf_op jit(solution)/shard_map/ppermute | solution.py:248
  7.2 12.5 %collective-permute-start.1 = (f32[4,16,1280]{2,1,0:T(8,128)S(1)}, f32[4,16,1280]{2,1,0:T(8,128)S(1)}, u32[]{:S(2)}, u32[]{:S(2)}) collective-permute-start(f32[4,16,1280]{2,1,0:T(8,128)S(1)} %get-tuple-element.33), channel_id=1, source_target_pairs={{0,704},{64,128},{128,64},{192,256},{256,192},{320,384},{384,320},... | collective-permute-start | bytes 983048 | tf_op jit(solution)/shard_map/ppermute | solution.py:248
  19.7 3.1 %collective-permute-start.2 = (f32[4,16,1280]{2,1,0:T(8,128)S(1)}, f32[4,16,1280]{2,1,0:T(8,128)S(1)}, u32[]{:S(2)}, u32[]{:S(2)}) collective-permute-start(f32[4,16,1280]{2,1,0:T(8,128)S(1)} %get-tuple-element.34), channel_id=1, source_target_pairs={{0,1},{1,0},{2,3},{3,2},{4,5},{5,4},{6,7},{7,6},{8,9},{9,8},{10,11... | collective-permute-start | bytes 983048 | tf_op jit(solution)/shard_map/ppermute | solution.py:248
  22.9 3.1 %collective-permute-start.3 = (f32[4,16,1280]{2,1,0:T(8,128)S(1)}, f32[4,16,1280]{2,1,0:T(8,128)S(1)}, u32[]{:S(2)}, u32[]{:S(2)}) collective-permute-start(f32[4,16,1280]{2,1,0:T(8,128)S(1)} %get-tuple-element.35), channel_id=1, source_target_pairs={{0,63},{1,2},{2,1},{3,4},{4,3},{5,6},{6,5},{7,8},{8,7},{9,10},{10,... | collective-permute-start | bytes 983048 | tf_op jit(solution)/shard_map/ppermute | solution.py:248
  27.3 4.3 %collective-permute-done.3.tile_second = f32[4,16,1280]{2,1,0:T(8,128)S(1)} collective-permute-done((f32[4,16,1280]{2,1,0:T(8,128)S(1)}, f32[4,16,1280]{2,1,0:T(8,128)S(1)}, u32[]{:S(2)}, u32[]{:S(2)}) %collective-permute-start.3) | collective-permute-done | bytes 327712 | tf_op jit(solution)/shard_map/ppermute | solution.py:248
  31.6 1.8 %move.2 = (f32[16,16,1280]{2,1,0:T(8,128)S(1)}, f32[16,1280]{1,0:T(8,128)S(1)}, f32[16,1280]{1,0:T(8,128)S(1)}) custom-call(s32[2,4,4]{2,1,0:T(4,128)S(1)} %copy-done.3, s32[2,4,4]{2,1,0:T(4,128)S(1)} %copy-done.4, f32[16,16,1280]{2,1,0:T(8,128)S(1)} %bitcast.4, f32[4,16,1280]{2,1,0:T(8,128)S(1)} %collective-permute-done.face_first, ...), custom_call_target="tpu_custom_call" | custom-call | bytes 6291456 | tf_op jit(solution)/shard_map/move/pallas_call | solution.py:284
  33.4 1.9 %collective-permute-start.4 = (f32[16,1280]{1,0:T(8,128)S(1)}, f32[16,1280]{1,0:T(8,128)S(1)}, u32[]{:S(2)}, u32[]{:S(2)}) collective-permute-start(f32[16,1280]{1,0:T(8,128)S(1)} %get-tuple-element.40), channel_id=1, source_target_pairs={{0,64},{64,0},{128,192},{192,128},{256,320},{320,256},{384,448},{4... | collective-permute-start | bytes 245768 | tf_op jit(solution)/shard_map/ppermute | solution.py:248
  35.3 2.8 %collective-permute-start.5 = (f32[16,1280]{1,0:T(8,128)S(1)}, f32[16,1280]{1,0:T(8,128)S(1)}, u32[]{:S(2)}, u32[]{:S(2)}) collective-permute-start(f32[16,1280]{1,0:T(8,128)S(1)} %get-tuple-element.41), channel_id=1, source_target_pairs={{0,704},{64,128},{128,64},{192,256},{256,192},{320,384},{384,320},... | collective-permute-start | bytes 245768 | tf_op jit(solution)/shard_map/ppermute | solution.py:248
  38.6 3.1 %collective-permute-done.5.face_second = f32[16,1280]{1,0:T(8,128)S(1)} collective-permute-done((f32[16,1280]{1,0:T(8,128)S(1)}, f32[16,1280]{1,0:T(8,128)S(1)}, u32[]{:S(2)}, u32[]{:S(2)}) %collective-permute-start.5) | collective-permute-done | bytes 81952 | tf_op jit(solution)/shard_map/ppermute | solution.py:248
  41.7 6.8 %collective-permute-start.6 = (f32[16,1280]{1,0:T(8,128)S(1)}, f32[16,1280]{1,0:T(8,128)S(1)}, u32[]{:S(2)}, u32[]{:S(2)}) collective-permute-start(f32[16,1280]{1,0:T(8,128)S(1)} %get-tuple-element.44), channel_id=1, source_target_pairs={{0,1},{1,0},{2,3},{3,2},{4,5},{5,4},{6,7},{7,6},{8,9},{9,8},{10,11... | collective-permute-start | bytes 245768 | tf_op jit(solution)/shard_map/ppermute | solution.py:248
  48.5 1.9 %collective-permute-start.7 = (f32[16,1280]{1,0:T(8,128)S(1)}, f32[16,1280]{1,0:T(8,128)S(1)}, u32[]{:S(2)}, u32[]{:S(2)}) collective-permute-start(f32[16,1280]{1,0:T(8,128)S(1)} %get-tuple-element.45), channel_id=1, source_target_pairs={{0,63},{1,2},{2,1},{3,4},{4,3},{5,6},{6,5},{7,8},{8,7},{9,10},{10,... | collective-permute-start | bytes 245768 | tf_op jit(solution)/shard_map/ppermute | solution.py:248
  50.6 3.7 %collective-permute-done.7.tile_second = f32[16,1280]{1,0:T(8,128)S(1)} collective-permute-done((f32[16,1280]{1,0:T(8,128)S(1)}, f32[16,1280]{1,0:T(8,128)S(1)}, u32[]{:S(2)}, u32[]{:S(2)}) %collective-permute-start.7) | collective-permute-done | bytes 81952 | tf_op jit(solution)/shard_map/ppermute | solution.py:248
  55.0 2.4 %collective-permute-start.8 = (f32[4,16,1280]{2,1,0:T(8,128)S(1)}, f32[4,16,1280]{2,1,0:T(8,128)S(1)}, u32[]{:S(2)}, u32[]{:S(2)}) collective-permute-start(f32[4,16,1280]{2,1,0:T(8,128)S(1)} %get-tuple-element.47), channel_id=1, source_target_pairs={{0,64},{64,0},{128,192},{192,128},{256,320},{320,256},{384,448},{4... | collective-permute-start | bytes 983048 | tf_op jit(solution)/shard_map/ppermute | solution.py:248
  57.5 2.6 %collective-permute-start.9 = (f32[4,16,1280]{2,1,0:T(8,128)S(1)}, f32[4,16,1280]{2,1,0:T(8,128)S(1)}, u32[]{:S(2)}, u32[]{:S(2)}) collective-permute-start(f32[4,16,1280]{2,1,0:T(8,128)S(1)} %get-tuple-element.48), channel_id=1, source_target_pairs={{0,704},{64,128},{128,64},{192,256},{256,192},{320,384},{384,320},... | collective-permute-start | bytes 983048 | tf_op jit(solution)/shard_map/ppermute | solution.py:248
  60.1 5.5 %collective-permute-start.10 = (f32[4,16,1280]{2,1,0:T(8,128)S(1)}, f32[4,16,1280]{2,1,0:T(8,128)S(1)}, u32[]{:S(2)}, u32[]{:S(2)}) collective-permute-start(f32[4,16,1280]{2,1,0:T(8,128)S(1)} %get-tuple-element.49), channel_id=1, source_target_pairs={{0,1},{1,0},{2,3},{3,2},{4,5},{5,4},{6,7},{7,6},{8,9},{9,8},{10,11... | collective-permute-start | bytes 983048 | tf_op jit(solution)/shard_map/ppermute | solution.py:248
  65.6 1.9 %collective-permute-start.11 = (f32[4,16,1280]{2,1,0:T(8,128)S(1)}, f32[4,16,1280]{2,1,0:T(8,128)S(1)}, u32[]{:S(2)}, u32[]{:S(2)}) collective-permute-start(f32[4,16,1280]{2,1,0:T(8,128)S(1)} %get-tuple-element.50), channel_id=1, source_target_pairs={{0,63},{1,2},{2,1},{3,4},{4,3},{5,6},{6,5},{7,8},{8,7},{9,10},{10,... | collective-permute-start | bytes 983048 | tf_op jit(solution)/shard_map/ppermute | solution.py:248
  67.6 6.7 %collective-permute-done.11.tile_second = f32[4,16,1280]{2,1,0:T(8,128)S(1)} collective-permute-done((f32[4,16,1280]{2,1,0:T(8,128)S(1)}, f32[4,16,1280]{2,1,0:T(8,128)S(1)}, u32[]{:S(2)}, u32[]{:S(2)}) %collective-permute-start.11) | collective-permute-done | bytes 327712 | tf_op jit(solution)/shard_map/ppermute | solution.py:248
  74.3 1.7 %move.3 = (f32[16,16,1280]{2,1,0:T(8,128)S(1)}, f32[16,1280]{1,0:T(8,128)S(1)}, f32[16,1280]{1,0:T(8,128)S(1)}) custom-call(s32[2,4,4]{2,1,0:T(4,128)S(1)} %copy-done.3, s32[2,4,4]{2,1,0:T(4,128)S(1)} %copy-done.4, f32[16,16,1280]{2,1,0:T(8,128)S(1)} %get-tuple-element.46.field, f32[4,16,1280]{2,1,0:T(8,128)S(1)} %collective-permute-done.8.face_first, ...), custom_call_target="tpu_custom_call" | custom-call | bytes 6291456 | tf_op jit(solution)/shard_map/move/pallas_call | solution.py:284
  76.0 2.2 %collective-permute-start.12 = (f32[16,1280]{1,0:T(8,128)S(1)}, f32[16,1280]{1,0:T(8,128)S(1)}, u32[]{:S(2)}, u32[]{:S(2)}) collective-permute-start(f32[16,1280]{1,0:T(8,128)S(1)} %get-tuple-element.53), channel_id=1, source_target_pairs={{0,64},{64,0},{128,192},{192,128},{256,320},{320,256},{384,448},{4... | collective-permute-start | bytes 245768 | tf_op jit(solution)/shard_map/ppermute | solution.py:248
  78.2 5.1 %collective-permute-start.13 = (f32[16,1280]{1,0:T(8,128)S(1)}, f32[16,1280]{1,0:T(8,128)S(1)}, u32[]{:S(2)}, u32[]{:S(2)}) collective-permute-start(f32[16,1280]{1,0:T(8,128)S(1)} %get-tuple-element.54), channel_id=1, source_target_pairs={{0,704},{64,128},{128,64},{192,256},{256,192},{320,384},{384,320},... | collective-permute-start | bytes 245768 | tf_op jit(solution)/shard_map/ppermute | solution.py:248
  85.2 6.1 %collective-permute-start.14 = (f32[16,1280]{1,0:T(8,128)S(1)}, f32[16,1280]{1,0:T(8,128)S(1)}, u32[]{:S(2)}, u32[]{:S(2)}) collective-permute-start(f32[16,1280]{1,0:T(8,128)S(1)} %get-tuple-element.57), channel_id=1, source_target_pairs={{0,1},{1,0},{2,3},{3,2},{4,5},{5,4},{6,7},{7,6},{8,9},{9,8},{10,11... | collective-permute-start | bytes 245768 | tf_op jit(solution)/shard_map/ppermute | solution.py:248
  91.3 1.9 %collective-permute-start.15 = (f32[16,1280]{1,0:T(8,128)S(1)}, f32[16,1280]{1,0:T(8,128)S(1)}, u32[]{:S(2)}, u32[]{:S(2)}) collective-permute-start(f32[16,1280]{1,0:T(8,128)S(1)} %get-tuple-element.58), channel_id=1, source_target_pairs={{0,63},{1,2},{2,1},{3,4},{4,3},{5,6},{6,5},{7,8},{8,7},{9,10},{10,... | collective-permute-start | bytes 245768 | tf_op jit(solution)/shard_map/ppermute | solution.py:248
  93.4 3.7 %collective-permute-done.15.tile_second = f32[16,1280]{1,0:T(8,128)S(1)} collective-permute-done((f32[16,1280]{1,0:T(8,128)S(1)}, f32[16,1280]{1,0:T(8,128)S(1)}, u32[]{:S(2)}, u32[]{:S(2)}) %collective-permute-start.15) | collective-permute-done | bytes 81952 | tf_op jit(solution)/shard_map/ppermute | solution.py:248
  (30 shorter events, 5.7 us)
Async XLA Ops:
  0.0 31.6 %copy-start = (f32[4,4,16,1280]{3,2,1,0:T(8,128)S(1)}, f32[4,4,16,1280]{3,2,1,0:T(8,128)}, u32[]{:S(2)}) copy-start(f32[4,4,16,1280]{3,2,1,0:T(8,128)} %param.5) | copy-start | bytes 3932164
  0.0 31.6 %copy-start.4 = (s32[2,4,4]{2,1,0:T(4,128)S(1)}, s32[2,4,4]{2,1,0:T(4,128)}, u32[]{:S(2)}) copy-start(s32[2,4,4]{2,1,0:T(4,128)} %slot.3) | copy-start | bytes 388
  0.0 31.6 %copy-start.3 = (s32[2,4,4]{2,1,0:T(4,128)S(1)}, s32[2,4,4]{2,1,0:T(4,128)}, u32[]{:S(2)}) copy-start(s32[2,4,4]{2,1,0:T(4,128)} %owner.3) | copy-start | bytes 388
  2.4 24.8 %collective-permute-start = (f32[4,16,1280]{2,1,0:T(8,128)S(1)}, f32[4,16,1280]{2,1,0:T(8,128)S(1)}, u32[]{:S(2)}, u32[]{:S(2)}) collective-permute-start(f32[4,16,1280]{2,1,0:T(8,128)S(1)} %get-tuple-element.32), channel_id=1, source_target_pairs={{0,64},{64,0},{128,192},{192,128},{256,320},{320,256},{384,448},{4... | collective-permute-start | bytes 983048 | tf_op jit(solution)/shard_map/ppermute | solution.py:248
  7.2 20.0 %collective-permute-start.1 = (f32[4,16,1280]{2,1,0:T(8,128)S(1)}, f32[4,16,1280]{2,1,0:T(8,128)S(1)}, u32[]{:S(2)}, u32[]{:S(2)}) collective-permute-start(f32[4,16,1280]{2,1,0:T(8,128)S(1)} %get-tuple-element.33), channel_id=1, source_target_pairs={{0,704},{64,128},{128,64},{192,256},{256,192},{320,384},{384,320},... | collective-permute-start | bytes 983048 | tf_op jit(solution)/shard_map/ppermute | solution.py:248
  19.7 7.5 %collective-permute-start.2 = (f32[4,16,1280]{2,1,0:T(8,128)S(1)}, f32[4,16,1280]{2,1,0:T(8,128)S(1)}, u32[]{:S(2)}, u32[]{:S(2)}) collective-permute-start(f32[4,16,1280]{2,1,0:T(8,128)S(1)} %get-tuple-element.34), channel_id=1, source_target_pairs={{0,1},{1,0},{2,3},{3,2},{4,5},{5,4},{6,7},{7,6},{8,9},{9,8},{10,11... | collective-permute-start | bytes 983048 | tf_op jit(solution)/shard_map/ppermute | solution.py:248
  22.9 8.7 %collective-permute-start.3 = (f32[4,16,1280]{2,1,0:T(8,128)S(1)}, f32[4,16,1280]{2,1,0:T(8,128)S(1)}, u32[]{:S(2)}, u32[]{:S(2)}) collective-permute-start(f32[4,16,1280]{2,1,0:T(8,128)S(1)} %get-tuple-element.35), channel_id=1, source_target_pairs={{0,63},{1,2},{2,1},{3,4},{4,3},{5,6},{6,5},{7,8},{8,7},{9,10},{10,... | collective-permute-start | bytes 983048 | tf_op jit(solution)/shard_map/ppermute | solution.py:248
  26.0 1.0 copy-start.2
  33.4 5.2 %collective-permute-start.4 = (f32[16,1280]{1,0:T(8,128)S(1)}, f32[16,1280]{1,0:T(8,128)S(1)}, u32[]{:S(2)}, u32[]{:S(2)}) collective-permute-start(f32[16,1280]{1,0:T(8,128)S(1)} %get-tuple-element.40), channel_id=1, source_target_pairs={{0,64},{64,0},{128,192},{192,128},{256,320},{320,256},{384,448},{4... | collective-permute-start | bytes 245768 | tf_op jit(solution)/shard_map/ppermute | solution.py:248
  35.3 6.4 %collective-permute-start.5 = (f32[16,1280]{1,0:T(8,128)S(1)}, f32[16,1280]{1,0:T(8,128)S(1)}, u32[]{:S(2)}, u32[]{:S(2)}) collective-permute-start(f32[16,1280]{1,0:T(8,128)S(1)} %get-tuple-element.41), channel_id=1, source_target_pairs={{0,704},{64,128},{128,64},{192,256},{256,192},{320,384},{384,320},... | collective-permute-start | bytes 245768 | tf_op jit(solution)/shard_map/ppermute | solution.py:248
  41.7 8.9 %collective-permute-start.6 = (f32[16,1280]{1,0:T(8,128)S(1)}, f32[16,1280]{1,0:T(8,128)S(1)}, u32[]{:S(2)}, u32[]{:S(2)}) collective-permute-start(f32[16,1280]{1,0:T(8,128)S(1)} %get-tuple-element.44), channel_id=1, source_target_pairs={{0,1},{1,0},{2,3},{3,2},{4,5},{5,4},{6,7},{7,6},{8,9},{9,8},{10,11... | collective-permute-start | bytes 245768 | tf_op jit(solution)/shard_map/ppermute | solution.py:248
  48.5 5.8 %collective-permute-start.7 = (f32[16,1280]{1,0:T(8,128)S(1)}, f32[16,1280]{1,0:T(8,128)S(1)}, u32[]{:S(2)}, u32[]{:S(2)}) collective-permute-start(f32[16,1280]{1,0:T(8,128)S(1)} %get-tuple-element.45), channel_id=1, source_target_pairs={{0,63},{1,2},{2,1},{3,4},{4,3},{5,6},{6,5},{7,8},{8,7},{9,10},{10,... | collective-permute-start | bytes 245768 | tf_op jit(solution)/shard_map/ppermute | solution.py:248
  50.5 3.8 %copy-start.1 = (s32[2,48,256]{2,1,0:T(8,128)S(1)}, s32[2,48,256]{2,1,0:T(8,128)}, u32[]{:S(2)}) copy-start(s32[2,48,256]{2,1,0:T(8,128)} %lists.3) | copy-start | bytes 294916
  55.0 12.5 %collective-permute-start.8 = (f32[4,16,1280]{2,1,0:T(8,128)S(1)}, f32[4,16,1280]{2,1,0:T(8,128)S(1)}, u32[]{:S(2)}, u32[]{:S(2)}) collective-permute-start(f32[4,16,1280]{2,1,0:T(8,128)S(1)} %get-tuple-element.47), channel_id=1, source_target_pairs={{0,64},{64,0},{128,192},{192,128},{256,320},{320,256},{384,448},{4... | collective-permute-start | bytes 983048 | tf_op jit(solution)/shard_map/ppermute | solution.py:248
  57.5 10.1 %collective-permute-start.9 = (f32[4,16,1280]{2,1,0:T(8,128)S(1)}, f32[4,16,1280]{2,1,0:T(8,128)S(1)}, u32[]{:S(2)}, u32[]{:S(2)}) collective-permute-start(f32[4,16,1280]{2,1,0:T(8,128)S(1)} %get-tuple-element.48), channel_id=1, source_target_pairs={{0,704},{64,128},{128,64},{192,256},{256,192},{320,384},{384,320},... | collective-permute-start | bytes 983048 | tf_op jit(solution)/shard_map/ppermute | solution.py:248
  60.1 7.5 %collective-permute-start.10 = (f32[4,16,1280]{2,1,0:T(8,128)S(1)}, f32[4,16,1280]{2,1,0:T(8,128)S(1)}, u32[]{:S(2)}, u32[]{:S(2)}) collective-permute-start(f32[4,16,1280]{2,1,0:T(8,128)S(1)} %get-tuple-element.49), channel_id=1, source_target_pairs={{0,1},{1,0},{2,3},{3,2},{4,5},{5,4},{6,7},{7,6},{8,9},{9,8},{10,11... | collective-permute-start | bytes 983048 | tf_op jit(solution)/shard_map/ppermute | solution.py:248
  65.6 8.7 %collective-permute-start.11 = (f32[4,16,1280]{2,1,0:T(8,128)S(1)}, f32[4,16,1280]{2,1,0:T(8,128)S(1)}, u32[]{:S(2)}, u32[]{:S(2)}) collective-permute-start(f32[4,16,1280]{2,1,0:T(8,128)S(1)} %get-tuple-element.50), channel_id=1, source_target_pairs={{0,63},{1,2},{2,1},{3,4},{4,3},{5,6},{6,5},{7,8},{8,7},{9,10},{10,... | collective-permute-start | bytes 983048 | tf_op jit(solution)/shard_map/ppermute | solution.py:248
  76.0 7.7 %collective-permute-start.12 = (f32[16,1280]{1,0:T(8,128)S(1)}, f32[16,1280]{1,0:T(8,128)S(1)}, u32[]{:S(2)}, u32[]{:S(2)}) collective-permute-start(f32[16,1280]{1,0:T(8,128)S(1)} %get-tuple-element.53), channel_id=1, source_target_pairs={{0,64},{64,0},{128,192},{192,128},{256,320},{320,256},{384,448},{4... | collective-permute-start | bytes 245768 | tf_op jit(solution)/shard_map/ppermute | solution.py:248
  78.2 6.9 %collective-permute-start.13 = (f32[16,1280]{1,0:T(8,128)S(1)}, f32[16,1280]{1,0:T(8,128)S(1)}, u32[]{:S(2)}, u32[]{:S(2)}) collective-permute-start(f32[16,1280]{1,0:T(8,128)S(1)} %get-tuple-element.54), channel_id=1, source_target_pairs={{0,704},{64,128},{128,64},{192,256},{256,192},{320,384},{384,320},... | collective-permute-start | bytes 245768 | tf_op jit(solution)/shard_map/ppermute | solution.py:248
  85.2 8.1 %collective-permute-start.14 = (f32[16,1280]{1,0:T(8,128)S(1)}, f32[16,1280]{1,0:T(8,128)S(1)}, u32[]{:S(2)}, u32[]{:S(2)}) collective-permute-start(f32[16,1280]{1,0:T(8,128)S(1)} %get-tuple-element.57), channel_id=1, source_target_pairs={{0,1},{1,0},{2,3},{3,2},{4,5},{5,4},{6,7},{7,6},{8,9},{9,8},{10,11... | collective-permute-start | bytes 245768 | tf_op jit(solution)/shard_map/ppermute | solution.py:248
  91.3 5.8 %collective-permute-start.15 = (f32[16,1280]{1,0:T(8,128)S(1)}, f32[16,1280]{1,0:T(8,128)S(1)}, u32[]{:S(2)}, u32[]{:S(2)}) collective-permute-start(f32[16,1280]{1,0:T(8,128)S(1)} %get-tuple-element.58), channel_id=1, source_target_pairs={{0,63},{1,2},{2,1},{3,4},{4,3},{5,6},{6,5},{7,8},{8,7},{9,10},{10,... | collective-permute-start | bytes 245768 | tf_op jit(solution)/shard_map/ppermute | solution.py:248

commit v2 on v1

--- a/solution.py
+++ b/solution.py
@@ -42,17 +42,18 @@
     return odd("face"), 1 - odd("face"), 2 + odd("tile"), 3 - odd("tile")
 
 
-def first_gather(lists, field, *rest):
-    sends, (table, list_sem, sems) = rest[:4], rest[4:]
+def first_gather(axis, lists, field, *rest):
+    sends, (table, list_sem, sems) = rest[:2], rest[2:]
     copy, row, col = list_copy(0, lists, table, list_sem)
     copy.start()
     copy.wait()
     copies = []
-    for k, j in enumerate(directions()):
+    toward = directions()[:2] if axis == "face" else directions()[2:]
+    for k in (1, 0):
         for c in range(CAP):
             copies.append(
                 pltpu.make_async_copy(
-                    field.at[table[row + j, col + c]], sends[k].at[c], sems.at[k * CAP + c]
+                    field.at[table[row + toward[k], col + c]], sends[k].at[c], sems.at[k * CAP + c]
                 )
             )
             copies[-1].start()
@@ -256,7 +257,7 @@
     return lax.rem(lax.axis_index(axis), 2)
 
 
-def local(tracers, basis_weights, up_owner, up_slot, send_list):
+def transport(tracers, basis_weights, up_owner, up_slot, send_list):
     columns = tracers.shape[3]
     steps = basis_weights.shape[0]
     block = jax.ShapeDtypeStruct((ELEMS, NODES, columns), F32)
@@ -269,11 +270,16 @@
     field = tracers.reshape(ELEMS, NODES, columns)
     weights = basis_weights.reshape(steps, 256, 16)
 
-    sends = pl.pallas_call(
-        first_gather, name="first_gather", out_shape=[listed] * 4, in_specs=[HBM, HBM], out_specs=[VMEM] * 4,
-        scratch_shapes=[table, pltpu.SemaphoreType.DMA, pltpu.SemaphoreType.DMA((16,))],
-        cost_estimate=cost(3 << 20), compiler_params=grant(12),
-    )(pltpu.with_memory_space_constraint(send_list, pltpu.HBM), pltpu.with_memory_space_constraint(field, pltpu.HBM))
+    lists_hbm = pltpu.with_memory_space_constraint(send_list, pltpu.HBM)
+    field_hbm = pltpu.with_memory_space_constraint(field, pltpu.HBM)
+    sends = []
+    for axis in ("face", "tile"):
+        sends += pl.pallas_call(
+            functools.partial(first_gather, axis), out_shape=[listed] * 2,
+            in_specs=[HBM, HBM], out_specs=[VMEM] * 2,
+            scratch_shapes=[table, pltpu.SemaphoreType.DMA, pltpu.SemaphoreType.DMA((8,))],
+            cost_estimate=cost(2 << 20), compiler_params=grant(12),
+        )(lists_hbm, field_hbm)
     high, low = pl.pallas_call(
         spread_weights, name="spread_weights", out_shape=[mats] * 2, in_specs=[VMEM], out_specs=[VMEM] * 2,
         cost_estimate=cost(2 << 20), compiler_params=grant(12),
@@ -322,7 +328,7 @@
 
 def solution(mesh):
     return jax.shard_map(
-        local,
+        transport,
         mesh=mesh,
         in_specs=(
             P("face", "tile", None, None),

time: 98.9 us -> 103 us (1.041)
  the two profiles are of different devices: /device:TPU:1 before, /device:TPU:64 now
where the time goes in v2:
time: 103 us; the launch traced here: 102 us
  starting transfers between devices  58 us (56%)
  waiting for transfers between devices  33.1 us (32%)
  Pallas kernels  10.9 us (11%)
    ppermute x16, starting transfers between devices, swap(): return lax.ppermute(x, axis, sorted(pairs))  58 us
    ppermute x16, waiting for transfers between devices, swap(): return lax.ppermute(x, axis, sorted(pairs))  33.1 us
    pallas_call x2, Pallas kernels, transport(): pl.pallas_call(functools.partial(first_gather, axis), out_shape=[listed]...  4.13 us
    pallas_call x2, Pallas kernels, transport(): pl.pallas_call(functools.partial(move, step), name='move', out_shape=[blo...  3.5 us
  transfers between devices with their start and end apart: 16, of which 8 were waited for; matrix products, arithmetic and copies ran while one was open for 0% of the time, Pallas kernels for 3%

profile of v2, /device:TPU:64, one launch (start us, length us, event | category | flops | bytes accessed | tf_op | source)
XLA Modules:
  0.0 102.3 jit_solution(7917637186755069456)
XLA Ops:
  0.0 2.1 %shard_map.56 = (f32[4,16,1280]{2,1,0:T(8,128)S(1)}, f32[4,16,1280]{2,1,0:T(8,128)S(1)}) custom-call(s32[2,48,256]{2,1,0:T(8,128)} %lists.5, f32[16,16,1280]{2,1,0:T(8,128)} %bitcast.3), custom_call_target="tpu_custom_call" | custom-call | bytes 2097152 | tf_op jit(solution)/shard_map/pallas_call | solution.py:277
  2.2 1.9 %collective-permute-start.2 = (f32[4,16,1280]{2,1,0:T(8,128)S(1)}, f32[4,16,1280]{2,1,0:T(8,128)S(1)}, u32[]{:S(2)}, u32[]{:S(2)}) collective-permute-start(f32[4,16,1280]{2,1,0:T(8,128)S(1)} %get-tuple-element.34), channel_id=1, source_target_pairs={{0,1},{1,0},{2,3},{3,2},{4,5},{5,4},{6,7},{7,6},{8,9},{9,8},{10,11... | collective-permute-start | bytes 983048 | tf_op jit(solution)/shard_map/ppermute | solution.py:249
  4.1 7.7 %collective-permute-start.3 = (f32[4,16,1280]{2,1,0:T(8,128)S(1)}, f32[4,16,1280]{2,1,0:T(8,128)S(1)}, u32[]{:S(2)}, u32[]{:S(2)}) collective-permute-start(f32[4,16,1280]{2,1,0:T(8,128)S(1)} %get-tuple-element.35), channel_id=1, source_target_pairs={{0,63},{1,2},{2,1},{3,4},{4,3},{5,6},{6,5},{7,8},{8,7},{9,10},{10,... | collective-permute-start | bytes 983048 | tf_op jit(solution)/shard_map/ppermute | solution.py:249
  11.8 2.0 %shard_map.55 = (f32[4,16,1280]{2,1,0:T(8,128)S(1)}, f32[4,16,1280]{2,1,0:T(8,128)S(1)}) custom-call(s32[2,48,256]{2,1,0:T(8,128)} %lists.5, f32[16,16,1280]{2,1,0:T(8,128)} %bitcast.4), custom_call_target="tpu_custom_call" | custom-call | bytes 2097152 | tf_op jit(solution)/shard_map/pallas_call | solution.py:277
  13.8 4.8 %collective-permute-start = (f32[4,16,1280]{2,1,0:T(8,128)S(1)}, f32[4,16,1280]{2,1,0:T(8,128)S(1)}, u32[]{:S(2)}, u32[]{:S(2)}) collective-permute-start(f32[4,16,1280]{2,1,0:T(8,128)S(1)} %get-tuple-element.32), channel_id=1, source_target_pairs={{0,64},{64,0},{128,192},{192,128},{256,320},{320,256},{384,448},{4... | collective-permute-start | bytes 983048 | tf_op jit(solution)/shard_map/ppermute | solution.py:249
  18.6 3.8 %collective-permute-start.1 = (f32[4,16,1280]{2,1,0:T(8,128)S(1)}, f32[4,16,1280]{2,1,0:T(8,128)S(1)}, u32[]{:S(2)}, u32[]{:S(2)}) collective-permute-start(f32[4,16,1280]{2,1,0:T(8,128)S(1)} %get-tuple-element.33), channel_id=1, source_target_pairs={{0,704},{64,128},{128,64},{192,256},{256,192},{320,384},{384,320},... | collective-permute-start | bytes 983048 | tf_op jit(solution)/shard_map/ppermute | solution.py:249
  22.7 4.3 %collective-permute-done.face_first = f32[4,16,1280]{2,1,0:T(8,128)S(1)} collective-permute-done((f32[4,16,1280]{2,1,0:T(8,128)S(1)}, f32[4,16,1280]{2,1,0:T(8,128)S(1)}, u32[]{:S(2)}, u32[]{:S(2)}) %collective-permute-start) | collective-permute-done | bytes 327712 | tf_op jit(solution)/shard_map/ppermute | solution.py:249
  26.9 3.4 %collective-permute-done.1.face_second = f32[4,16,1280]{2,1,0:T(8,128)S(1)} collective-permute-done((f32[4,16,1280]{2,1,0:T(8,128)S(1)}, f32[4,16,1280]{2,1,0:T(8,128)S(1)}, u32[]{:S(2)}, u32[]{:S(2)}) %collective-permute-start.1) | collective-permute-done | bytes 327712 | tf_op jit(solution)/shard_map/ppermute | solution.py:249
  32.1 7.2 %collective-permute-start.4 = (f32[16,1280]{1,0:T(8,128)S(1)}, f32[16,1280]{1,0:T(8,128)S(1)}, u32[]{:S(2)}, u32[]{:S(2)}) collective-permute-start(f32[16,1280]{1,0:T(8,128)S(1)} %get-tuple-element.40), channel_id=1, source_target_pairs={{0,64},{64,0},{128,192},{192,128},{256,320},{320,256},{384,448},{4... | collective-permute-start | bytes 245768 | tf_op jit(solution)/shard_map/ppermute | solution.py:249
  39.2 1.9 %collective-permute-start.5 = (f32[16,1280]{1,0:T(8,128)S(1)}, f32[16,1280]{1,0:T(8,128)S(1)}, u32[]{:S(2)}, u32[]{:S(2)}) collective-permute-start(f32[16,1280]{1,0:T(8,128)S(1)} %get-tuple-element.41), channel_id=1, source_target_pairs={{0,704},{64,128},{128,64},{192,256},{256,192},{320,384},{384,320},... | collective-permute-start | bytes 245768 | tf_op jit(solution)/shard_map/ppermute | solution.py:249
  41.6 3.9 %collective-permute-done.5.face_second = f32[16,1280]{1,0:T(8,128)S(1)} collective-permute-done((f32[16,1280]{1,0:T(8,128)S(1)}, f32[16,1280]{1,0:T(8,128)S(1)}, u32[]{:S(2)}, u32[]{:S(2)}) %collective-permute-start.5) | collective-permute-done | bytes 81952 | tf_op jit(solution)/shard_map/ppermute | solution.py:249
  45.6 1.9 %collective-permute-start.6 = (f32[16,1280]{1,0:T(8,128)S(1)}, f32[16,1280]{1,0:T(8,128)S(1)}, u32[]{:S(2)}, u32[]{:S(2)}) collective-permute-start(f32[16,1280]{1,0:T(8,128)S(1)} %get-tuple-element.44), channel_id=1, source_target_pairs={{0,1},{1,0},{2,3},{3,2},{4,5},{5,4},{6,7},{7,6},{8,9},{9,8},{10,11... | collective-permute-start | bytes 245768 | tf_op jit(solution)/shard_map/ppermute | solution.py:249
  47.5 5.0 %collective-permute-start.7 = (f32[16,1280]{1,0:T(8,128)S(1)}, f32[16,1280]{1,0:T(8,128)S(1)}, u32[]{:S(2)}, u32[]{:S(2)}) collective-permute-start(f32[16,1280]{1,0:T(8,128)S(1)} %get-tuple-element.45), channel_id=1, source_target_pairs={{0,63},{1,2},{2,1},{3,4},{4,3},{5,6},{6,5},{7,8},{8,7},{9,10},{10,... | collective-permute-start | bytes 245768 | tf_op jit(solution)/shard_map/ppermute | solution.py:249
  52.6 4.0 %collective-permute-done.7.tile_second = f32[16,1280]{1,0:T(8,128)S(1)} collective-permute-done((f32[16,1280]{1,0:T(8,128)S(1)}, f32[16,1280]{1,0:T(8,128)S(1)}, u32[]{:S(2)}, u32[]{:S(2)}) %collective-permute-start.7) | collective-permute-done | bytes 81952 | tf_op jit(solution)/shard_map/ppermute | solution.py:249
  57.4 3.4 %collective-permute-start.8 = (f32[4,16,1280]{2,1,0:T(8,128)S(1)}, f32[4,16,1280]{2,1,0:T(8,128)S(1)}, u32[]{:S(2)}, u32[]{:S(2)}) collective-permute-start(f32[4,16,1280]{2,1,0:T(8,128)S(1)} %get-tuple-element.47), channel_id=1, source_target_pairs={{0,64},{64,0},{128,192},{192,128},{256,320},{320,256},{384,448},{4... | collective-permute-start | bytes 983048 | tf_op jit(solution)/shard_map/ppermute | solution.py:249
  60.8 1.9 %collective-permute-start.9 = (f32[4,16,1280]{2,1,0:T(8,128)S(1)}, f32[4,16,1280]{2,1,0:T(8,128)S(1)}, u32[]{:S(2)}, u32[]{:S(2)}) collective-permute-start(f32[4,16,1280]{2,1,0:T(8,128)S(1)} %get-tuple-element.48), channel_id=1, source_target_pairs={{0,704},{64,128},{128,64},{192,256},{256,192},{320,384},{384,320},... | collective-permute-start | bytes 983048 | tf_op jit(solution)/shard_map/ppermute | solution.py:249
  62.7 1.9 %collective-permute-start.10 = (f32[4,16,1280]{2,1,0:T(8,128)S(1)}, f32[4,16,1280]{2,1,0:T(8,128)S(1)}, u32[]{:S(2)}, u32[]{:S(2)}) collective-permute-start(f32[4,16,1280]{2,1,0:T(8,128)S(1)} %get-tuple-element.49), channel_id=1, source_target_pairs={{0,1},{1,0},{2,3},{3,2},{4,5},{5,4},{6,7},{7,6},{8,9},{9,8},{10,11... | collective-permute-start | bytes 983048 | tf_op jit(solution)/shard_map/ppermute | solution.py:249
  64.6 4.4 %collective-permute-start.11 = (f32[4,16,1280]{2,1,0:T(8,128)S(1)}, f32[4,16,1280]{2,1,0:T(8,128)S(1)}, u32[]{:S(2)}, u32[]{:S(2)}) collective-permute-start(f32[4,16,1280]{2,1,0:T(8,128)S(1)} %get-tuple-element.50), channel_id=1, source_target_pairs={{0,63},{1,2},{2,1},{3,4},{4,3},{5,6},{6,5},{7,8},{8,7},{9,10},{10,... | collective-permute-start | bytes 983048 | tf_op jit(solution)/shard_map/ppermute | solution.py:249
  69.7 6.6 %collective-permute-done.11.tile_second = f32[4,16,1280]{2,1,0:T(8,128)S(1)} collective-permute-done((f32[4,16,1280]{2,1,0:T(8,128)S(1)}, f32[4,16,1280]{2,1,0:T(8,128)S(1)}, u32[]{:S(2)}, u32[]{:S(2)}) %collective-permute-start.11) | collective-permute-done | bytes 327712 | tf_op jit(solution)/shard_map/ppermute | solution.py:249
  78.1 5.7 %collective-permute-start.12 = (f32[16,1280]{1,0:T(8,128)S(1)}, f32[16,1280]{1,0:T(8,128)S(1)}, u32[]{:S(2)}, u32[]{:S(2)}) collective-permute-start(f32[16,1280]{1,0:T(8,128)S(1)} %get-tuple-element.53), channel_id=1, source_target_pairs={{0,64},{64,0},{128,192},{192,128},{256,320},{320,256},{384,448},{4... | collective-permute-start | bytes 245768 | tf_op jit(solution)/shard_map/ppermute | solution.py:249
  86.2 3.9 %collective-permute-done.13.face_second = f32[16,1280]{1,0:T(8,128)S(1)} collective-permute-done((f32[16,1280]{1,0:T(8,128)S(1)}, f32[16,1280]{1,0:T(8,128)S(1)}, u32[]{:S(2)}, u32[]{:S(2)}) %collective-permute-start.13) | collective-permute-done | bytes 81952 | tf_op jit(solution)/shard_map/ppermute | solution.py:249
  90.1 1.9 %collective-permute-start.14 = (f32[16,1280]{1,0:T(8,128)S(1)}, f32[16,1280]{1,0:T(8,128)S(1)}, u32[]{:S(2)}, u32[]{:S(2)}) collective-permute-start(f32[16,1280]{1,0:T(8,128)S(1)} %get-tuple-element.57), channel_id=1, source_target_pairs={{0,1},{1,0},{2,3},{3,2},{4,5},{5,4},{6,7},{7,6},{8,9},{9,8},{10,11... | collective-permute-start | bytes 245768 | tf_op jit(solution)/shard_map/ppermute | solution.py:249
  92.1 2.7 %collective-permute-start.15 = (f32[16,1280]{1,0:T(8,128)S(1)}, f32[16,1280]{1,0:T(8,128)S(1)}, u32[]{:S(2)}, u32[]{:S(2)}) collective-permute-start(f32[16,1280]{1,0:T(8,128)S(1)} %get-tuple-element.58), channel_id=1, source_target_pairs={{0,63},{1,2},{2,1},{3,4},{4,3},{5,6},{6,5},{7,8},{8,7},{9,10},{10,... | collective-permute-start | bytes 245768 | tf_op jit(solution)/shard_map/ppermute | solution.py:249
  94.9 6.3 %collective-permute-done.15.tile_second = f32[16,1280]{1,0:T(8,128)S(1)} collective-permute-done((f32[16,1280]{1,0:T(8,128)S(1)}, f32[16,1280]{1,0:T(8,128)S(1)}, u32[]{:S(2)}, u32[]{:S(2)}) %collective-permute-start.15) | collective-permute-done | bytes 81952 | tf_op jit(solution)/shard_map/ppermute | solution.py:249
  (31 shorter events, 9.5 us)
Async XLA Ops:
  0.0 22.4 %copy-start.2 = (f32[2,4,4,16,16]{4,3,2,1,0:T(8,128)S(1)}, f32[2,4,4,16,16]{4,3,2,1,0:T(8,128)}, u32[]{:S(2)}) copy-start(f32[2,4,4,16,16]{4,3,2,1,0:T(8,128)} %param.6) | copy-start | bytes 98308
  0.0 30.3 %copy-start = (f32[4,4,16,1280]{3,2,1,0:T(8,128)S(1)}, f32[4,4,16,1280]{3,2,1,0:T(8,128)}, u32[]{:S(2)}) copy-start(f32[4,4,16,1280]{3,2,1,0:T(8,128)} %param.5) | copy-start | bytes 3932164
  0.0 30.3 %copy-start.3 = (s32[2,4,4]{2,1,0:T(4,128)S(1)}, s32[2,4,4]{2,1,0:T(4,128)}, u32[]{:S(2)}) copy-start(s32[2,4,4]{2,1,0:T(4,128)} %owner.3) | copy-start | bytes 388
  0.0 30.3 %copy-start.4 = (s32[2,4,4]{2,1,0:T(4,128)S(1)}, s32[2,4,4]{2,1,0:T(4,128)}, u32[]{:S(2)}) copy-start(s32[2,4,4]{2,1,0:T(4,128)} %slot.3) | copy-start | bytes 388
  2.2 20.5 %collective-permute-start.2 = (f32[4,16,1280]{2,1,0:T(8,128)S(1)}, f32[4,16,1280]{2,1,0:T(8,128)S(1)}, u32[]{:S(2)}, u32[]{:S(2)}) collective-permute-start(f32[4,16,1280]{2,1,0:T(8,128)S(1)} %get-tuple-element.34), channel_id=1, source_target_pairs={{0,1},{1,0},{2,3},{3,2},{4,5},{5,4},{6,7},{7,6},{8,9},{9,8},{10,11... | collective-permute-start | bytes 983048 | tf_op jit(solution)/shard_map/ppermute | solution.py:249
  4.1 18.6 %collective-permute-start.3 = (f32[4,16,1280]{2,1,0:T(8,128)S(1)}, f32[4,16,1280]{2,1,0:T(8,128)S(1)}, u32[]{:S(2)}, u32[]{:S(2)}) collective-permute-start(f32[4,16,1280]{2,1,0:T(8,128)S(1)} %get-tuple-element.35), channel_id=1, source_target_pairs={{0,63},{1,2},{2,1},{3,4},{4,3},{5,6},{6,5},{7,8},{8,7},{9,10},{10,... | collective-permute-start | bytes 983048 | tf_op jit(solution)/shard_map/ppermute | solution.py:249
  13.8 13.1 %collective-permute-start = (f32[4,16,1280]{2,1,0:T(8,128)S(1)}, f32[4,16,1280]{2,1,0:T(8,128)S(1)}, u32[]{:S(2)}, u32[]{:S(2)}) collective-permute-start(f32[4,16,1280]{2,1,0:T(8,128)S(1)} %get-tuple-element.32), channel_id=1, source_target_pairs={{0,64},{64,0},{128,192},{192,128},{256,320},{320,256},{384,448},{4... | collective-permute-start | bytes 983048 | tf_op jit(solution)/shard_map/ppermute | solution.py:249
  18.6 11.7 %collective-permute-start.1 = (f32[4,16,1280]{2,1,0:T(8,128)S(1)}, f32[4,16,1280]{2,1,0:T(8,128)S(1)}, u32[]{:S(2)}, u32[]{:S(2)}) collective-permute-start(f32[4,16,1280]{2,1,0:T(8,128)S(1)} %get-tuple-element.33), channel_id=1, source_target_pairs={{0,704},{64,128},{128,64},{192,256},{256,192},{320,384},{384,320},... | collective-permute-start | bytes 983048 | tf_op jit(solution)/shard_map/ppermute | solution.py:249
  32.1 9.6 %collective-permute-start.4 = (f32[16,1280]{1,0:T(8,128)S(1)}, f32[16,1280]{1,0:T(8,128)S(1)}, u32[]{:S(2)}, u32[]{:S(2)}) collective-permute-start(f32[16,1280]{1,0:T(8,128)S(1)} %get-tuple-element.40), channel_id=1, source_target_pairs={{0,64},{64,0},{128,192},{192,128},{256,320},{320,256},{384,448},{4... | collective-permute-start | bytes 245768 | tf_op jit(solution)/shard_map/ppermute | solution.py:249
  39.2 6.3 %collective-permute-start.5 = (f32[16,1280]{1,0:T(8,128)S(1)}, f32[16,1280]{1,0:T(8,128)S(1)}, u32[]{:S(2)}, u32[]{:S(2)}) collective-permute-start(f32[16,1280]{1,0:T(8,128)S(1)} %get-tuple-element.41), channel_id=1, source_target_pairs={{0,704},{64,128},{128,64},{192,256},{256,192},{320,384},{384,320},... | collective-permute-start | bytes 245768 | tf_op jit(solution)/shard_map/ppermute | solution.py:249
  45.6 7.0 %collective-permute-start.6 = (f32[16,1280]{1,0:T(8,128)S(1)}, f32[16,1280]{1,0:T(8,128)S(1)}, u32[]{:S(2)}, u32[]{:S(2)}) collective-permute-start(f32[16,1280]{1,0:T(8,128)S(1)} %get-tuple-element.44), channel_id=1, source_target_pairs={{0,1},{1,0},{2,3},{3,2},{4,5},{5,4},{6,7},{7,6},{8,9},{9,8},{10,11... | collective-permute-start | bytes 245768 | tf_op jit(solution)/shard_map/ppermute | solution.py:249
  47.5 9.1 %collective-permute-start.7 = (f32[16,1280]{1,0:T(8,128)S(1)}, f32[16,1280]{1,0:T(8,128)S(1)}, u32[]{:S(2)}, u32[]{:S(2)}) collective-permute-start(f32[16,1280]{1,0:T(8,128)S(1)} %get-tuple-element.45), channel_id=1, source_target_pairs={{0,63},{1,2},{2,1},{3,4},{4,3},{5,6},{6,5},{7,8},{8,7},{9,10},{10,... | collective-permute-start | bytes 245768 | tf_op jit(solution)/shard_map/ppermute | solution.py:249
  52.5 4.1 %copy-start.1 = (s32[2,48,256]{2,1,0:T(8,128)S(1)}, s32[2,48,256]{2,1,0:T(8,128)}, u32[]{:S(2)}) copy-start(s32[2,48,256]{2,1,0:T(8,128)} %lists.5) | copy-start | bytes 294916
  57.4 11.7 %collective-permute-start.8 = (f32[4,16,1280]{2,1,0:T(8,128)S(1)}, f32[4,16,1280]{2,1,0:T(8,128)S(1)}, u32[]{:S(2)}, u32[]{:S(2)}) collective-permute-start(f32[4,16,1280]{2,1,0:T(8,128)S(1)} %get-tuple-element.47), channel_id=1, source_target_pairs={{0,64},{64,0},{128,192},{192,128},{256,320},{320,256},{384,448},{4... | collective-permute-start | bytes 983048 | tf_op jit(solution)/shard_map/ppermute | solution.py:249
  60.8 9.0 %collective-permute-start.9 = (f32[4,16,1280]{2,1,0:T(8,128)S(1)}, f32[4,16,1280]{2,1,0:T(8,128)S(1)}, u32[]{:S(2)}, u32[]{:S(2)}) collective-permute-start(f32[4,16,1280]{2,1,0:T(8,128)S(1)} %get-tuple-element.48), channel_id=1, source_target_pairs={{0,704},{64,128},{128,64},{192,256},{256,192},{320,384},{384,320},... | collective-permute-start | bytes 983048 | tf_op jit(solution)/shard_map/ppermute | solution.py:249
  62.7 7.0 %collective-permute-start.10 = (f32[4,16,1280]{2,1,0:T(8,128)S(1)}, f32[4,16,1280]{2,1,0:T(8,128)S(1)}, u32[]{:S(2)}, u32[]{:S(2)}) collective-permute-start(f32[4,16,1280]{2,1,0:T(8,128)S(1)} %get-tuple-element.49), channel_id=1, source_target_pairs={{0,1},{1,0},{2,3},{3,2},{4,5},{5,4},{6,7},{7,6},{8,9},{9,8},{10,11... | collective-permute-start | bytes 983048 | tf_op jit(solution)/shard_map/ppermute | solution.py:249
  64.6 11.7 %collective-permute-start.11 = (f32[4,16,1280]{2,1,0:T(8,128)S(1)}, f32[4,16,1280]{2,1,0:T(8,128)S(1)}, u32[]{:S(2)}, u32[]{:S(2)}) collective-permute-start(f32[4,16,1280]{2,1,0:T(8,128)S(1)} %get-tuple-element.50), channel_id=1, source_target_pairs={{0,63},{1,2},{2,1},{3,4},{4,3},{5,6},{6,5},{7,8},{8,7},{9,10},{10,... | collective-permute-start | bytes 983048 | tf_op jit(solution)/shard_map/ppermute | solution.py:249
  78.1 8.1 %collective-permute-start.12 = (f32[16,1280]{1,0:T(8,128)S(1)}, f32[16,1280]{1,0:T(8,128)S(1)}, u32[]{:S(2)}, u32[]{:S(2)}) collective-permute-start(f32[16,1280]{1,0:T(8,128)S(1)} %get-tuple-element.53), channel_id=1, source_target_pairs={{0,64},{64,0},{128,192},{192,128},{256,320},{320,256},{384,448},{4... | collective-permute-start | bytes 245768 | tf_op jit(solution)/shard_map/ppermute | solution.py:249
  83.8 6.3 %collective-permute-start.13 = (f32[16,1280]{1,0:T(8,128)S(1)}, f32[16,1280]{1,0:T(8,128)S(1)}, u32[]{:S(2)}, u32[]{:S(2)}) collective-permute-start(f32[16,1280]{1,0:T(8,128)S(1)} %get-tuple-element.54), channel_id=1, source_target_pairs={{0,704},{64,128},{128,64},{192,256},{256,192},{320,384},{384,320},... | collective-permute-start | bytes 245768 | tf_op jit(solution)/shard_map/ppermute | solution.py:249
  90.1 4.7 %collective-permute-start.14 = (f32[16,1280]{1,0:T(8,128)S(1)}, f32[16,1280]{1,0:T(8,128)S(1)}, u32[]{:S(2)}, u32[]{:S(2)}) collective-permute-start(f32[16,1280]{1,0:T(8,128)S(1)} %get-tuple-element.57), channel_id=1, source_target_pairs={{0,1},{1,0},{2,3},{3,2},{4,5},{5,4},{6,7},{7,6},{8,9},{9,8},{10,11... | collective-permute-start | bytes 245768 | tf_op jit(solution)/shard_map/ppermute | solution.py:249
  92.1 9.1 %collective-permute-start.15 = (f32[16,1280]{1,0:T(8,128)S(1)}, f32[16,1280]{1,0:T(8,128)S(1)}, u32[]{:S(2)}, u32[]{:S(2)}) collective-permute-start(f32[16,1280]{1,0:T(8,128)S(1)} %get-tuple-element.58), channel_id=1, source_target_pairs={{0,63},{1,2},{2,1},{3,4},{4,3},{5,6},{6,5},{7,8},{8,7},{9,10},{10,... | collective-permute-start | bytes 245768 | tf_op jit(solution)/shard_map/ppermute | solution.py:249

commit v3 on v2

v3 whole, which is shorter than its diff:
```python
import functools

import jax
import jax.numpy as jnp
from jax import lax
from jax.experimental import pallas as pl
from jax.experimental.pallas import tpu as pltpu
from jax.sharding import PartitionSpec as P

F32 = jnp.float32
BF16 = jnp.bfloat16
VMEM = pl.BlockSpec(memory_space=pltpu.VMEM)
SMEM = pl.BlockSpec(memory_space=pltpu.SMEM)
HBM = pl.BlockSpec(memory_space=pltpu.HBM)
ELEMS = 16
NODES = 16
CAP = 4


def run(kernel, in_specs, out, mib, scratch, *args, out_space=VMEM):
    out_specs = [out_space] * len(out) if isinstance(out, list) else out_space
    return pl.pallas_call(
        kernel,
        out_shape=out,
        in_specs=in_specs,
        out_specs=out_specs,
        scratch_shapes=scratch,
        cost_estimate=pl.CostEstimate(flops=0, transcendentals=0, bytes_accessed=mib << 20),
        compiler_params=pltpu.CompilerParams(vmem_limit_bytes=12 << 20),
    )(*args)


def list_copy(step, lists, table, sem):
    rows, cols = table.shape
    row = lax.axis_index("face") * 4
    col = lax.axis_index("tile") * CAP
    row0, col0 = lax.div(row, rows) * rows, lax.div(col, cols) * cols
    copy = pltpu.make_async_copy(
        lists.at[step, pl.ds(pl.multiple_of(row0, rows), rows), pl.ds(pl.multiple_of(col0, cols), cols)],
        table,
        sem,
    )
    return copy, row - row0, col - col0


def directions():
    return odd("face"), 1 - odd("face"), 2 + odd("tile"), 3 - odd("tile")


def first_gather(lists, field, face_first, face_second, tile_first, tile_second, held, table, list_sem, sem):
    copy, row, col = list_copy(0, lists, table, list_sem)
    copy.start()
    whole = pltpu.make_async_copy(field, held, sem)
    whole.start()
    copy.wait()
    whole.wait()
    for send, j in zip((face_first, face_second, tile_first, tile_second), directions()):
        for c in range(CAP):
            send[c] = held[table[row + j, col + c]]


def read_lists(step, lists, listed, table, list_sem):
    copy, row, col = list_copy(step, lists, table, list_sem)
    copy.start()
    copy.wait()
    at_row = lax.broadcasted_iota(jnp.int32, listed.shape, 0)
    at_col = lax.broadcasted_iota(jnp.int32, listed.shape, 1)
    values = jnp.zeros(listed.shape, jnp.int32)
    for k, j in enumerate(directions()):
        for c in range(CAP):
            values = jnp.where((at_row == k) & (at_col == c), table[row + j, col + c], values)
    listed[...] = values


def spread_weights(weights, high, low, joined):
    lane = lax.broadcasted_iota(jnp.int32, (16, 256), 1)
    row = lax.broadcasted_iota(jnp.int32, (16, 256), 0)
    spread = jnp.where(lane % 16 == row, 1.0, 0.0).astype(BF16)
    out_row = lax.broadcasted_iota(jnp.int32, (256, 256), 0)
    out_col = lax.broadcasted_iota(jnp.int32, (256, 256), 1)
    own = out_row // 16 == out_col // 16
    for step in range(weights.shape[0]):
        w = weights[step]
        w_high = w.astype(BF16)
        w_low = (w - w_high.astype(F32)).astype(BF16)
        joined[step] = jnp.concatenate([w_high, w_high, w_low], axis=1).reshape(16, 16, 48)
        for part, out in ((w_high, high), (w_low, low)):
            wide = jnp.dot(part, spread, preferred_element_type=F32)
            out[step] = jnp.where(own, wide, 0.0).astype(BF16)


def sublane(shape=(8, 1)):
    return lax.broadcasted_iota(jnp.int32, shape, 0)


def roll(x, by):
    return x if by % 8 == 0 else pltpu.roll(x, by % 8, 0)


def move_most(step, owner, slot, field, face_first, face_second, tile_first, high, low, joined,
              moved, far_weights, is_far, source, split_high, split_low):
    owners = (2 - odd("face"), 1 + odd("face"), 4 - odd("tile"))
    far = 3 + odd("tile")
    target = [jnp.int32(-1)] * CAP
    for e in range(ELEMS):
        o = owner[step, e // 4, e % 4]
        p = slot[step, e // 4, e % 4]
        c = jnp.minimum(p, CAP - 1)
        block = field[p]
        for code, arrived in zip(owners, (face_first, face_second, tile_first)):
            block = jnp.where(o == code, arrived[c], block)
        for k in range(CAP):
            hit = (o == far) & (p == k)
            target[k] = jnp.where(hit, e, target[k])
            is_far[k * ELEMS + e : k * ELEMS + e + 1, :] = jnp.full((1, 128), jnp.where(hit, 1.0, 0.0), F32)
        source[e] = block
        part = block.astype(BF16)
        split_high[pl.ds(e * 16, 16), :] = part
        split_low[pl.ds(e * 16, 16), :] = (block - part.astype(F32)).astype(BF16)
    for k in range(CAP):
        far_weights[k] = joined[step, jnp.maximum(target[k], 0)]
    wide = 256
    for n in range(0, field.shape[2], wide):
        cols = pl.ds(n, wide)
        s_high, s_low = split_high[:, cols], split_low[:, cols]
        w_high, w_low = high[step], low[step]
        total = jnp.dot(w_high, s_high, preferred_element_type=F32)
        total += jnp.dot(w_high, s_low, preferred_element_type=F32)
        total += jnp.dot(w_low, s_high, preferred_element_type=F32)
        for e in range(ELEMS):
            src = source[e, :, cols]
            least = jnp.min(src, axis=0, keepdims=True)
            most = jnp.max(src, axis=0, keepdims=True)
            moved[e, :, cols] = jnp.clip(total[e * 16 : e * 16 + 16], least, most)


def with_far(e, rows, cols, moved, far, is_far):
    t = moved[e, rows, cols]
    for k in range(CAP):
        t = jnp.where(is_far[k * ELEMS + e : k * ELEMS + e + 1, :] > 0.5, far[k, rows, cols], t)
    return t


def move_far(arrived, far_weights, moved, is_far, far, row_first, row_second):
    for k in range(CAP):
        src = arrived[k]
        s_high = src.astype(BF16)
        s_low = (src - s_high.astype(F32)).astype(BF16)
        total = jnp.dot(
            far_weights[k], jnp.concatenate([s_high, s_low, s_high], axis=0), preferred_element_type=F32
        )
        far[k] = jnp.clip(total, jnp.min(src, axis=0, keepdims=True), jnp.max(src, axis=0, keepdims=True))
    sub = sublane()
    flip = odd("face") == 1
    for n in range(0, moved.shape[2], 128):
        cols = slice(n, n + 128)
        packed = []
        for x, tile in ((0, 0), (3, 1)):
            rows = []
            for pair in range(2):
                at = slice(8 * tile, 8 * tile + 8)
                even = with_far(4 * x + 2 * pair, at, cols, moved, far, is_far)
                after = with_far(4 * x + 2 * pair + 1, at, cols, moved, far, is_far)
                if tile == 0:
                    rows.append(jnp.where(sub < 4, even, roll(after, 4)))
                else:
                    rows.append(jnp.where(sub < 4, roll(even, 4), after))
            left, right = rows
            inner = []
            for t in rows:
                t2 = jnp.where(sub == 3, 0.5 * (t + roll(t, 7)), t)
                inner.append(jnp.where(sub == 4, 0.5 * (t + roll(t, 1)), t2))
            inner[0] = jnp.where(sub == 7, 0.5 * (left + roll(right, 7)), inner[0])
            inner[1] = jnp.where(sub == 0, 0.5 * (right + roll(left, 1)), inner[1])
            packed.append(inner)
        for k in range(2):
            rows = slice(8 * k, 8 * k + 8)
            top, bottom = packed[0][k], packed[1][k]
            row_first[rows, cols] = jnp.where(flip, top, bottom)
            row_second[rows, cols] = jnp.where(flip, bottom, top)


def average_inside(moved, far, is_far, inside, left, right, draft, whole):
    sub = sublane()
    for e in range(ELEMS):
        for k in range(2):
            rows = slice(8 * k, 8 * k + 8)
            for n in range(0, moved.shape[2], 128):
                cols = slice(n, n + 128)
                whole[e, rows, cols] = with_far(e, rows, cols, moved, far, is_far)
    moved = whole
    first, last = sub % 4 == 0, sub % 4 == 3
    for e in range(ELEMS):
        y = e % 4
        for k in range(2):
            rows = slice(8 * k, 8 * k + 8)
            m = moved[e, rows, :]
            c = m
            if y < 3:
                c = jnp.where(last, 0.5 * (m + roll(moved[e + 1, rows, :], 3)), c)
            if y > 0:
                c = jnp.where(first, 0.5 * (m + roll(moved[e - 1, rows, :], 5)), c)
            draft[e, rows, :] = c
    for e in range(ELEMS):
        x = e // 4
        t0, t1 = draft[e, 0:8, :], draft[e, 8:16, :]
        if x > 0:
            t0 = jnp.where(sub < 4, 0.5 * (t0 + roll(draft[e - 4, 8:16, :], 4)), t0)
        if x < 3:
            t1 = jnp.where(sub >= 4, 0.5 * (t1 + roll(draft[e + 4, 0:8, :], 4)), t1)
        inside[e, 0:8, :] = t0
        inside[e, 8:16, :] = t1
    for out, y, at in ((left, 0, 0), (right, 3, 3)):
        for pair in range(2):
            packed = None
            for place in range(4):
                e = 4 * (2 * pair + place // 2) + y
                k = place % 2
                t = roll(inside[e, 8 * k : 8 * k + 8, :], place - at)
                packed = t if packed is None else jnp.where(sub % 4 == place, t, packed)
            out[8 * pair : 8 * pair + 8, :] = packed


def finish_columns(left, right, face_first, face_second, column_first, column_second):
    sub = sublane()
    flip = odd("face") == 1
    lo, hi = slice(0, 8), slice(8, 16)
    a0, a1, b0, b1 = (
        jnp.where(flip == from_first, face_first[rows, :], face_second[rows, :])
        for from_first in (True, False)
        for rows in (lo, hi)
    )
    l0 = jnp.where(sub == 0, 0.5 * (left[lo, :] + a0), left[lo, :])
    l1 = jnp.where(sub == 7, 0.5 * (left[hi, :] + roll(b0, 7)), left[hi, :])
    r0 = jnp.where(sub == 0, 0.5 * (right[lo, :] + roll(a1, 1)), right[lo, :])
    r1 = jnp.where(sub == 7, 0.5 * (right[hi, :] + b1), right[hi, :])
    flip = odd("tile") == 1
    for rows, l, r in ((lo, l0, r0), (hi, l1, r1)):
        column_first[rows, :] = jnp.where(flip, l, r)
        column_second[rows, :] = jnp.where(flip, r, l)


def finish_rows(inside, face_first, face_second, out):
    sub = sublane()
    flip = odd("face") == 1
    out[4:12] = inside[4:12]
    for y in range(4):
        first = face_first[8 * (y // 2) : 8 * (y // 2) + 8, :]
        second = face_second[8 * (y // 2) : 8 * (y // 2) + 8, :]
        a, b = jnp.where(flip, first, second), jnp.where(flip, second, first)
        t = inside[y, 0:8, :]
        out[y, 0:8, :] = jnp.where(sub < 4, 0.5 * (t + roll(a, 4 * (y % 2))), t)
        out[y, 8:16, :] = inside[y, 8:16, :]
        out[12 + y, 0:8, :] = inside[12 + y, 0:8, :]
        t = inside[12 + y, 8:16, :]
        out[12 + y, 8:16, :] = jnp.where(sub >= 4, 0.5 * (t + roll(b, 4 - 4 * (y % 2))), t)


def fix_edges(inside, tile_first, tile_second, put):
    sub = sublane()
    first, last = sub % 4 == 0, sub % 4 == 3
    flip = odd("tile") == 1
    for x in range(4):
        one = tile_first[8 * (x // 2) : 8 * (x // 2) + 8, :]
        two = tile_second[8 * (x // 2) : 8 * (x // 2) + 8, :]
        before, after = jnp.where(flip, one, two), jnp.where(flip, two, one)
        for k in range(2):
            place = 2 * (x % 2) + k
            rows = slice(8 * k, 8 * k + 8)
            t = inside[4 * x, rows, :]
            put(x, 0, rows, jnp.where(first, 0.5 * (t + roll(before, -place)), t))
            t = inside[4 * x + 3, rows, :]
            put(x, 1, rows, jnp.where(last, 0.5 * (t + roll(after, 3 - place)), t))


def finish_sends(listed, inside, tile_first, tile_second, *rest):
    sends, edges = rest[:4], rest[4]
    values = listed[...]

    def put(x, right, rows, t):
        edges[2 * x + right, rows, :] = t

    fix_edges(inside, tile_first, tile_second, put)
    for k in range(4):
        for c in range(CAP):
            e = values[k, c]
            y = e & 3
            at_edge = (y == 0) | (y == 3)
            place = 2 * (e >> 2) + (y >> 1)
            sends[k][c] = jnp.where(at_edge, edges[place], inside[e])


def finish_field(inside, tile_first, tile_second, field):
    def put(x, right, rows, t):
        field[4 * x + 3 * right, rows, :] = t

    fix_edges(inside, tile_first, tile_second, put)
    for x in range(4):
        field[4 * x + 1 : 4 * x + 3] = inside[4 * x + 1 : 4 * x + 3]


def finish_last(inside, tile_first, tile_second, field, edges, sems):
    copies = []
    for x in range(4):
        part = pl.ds(4 * x + 1, 2)
        copies.append(pltpu.make_async_copy(inside.at[part], field.at[part], sems.at[x]))
        copies[-1].start()

    def put(x, right, rows, t):
        edges[2 * x + right, rows, :] = t

    fix_edges(inside, tile_first, tile_second, put)
    for i in range(8):
        copies.append(
            pltpu.make_async_copy(edges.at[i], field.at[4 * (i // 2) + 3 * (i % 2)], sems.at[4 + i])
        )
        copies[-1].start()
    for copy in copies:
        copy.wait()


def swap(axis, offset, x):
    count = lax.axis_size(axis)
    pairs = []
    for i in range(offset, count + offset, 2):
        pairs += [(i % count, (i + 1) % count), ((i + 1) % count, i % count)]
    return lax.ppermute(x, axis, sorted(pairs))


def swaps(axis, first, second):
    return swap(axis, 0, first), swap(axis, 1, second)


def odd(axis):
    return lax.rem(lax.axis_index(axis), 2)


def transport(tracers, basis_weights, up_owner, up_slot, send_list):
    columns = tracers.shape[3]
    steps = basis_weights.shape[0]
    block = jax.ShapeDtypeStruct((ELEMS, NODES, columns), F32)
    edge = jax.ShapeDtypeStruct((16, columns), F32)
    listed = jax.ShapeDtypeStruct((CAP, NODES, columns), F32)
    mats = jax.ShapeDtypeStruct((steps, 256, 256), BF16)
    own = jax.ShapeDtypeStruct((steps, 16, 16, 48), BF16)
    far_own = jax.ShapeDtypeStruct((CAP, 16, 48), BF16)
    own_lists = jax.ShapeDtypeStruct((8, 128), jnp.int32)
    flags = jax.ShapeDtypeStruct((CAP * ELEMS, 128), F32)
    table = pltpu.SMEM(
        (min(8, send_list.shape[1]), 128 if send_list.shape[2] % 128 == 0 else send_list.shape[2]), jnp.int32
    )
    field = tracers.reshape(ELEMS, NODES, columns)
    weights = basis_weights.reshape(steps, 256, 16)

    lists_hbm = pltpu.with_memory_space_constraint(send_list, pltpu.HBM)
    field_hbm = pltpu.with_memory_space_constraint(field, pltpu.HBM)
    whole = pltpu.VMEM(block.shape, F32)
    edges = pltpu.VMEM((8, NODES, columns), F32)
    halves = pltpu.VMEM((256, columns), BF16)
    dma = pltpu.SemaphoreType.DMA
    *sends, field = run(first_gather, [HBM, HBM], [listed] * 4 + [block], 1, [table, dma, dma], lists_hbm, field_hbm)
    high, low, joined = run(spread_weights, [VMEM], [mats, mats, own], 1, [], weights)
    for step in range(steps):
        face = swaps("face", sends[0], sends[1])
        tile = swaps("tile", sends[2], sends[3])
        if step < steps - 1:
            upcoming = run(functools.partial(read_lists, step + 1), [HBM], own_lists, 1, [table, dma], lists_hbm)
        if step > 0:
            field = run(finish_field, [VMEM] * 3, block, 2, [], inside, *edge_tile)
        moved, far_weights, is_far = run(
            functools.partial(move_most, step), [SMEM, SMEM] + [VMEM] * 7,
            [block, far_own, flags], 5, [whole, halves, halves],
            up_owner, up_slot, field, *face, tile[0], high, low, joined,
        )
        far, *rows = run(move_far, [VMEM] * 4, [listed, edge, edge], 1, [], tile[1], far_weights, moved, is_far)
        edge_face = swaps("face", *rows)
        inside, left, right = run(
            average_inside, [VMEM] * 3, [block, edge, edge], 3, [whole, whole],
            moved, far, is_far,
        )
        ends = run(finish_columns, [VMEM] * 4, [edge] * 2, 1, [], left, right, *edge_face)
        edge_tile = swaps("tile", *ends)
        inside = run(finish_rows, [VMEM] * 3, block, 1, [], inside, *edge_face)
        if step < steps - 1:
            sends = run(finish_sends, [VMEM] * 4, [listed] * 4, 2, [edges], upcoming, inside, *edge_tile)
        else:
            field = run(
                finish_last, [VMEM] * 3, block, 2, [edges, dma((12,))], inside, *edge_tile,
                out_space=HBM,
            )
    return field.reshape(tracers.shape)


def solution(mesh):
    return jax.shard_map(
        transport,
        mesh=mesh,
        in_specs=(
            P("face", "tile", None, None),
            P(None, "face", "tile", None, None),
            P(None, "face", "tile"),
            P(None, "face", "tile"),
            P(),
        ),
        out_specs=P("face", "tile", None, None),
        check_vma=False,
    )
```

time: 103 us -> 94.7 us (0.919)
  the two profiles are of different devices: /device:TPU:64 before, /device:TPU:1 now
where the time goes in v3:
time: 94.7 us; the launch traced here: 94.1 us
  starting transfers between devices  64.8 us (68%)
  waiting for transfers between devices  18.7 us (20%)
  Pallas kernels  10.3 us (11%)
    ppermute x16, starting transfers between devices, swap(): return lax.ppermute(x, axis, sorted(pairs))  64.8 us
    ppermute x16, waiting for transfers between devices, swap(): return lax.ppermute(x, axis, sorted(pairs))  18.7 us
    pallas_call x16, Pallas kernels, run(): pl.pallas_call(kernel, out_shape=out, in_specs=in_specs, out_specs=out_sp...  10.3 us
  transfers between devices with their start and end apart: 16, of which 7 were waited for; matrix products, arithmetic and copies ran while one was open for 0% of the time, Pallas kernels for 7%

profile of v3, /device:TPU:1, one launch (start us, length us, event | category | flops | bytes accessed | tf_op | source)
XLA Modules:
  0.0 94.1 jit_solution(8417418270974088754)
XLA Ops:
  0.0 1.5 %shard_map.55 = (f32[4,16,1280]{2,1,0:T(8,128)S(1)}, f32[4,16,1280]{2,1,0:T(8,128)S(1)}, f32[4,16,1280]{2,1,0:T(8,128)S(1)}, f32[4,16,1280]{2,1,0:T(8,128)S(1)}, f32[16,16,1280]{2,1,0:T(8,128)S(1)}) custom-call(s32[2,48,256]{2,1,0:T(8,128)} %lists.3, f32[16,16,1280]{2,1,0:T(8,128)} %bitcast.4), custom_call_target="tpu_custom_call" | custom-call | bytes 1048576 | tf_op jit(solution)/shard_map/pallas_call | solution.py:22
  1.5 4.8 %collective-permute-start = (f32[4,16,1280]{2,1,0:T(8,128)S(1)}, f32[4,16,1280]{2,1,0:T(8,128)S(1)}, u32[]{:S(2)}, u32[]{:S(2)}) collective-permute-start(f32[4,16,1280]{2,1,0:T(8,128)S(1)} %get-tuple-element.40), channel_id=1, source_target_pairs={{0,64},{64,0},{128,192},{192,128},{256,320},{320,256},{384,448},{4... | collective-permute-start | bytes 983048 | tf_op jit(solution)/shard_map/ppermute | solution.py:327
  6.3 12.5 %collective-permute-start.1 = (f32[4,16,1280]{2,1,0:T(8,128)S(1)}, f32[4,16,1280]{2,1,0:T(8,128)S(1)}, u32[]{:S(2)}, u32[]{:S(2)}) collective-permute-start(f32[4,16,1280]{2,1,0:T(8,128)S(1)} %get-tuple-element.41), channel_id=1, source_target_pairs={{0,704},{64,128},{128,64},{192,256},{256,192},{320,384},{384,320},... | collective-permute-start | bytes 983048 | tf_op jit(solution)/shard_map/ppermute | solution.py:327
  18.8 3.1 %collective-permute-start.2 = (f32[4,16,1280]{2,1,0:T(8,128)S(1)}, f32[4,16,1280]{2,1,0:T(8,128)S(1)}, u32[]{:S(2)}, u32[]{:S(2)}) collective-permute-start(f32[4,16,1280]{2,1,0:T(8,128)S(1)} %get-tuple-element.42), channel_id=1, source_target_pairs={{0,1},{1,0},{2,3},{3,2},{4,5},{5,4},{6,7},{7,6},{8,9},{9,8},{10,11... | collective-permute-start | bytes 983048 | tf_op jit(solution)/shard_map/ppermute | solution.py:327
  22.0 3.1 %collective-permute-start.3 = (f32[4,16,1280]{2,1,0:T(8,128)S(1)}, f32[4,16,1280]{2,1,0:T(8,128)S(1)}, u32[]{:S(2)}, u32[]{:S(2)}) collective-permute-start(f32[4,16,1280]{2,1,0:T(8,128)S(1)} %get-tuple-element.47), channel_id=1, source_target_pairs={{0,63},{1,2},{2,1},{3,4},{4,3},{5,6},{6,5},{7,8},{8,7},{9,10},{10,... | collective-permute-start | bytes 983048 | tf_op jit(solution)/shard_map/ppermute | solution.py:327
  25.9 1.7 %shard_map.57 = (f32[16,16,1280]{2,1,0:T(8,128)S(1)}, bf16[4,16,48]{2,1,0:T(8,128)(2,1)S(1)}, f32[64,128]{1,0:T(8,128)S(1)}) custom-call(s32[2,4,4]{2,1,0:T(4,128)S(1)} %copy-done.1, s32[2,4,4]{2,1,0:T(4,128)S(1)} %copy-done.2, f32[16,16,1280]{2,1,0:T(8,128)S(1)} %get-tuple-element.39.field, f32[4,16,1280]{2,1,0:T(8,128)S(1)} %collective-permute-done.face_first, ...), custom_call_target="tpu_custom_call" | custom-call | bytes 5242880 | tf_op jit(solution)/shard_map/pallas_call | solution.py:22
  27.7 3.0 %collective-permute-done.3.arrived = f32[4,16,1280]{2,1,0:T(8,128)S(1)} collective-permute-done((f32[4,16,1280]{2,1,0:T(8,128)S(1)}, f32[4,16,1280]{2,1,0:T(8,128)S(1)}, u32[]{:S(2)}, u32[]{:S(2)}) %collective-permute-start.3) | collective-permute-done | bytes 327712 | tf_op jit(solution)/shard_map/ppermute | solution.py:327
  31.0 1.9 %collective-permute-start.4 = (f32[16,1280]{1,0:T(8,128)S(1)}, f32[16,1280]{1,0:T(8,128)S(1)}, u32[]{:S(2)}, u32[]{:S(2)}) collective-permute-start(f32[16,1280]{1,0:T(8,128)S(1)} %get-tuple-element.52), channel_id=1, source_target_pairs={{0,64},{64,0},{128,192},{192,128},{256,320},{320,256},{384,448},{4... | collective-permute-start | bytes 245768 | tf_op jit(solution)/shard_map/ppermute | solution.py:327
  33.0 2.8 %collective-permute-start.5 = (f32[16,1280]{1,0:T(8,128)S(1)}, f32[16,1280]{1,0:T(8,128)S(1)}, u32[]{:S(2)}, u32[]{:S(2)}) collective-permute-start(f32[16,1280]{1,0:T(8,128)S(1)} %get-tuple-element.53), channel_id=1, source_target_pairs={{0,704},{64,128},{128,64},{192,256},{256,192},{320,384},{384,320},... | collective-permute-start | bytes 245768 | tf_op jit(solution)/shard_map/ppermute | solution.py:327
  36.7 2.7 %collective-permute-done.5.face_second = f32[16,1280]{1,0:T(8,128)S(1)} collective-permute-done((f32[16,1280]{1,0:T(8,128)S(1)}, f32[16,1280]{1,0:T(8,128)S(1)}, u32[]{:S(2)}, u32[]{:S(2)}) %collective-permute-start.5) | collective-permute-done | bytes 81952 | tf_op jit(solution)/shard_map/ppermute | solution.py:327
  39.4 6.8 %collective-permute-start.6 = (f32[16,1280]{1,0:T(8,128)S(1)}, f32[16,1280]{1,0:T(8,128)S(1)}, u32[]{:S(2)}, u32[]{:S(2)}) collective-permute-start(f32[16,1280]{1,0:T(8,128)S(1)} %get-tuple-element.56), channel_id=1, source_target_pairs={{0,1},{1,0},{2,3},{3,2},{4,5},{5,4},{6,7},{7,6},{8,9},{9,8},{10,11... | collective-permute-start | bytes 245768 | tf_op jit(solution)/shard_map/ppermute | solution.py:327
  46.2 1.9 %collective-permute-start.7 = (f32[16,1280]{1,0:T(8,128)S(1)}, f32[16,1280]{1,0:T(8,128)S(1)}, u32[]{:S(2)}, u32[]{:S(2)}) collective-permute-start(f32[16,1280]{1,0:T(8,128)S(1)} %get-tuple-element.57), channel_id=1, source_target_pairs={{0,63},{1,2},{2,1},{3,4},{4,3},{5,6},{6,5},{7,8},{8,7},{9,10},{10,... | collective-permute-start | bytes 245768 | tf_op jit(solution)/shard_map/ppermute | solution.py:327
  49.0 2.9 %collective-permute-done.7.tile_second = f32[16,1280]{1,0:T(8,128)S(1)} collective-permute-done((f32[16,1280]{1,0:T(8,128)S(1)}, f32[16,1280]{1,0:T(8,128)S(1)}, u32[]{:S(2)}, u32[]{:S(2)}) %collective-permute-start.7) | collective-permute-done | bytes 81952 | tf_op jit(solution)/shard_map/ppermute | solution.py:327
  52.3 2.4 %collective-permute-start.8 = (f32[4,16,1280]{2,1,0:T(8,128)S(1)}, f32[4,16,1280]{2,1,0:T(8,128)S(1)}, u32[]{:S(2)}, u32[]{:S(2)}) collective-permute-start(f32[4,16,1280]{2,1,0:T(8,128)S(1)} %get-tuple-element.58), channel_id=1, source_target_pairs={{0,64},{64,0},{128,192},{192,128},{256,320},{320,256},{384,448},{4... | collective-permute-start | bytes 983048 | tf_op jit(solution)/shard_map/ppermute | solution.py:327
  54.7 2.6 %collective-permute-start.9 = (f32[4,16,1280]{2,1,0:T(8,128)S(1)}, f32[4,16,1280]{2,1,0:T(8,128)S(1)}, u32[]{:S(2)}, u32[]{:S(2)}) collective-permute-start(f32[4,16,1280]{2,1,0:T(8,128)S(1)} %get-tuple-element.59), channel_id=1, source_target_pairs={{0,704},{64,128},{128,64},{192,256},{256,192},{320,384},{384,320},... | collective-permute-start | bytes 983048 | tf_op jit(solution)/shard_map/ppermute | solution.py:327
  57.3 5.5 %collective-permute-start.10 = (f32[4,16,1280]{2,1,0:T(8,128)S(1)}, f32[4,16,1280]{2,1,0:T(8,128)S(1)}, u32[]{:S(2)}, u32[]{:S(2)}) collective-permute-start(f32[4,16,1280]{2,1,0:T(8,128)S(1)} %get-tuple-element.60), channel_id=1, source_target_pairs={{0,1},{1,0},{2,3},{3,2},{4,5},{5,4},{6,7},{7,6},{8,9},{9,8},{10,11... | collective-permute-start | bytes 983048 | tf_op jit(solution)/shard_map/ppermute | solution.py:327
  62.8 1.9 %collective-permute-start.11 = (f32[4,16,1280]{2,1,0:T(8,128)S(1)}, f32[4,16,1280]{2,1,0:T(8,128)S(1)}, u32[]{:S(2)}, u32[]{:S(2)}) collective-permute-start(f32[4,16,1280]{2,1,0:T(8,128)S(1)} %get-tuple-element.62), channel_id=1, source_target_pairs={{0,63},{1,2},{2,1},{3,4},{4,3},{5,6},{6,5},{7,8},{8,7},{9,10},{10,... | collective-permute-start | bytes 983048 | tf_op jit(solution)/shard_map/ppermute | solution.py:327
  64.9 1.7 %shard_map.65 = (f32[16,16,1280]{2,1,0:T(8,128)S(1)}, bf16[4,16,48]{2,1,0:T(8,128)(2,1)S(1)}, f32[64,128]{1,0:T(8,128)S(1)}) custom-call(s32[2,4,4]{2,1,0:T(4,128)S(1)} %copy-done.1, s32[2,4,4]{2,1,0:T(4,128)S(1)} %copy-done.2, f32[16,16,1280]{2,1,0:T(8,128)S(1)} %shard_map.62.field, f32[4,16,1280]{2,1,0:T(8,128)S(1)} %collective-permute-done.8.face_first, ...), custom_call_target="tpu_custom_call" | custom-call | bytes 5242880 | tf_op jit(solution)/shard_map/pallas_call | solution.py:22
  66.6 4.9 %collective-permute-done.11.arrived = f32[4,16,1280]{2,1,0:T(8,128)S(1)} collective-permute-done((f32[4,16,1280]{2,1,0:T(8,128)S(1)}, f32[4,16,1280]{2,1,0:T(8,128)S(1)}, u32[]{:S(2)}, u32[]{:S(2)}) %collective-permute-start.11) | collective-permute-done | bytes 327712 | tf_op jit(solution)/shard_map/ppermute | solution.py:327
  71.9 2.2 %collective-permute-start.12 = (f32[16,1280]{1,0:T(8,128)S(1)}, f32[16,1280]{1,0:T(8,128)S(1)}, u32[]{:S(2)}, u32[]{:S(2)}) collective-permute-start(f32[16,1280]{1,0:T(8,128)S(1)} %get-tuple-element.67), channel_id=1, source_target_pairs={{0,64},{64,0},{128,192},{192,128},{256,320},{320,256},{384,448},{4... | collective-permute-start | bytes 245768 | tf_op jit(solution)/shard_map/ppermute | solution.py:327
  74.1 5.1 %collective-permute-start.13 = (f32[16,1280]{1,0:T(8,128)S(1)}, f32[16,1280]{1,0:T(8,128)S(1)}, u32[]{:S(2)}, u32[]{:S(2)}) collective-permute-start(f32[16,1280]{1,0:T(8,128)S(1)} %get-tuple-element.68), channel_id=1, source_target_pairs={{0,704},{64,128},{128,64},{192,256},{256,192},{320,384},{384,320},... | collective-permute-start | bytes 245768 | tf_op jit(solution)/shard_map/ppermute | solution.py:327
  81.1 6.1 %collective-permute-start.14 = (f32[16,1280]{1,0:T(8,128)S(1)}, f32[16,1280]{1,0:T(8,128)S(1)}, u32[]{:S(2)}, u32[]{:S(2)}) collective-permute-start(f32[16,1280]{1,0:T(8,128)S(1)} %get-tuple-element.71), channel_id=1, source_target_pairs={{0,1},{1,0},{2,3},{3,2},{4,5},{5,4},{6,7},{7,6},{8,9},{9,8},{10,11... | collective-permute-start | bytes 245768 | tf_op jit(solution)/shard_map/ppermute | solution.py:327
  87.2 1.9 %collective-permute-start.15 = (f32[16,1280]{1,0:T(8,128)S(1)}, f32[16,1280]{1,0:T(8,128)S(1)}, u32[]{:S(2)}, u32[]{:S(2)}) collective-permute-start(f32[16,1280]{1,0:T(8,128)S(1)} %get-tuple-element.72), channel_id=1, source_target_pairs={{0,63},{1,2},{2,1},{3,4},{4,3},{5,6},{6,5},{7,8},{8,7},{9,10},{10,... | collective-permute-start | bytes 245768 | tf_op jit(solution)/shard_map/ppermute | solution.py:327
  89.2 3.7 %collective-permute-done.15.tile_second = f32[16,1280]{1,0:T(8,128)S(1)} collective-permute-done((f32[16,1280]{1,0:T(8,128)S(1)}, f32[16,1280]{1,0:T(8,128)S(1)}, u32[]{:S(2)}, u32[]{:S(2)}) %collective-permute-start.15) | collective-permute-done | bytes 81952 | tf_op jit(solution)/shard_map/ppermute | solution.py:327
  (30 shorter events, 6.9 us)
Async XLA Ops:
  0.0 25.1 %copy-start = (f32[2,4,4,16,16]{4,3,2,1,0:T(8,128)S(1)}, f32[2,4,4,16,16]{4,3,2,1,0:T(8,128)}, u32[]{:S(2)}) copy-start(f32[2,4,4,16,16]{4,3,2,1,0:T(8,128)} %param.6) | copy-start | bytes 98308
  0.0 25.9 %copy-start.2 = (s32[2,4,4]{2,1,0:T(4,128)S(1)}, s32[2,4,4]{2,1,0:T(4,128)}, u32[]{:S(2)}) copy-start(s32[2,4,4]{2,1,0:T(4,128)} %slot.3) | copy-start | bytes 388
  0.0 25.9 %copy-start.1 = (s32[2,4,4]{2,1,0:T(4,128)S(1)}, s32[2,4,4]{2,1,0:T(4,128)}, u32[]{:S(2)}) copy-start(s32[2,4,4]{2,1,0:T(4,128)} %owner.3) | copy-start | bytes 388
  1.5 23.9 %collective-permute-start = (f32[4,16,1280]{2,1,0:T(8,128)S(1)}, f32[4,16,1280]{2,1,0:T(8,128)S(1)}, u32[]{:S(2)}, u32[]{:S(2)}) collective-permute-start(f32[4,16,1280]{2,1,0:T(8,128)S(1)} %get-tuple-element.40), channel_id=1, source_target_pairs={{0,64},{64,0},{128,192},{192,128},{256,320},{320,256},{384,448},{4... | collective-permute-start | bytes 983048 | tf_op jit(solution)/shard_map/ppermute | solution.py:327
  6.3 19.6 %collective-permute-start.1 = (f32[4,16,1280]{2,1,0:T(8,128)S(1)}, f32[4,16,1280]{2,1,0:T(8,128)S(1)}, u32[]{:S(2)}, u32[]{:S(2)}) collective-permute-start(f32[4,16,1280]{2,1,0:T(8,128)S(1)} %get-tuple-element.41), channel_id=1, source_target_pairs={{0,704},{64,128},{128,64},{192,256},{256,192},{320,384},{384,320},... | collective-permute-start | bytes 983048 | tf_op jit(solution)/shard_map/ppermute | solution.py:327
  18.8 7.1 %collective-permute-start.2 = (f32[4,16,1280]{2,1,0:T(8,128)S(1)}, f32[4,16,1280]{2,1,0:T(8,128)S(1)}, u32[]{:S(2)}, u32[]{:S(2)}) collective-permute-start(f32[4,16,1280]{2,1,0:T(8,128)S(1)} %get-tuple-element.42), channel_id=1, source_target_pairs={{0,1},{1,0},{2,3},{3,2},{4,5},{5,4},{6,7},{7,6},{8,9},{9,8},{10,11... | collective-permute-start | bytes 983048 | tf_op jit(solution)/shard_map/ppermute | solution.py:327
  22.0 8.7 %collective-permute-start.3 = (f32[4,16,1280]{2,1,0:T(8,128)S(1)}, f32[4,16,1280]{2,1,0:T(8,128)S(1)}, u32[]{:S(2)}, u32[]{:S(2)}) collective-permute-start(f32[4,16,1280]{2,1,0:T(8,128)S(1)} %get-tuple-element.47), channel_id=1, source_target_pairs={{0,63},{1,2},{2,1},{3,4},{4,3},{5,6},{6,5},{7,8},{8,7},{9,10},{10,... | collective-permute-start | bytes 983048 | tf_op jit(solution)/shard_map/ppermute | solution.py:327
  31.0 5.6 %collective-permute-start.4 = (f32[16,1280]{1,0:T(8,128)S(1)}, f32[16,1280]{1,0:T(8,128)S(1)}, u32[]{:S(2)}, u32[]{:S(2)}) collective-permute-start(f32[16,1280]{1,0:T(8,128)S(1)} %get-tuple-element.52), channel_id=1, source_target_pairs={{0,64},{64,0},{128,192},{192,128},{256,320},{320,256},{384,448},{4... | collective-permute-start | bytes 245768 | tf_op jit(solution)/shard_map/ppermute | solution.py:327
  33.0 6.4 %collective-permute-start.5 = (f32[16,1280]{1,0:T(8,128)S(1)}, f32[16,1280]{1,0:T(8,128)S(1)}, u32[]{:S(2)}, u32[]{:S(2)}) collective-permute-start(f32[16,1280]{1,0:T(8,128)S(1)} %get-tuple-element.53), channel_id=1, source_target_pairs={{0,704},{64,128},{128,64},{192,256},{256,192},{320,384},{384,320},... | collective-permute-start | bytes 245768 | tf_op jit(solution)/shard_map/ppermute | solution.py:327
  39.4 9.6 %collective-permute-start.6 = (f32[16,1280]{1,0:T(8,128)S(1)}, f32[16,1280]{1,0:T(8,128)S(1)}, u32[]{:S(2)}, u32[]{:S(2)}) collective-permute-start(f32[16,1280]{1,0:T(8,128)S(1)} %get-tuple-element.56), channel_id=1, source_target_pairs={{0,1},{1,0},{2,3},{3,2},{4,5},{5,4},{6,7},{7,6},{8,9},{9,8},{10,11... | collective-permute-start | bytes 245768 | tf_op jit(solution)/shard_map/ppermute | solution.py:327
  46.2 5.8 %collective-permute-start.7 = (f32[16,1280]{1,0:T(8,128)S(1)}, f32[16,1280]{1,0:T(8,128)S(1)}, u32[]{:S(2)}, u32[]{:S(2)}) collective-permute-start(f32[16,1280]{1,0:T(8,128)S(1)} %get-tuple-element.57), channel_id=1, source_target_pairs={{0,63},{1,2},{2,1},{3,4},{4,3},{5,6},{6,5},{7,8},{8,7},{9,10},{10,... | collective-permute-start | bytes 245768 | tf_op jit(solution)/shard_map/ppermute | solution.py:327
  52.3 12.6 %collective-permute-start.8 = (f32[4,16,1280]{2,1,0:T(8,128)S(1)}, f32[4,16,1280]{2,1,0:T(8,128)S(1)}, u32[]{:S(2)}, u32[]{:S(2)}) collective-permute-start(f32[4,16,1280]{2,1,0:T(8,128)S(1)} %get-tuple-element.58), channel_id=1, source_target_pairs={{0,64},{64,0},{128,192},{192,128},{256,320},{320,256},{384,448},{4... | collective-permute-start | bytes 983048 | tf_op jit(solution)/shard_map/ppermute | solution.py:327
  54.7 10.2 %collective-permute-start.9 = (f32[4,16,1280]{2,1,0:T(8,128)S(1)}, f32[4,16,1280]{2,1,0:T(8,128)S(1)}, u32[]{:S(2)}, u32[]{:S(2)}) collective-permute-start(f32[4,16,1280]{2,1,0:T(8,128)S(1)} %get-tuple-element.59), channel_id=1, source_target_pairs={{0,704},{64,128},{128,64},{192,256},{256,192},{320,384},{384,320},... | collective-permute-start | bytes 983048 | tf_op jit(solution)/shard_map/ppermute | solution.py:327
  57.3 7.6 %collective-permute-start.10 = (f32[4,16,1280]{2,1,0:T(8,128)S(1)}, f32[4,16,1280]{2,1,0:T(8,128)S(1)}, u32[]{:S(2)}, u32[]{:S(2)}) collective-permute-start(f32[4,16,1280]{2,1,0:T(8,128)S(1)} %get-tuple-element.60), channel_id=1, source_target_pairs={{0,1},{1,0},{2,3},{3,2},{4,5},{5,4},{6,7},{7,6},{8,9},{9,8},{10,11... | collective-permute-start | bytes 983048 | tf_op jit(solution)/shard_map/ppermute | solution.py:327
  62.8 8.7 %collective-permute-start.11 = (f32[4,16,1280]{2,1,0:T(8,128)S(1)}, f32[4,16,1280]{2,1,0:T(8,128)S(1)}, u32[]{:S(2)}, u32[]{:S(2)}) collective-permute-start(f32[4,16,1280]{2,1,0:T(8,128)S(1)} %get-tuple-element.62), channel_id=1, source_target_pairs={{0,63},{1,2},{2,1},{3,4},{4,3},{5,6},{6,5},{7,8},{8,7},{9,10},{10,... | collective-permute-start | bytes 983048 | tf_op jit(solution)/shard_map/ppermute | solution.py:327
  71.9 8.2 %collective-permute-start.12 = (f32[16,1280]{1,0:T(8,128)S(1)}, f32[16,1280]{1,0:T(8,128)S(1)}, u32[]{:S(2)}, u32[]{:S(2)}) collective-permute-start(f32[16,1280]{1,0:T(8,128)S(1)} %get-tuple-element.67), channel_id=1, source_target_pairs={{0,64},{64,0},{128,192},{192,128},{256,320},{320,256},{384,448},{4... | collective-permute-start | bytes 245768 | tf_op jit(solution)/shard_map/ppermute | solution.py:327
  74.1 6.9 %collective-permute-start.13 = (f32[16,1280]{1,0:T(8,128)S(1)}, f32[16,1280]{1,0:T(8,128)S(1)}, u32[]{:S(2)}, u32[]{:S(2)}) collective-permute-start(f32[16,1280]{1,0:T(8,128)S(1)} %get-tuple-element.68), channel_id=1, source_target_pairs={{0,704},{64,128},{128,64},{192,256},{256,192},{320,384},{384,320},... | collective-permute-start | bytes 245768 | tf_op jit(solution)/shard_map/ppermute | solution.py:327
  81.1 8.1 %collective-permute-start.14 = (f32[16,1280]{1,0:T(8,128)S(1)}, f32[16,1280]{1,0:T(8,128)S(1)}, u32[]{:S(2)}, u32[]{:S(2)}) collective-permute-start(f32[16,1280]{1,0:T(8,128)S(1)} %get-tuple-element.71), channel_id=1, source_target_pairs={{0,1},{1,0},{2,3},{3,2},{4,5},{5,4},{6,7},{7,6},{8,9},{9,8},{10,11... | collective-permute-start | bytes 245768 | tf_op jit(solution)/shard_map/ppermute | solution.py:327
  87.2 5.8 %collective-permute-start.15 = (f32[16,1280]{1,0:T(8,128)S(1)}, f32[16,1280]{1,0:T(8,128)S(1)}, u32[]{:S(2)}, u32[]{:S(2)}) collective-permute-start(f32[16,1280]{1,0:T(8,128)S(1)} %get-tuple-element.72), channel_id=1, source_target_pairs={{0,63},{1,2},{2,1},{3,4},{4,3},{5,6},{6,5},{7,8},{8,7},{9,10},{10,... | collective-permute-start | bytes 245768 | tf_op jit(solution)/shard_map/ppermute | solution.py:327

commit v4 on v3

--- a/solution.py
+++ b/solution.py
@@ -12,6 +12,7 @@
 VMEM = pl.BlockSpec(memory_space=pltpu.VMEM)
 SMEM = pl.BlockSpec(memory_space=pltpu.SMEM)
 HBM = pl.BlockSpec(memory_space=pltpu.HBM)
+LAST = 0
 ELEMS = 16
 NODES = 16
 CAP = 4
@@ -44,7 +45,7 @@
 
 
 def directions():
-    return odd("face"), 1 - odd("face"), 2 + odd("tile"), 3 - odd("tile")
+    return odd("mixed"), 1 - odd("mixed"), 2 + odd("tile"), 3 - odd("tile")
 
 
 def first_gather(lists, field, face_first, face_second, tile_first, tile_second, held, table, list_sem, sem):
@@ -97,17 +98,17 @@
     return x if by % 8 == 0 else pltpu.roll(x, by % 8, 0)
 
 
-def move_most(step, owner, slot, field, face_first, face_second, tile_first, high, low, joined,
+def move_most(step, owner, slot, field, early_a, early_b, early_c, high, low, joined,
               moved, far_weights, is_far, source, split_high, split_low):
-    owners = (2 - odd("face"), 1 + odd("face"), 4 - odd("tile"))
-    far = 3 + odd("tile")
+    owners = [2 - odd("mixed"), 1 + odd("mixed"), 4 - odd("tile"), 3 + odd("tile")]
+    far = owners.pop(LAST)
     target = [jnp.int32(-1)] * CAP
     for e in range(ELEMS):
         o = owner[step, e // 4, e % 4]
         p = slot[step, e // 4, e % 4]
         c = jnp.minimum(p, CAP - 1)
         block = field[p]
-        for code, arrived in zip(owners, (face_first, face_second, tile_first)):
+        for code, arrived in zip(owners, (early_a, early_b, early_c)):
             block = jnp.where(o == code, arrived[c], block)
         for k in range(CAP):
             hit = (o == far) & (p == k)
@@ -319,12 +320,16 @@
         copy.wait()
 
 
-def swap(axis, offset, x):
-    count = lax.axis_size(axis)
+def swap(axis, slot, x):
+    faces, tiles = lax.axis_size("face"), lax.axis_size("tile")
     pairs = []
-    for i in range(offset, count + offset, 2):
-        pairs += [(i % count, (i + 1) % count), ((i + 1) % count, i % count)]
-    return lax.ppermute(x, axis, sorted(pairs))
+    for f in range(faces):
+        for t in range(tiles):
+            parity = {"face": f, "mixed": f + t, "tile": t}[axis]
+            step = 1 if (parity + slot) % 2 == 0 else -1
+            target = f * tiles + (t + step) % tiles if axis == "tile" else (f + step) % faces * tiles + t
+            pairs.append((f * tiles + t, target))
+    return lax.ppermute(x, ("face", "tile"), pairs)
 
 
 def swaps(axis, first, second):
@@ -332,7 +337,10 @@
 
 
 def odd(axis):
-    return lax.rem(lax.axis_index(axis), 2)
+    place = lax.axis_index("face" if axis == "face" else "tile")
+    if axis == "mixed":
+        place += lax.axis_index("face")
+    return lax.rem(place, 2)
 
 
 def transport(tracers, basis_weights, up_owner, up_slot, send_list):
@@ -361,18 +369,20 @@
     *sends, field = run(first_gather, [HBM, HBM], [listed] * 4 + [block], 1, [table, dma, dma], lists_hbm, field_hbm)
     high, low, joined = run(spread_weights, [VMEM], [mats, mats, own], 1, [], weights)
     for step in range(steps):
-        face = swaps("face", sends[0], sends[1])
+        face = swaps("mixed", sends[0], sends[1])
         tile = swaps("tile", sends[2], sends[3])
         if step < steps - 1:
             upcoming = run(functools.partial(read_lists, step + 1), [HBM], own_lists, 1, [table, dma], lists_hbm)
         if step > 0:
             field = run(finish_field, [VMEM] * 3, block, 2, [], inside, *edge_tile)
+        blocks = [*face, *tile]
+        last = blocks.pop(LAST)
         moved, far_weights, is_far = run(
             functools.partial(move_most, step), [SMEM, SMEM] + [VMEM] * 7,
             [block, far_own, flags], 5, [whole, halves, halves],
-            up_owner, up_slot, field, *face, tile[0], high, low, joined,
+            up_owner, up_slot, field, *blocks, high, low, joined,
         )
-        far, *rows = run(move_far, [VMEM] * 4, [listed, edge, edge], 1, [], tile[1], far_weights, moved, is_far)
+        far, *rows = run(move_far, [VMEM] * 4, [listed, edge, edge], 1, [], last, far_weights, moved, is_far)
         edge_face = swaps("face", *rows)
         inside, left, right = run(
             average_inside, [VMEM] * 3, [block, edge, edge], 3, [whole, whole],

time: 94.7 us -> 95.3 us (level)
  the two profiles are of different devices: /device:TPU:1 before, /device:TPU:64 now
where the time goes in v4:
time: 95.3 us; the launch traced here: 94.7 us
  starting transfers between devices  59.8 us (63%)
  waiting for transfers between devices  24.3 us (25%)
  Pallas kernels  10.3 us (11%)
    ppermute x16, starting transfers between devices, swap(): return lax.ppermute(x, ('face', 'tile'), pairs)  59.8 us
    ppermute x16, waiting for transfers between devices, swap(): return lax.ppermute(x, ('face', 'tile'), pairs)  24.3 us
    pallas_call x16, Pallas kernels, run(): pl.pallas_call(kernel, out_shape=out, in_specs=in_specs, out_specs=out_sp...  10.3 us
  transfers between devices with their start and end apart: 16, of which 7 were waited for; matrix products, arithmetic and copies ran while one was open for 0% of the time, Pallas kernels for 7%

profile of v4, /device:TPU:64, one launch (start us, length us, event | category | flops | bytes accessed | tf_op | source)
XLA Modules:
  0.0 94.7 jit_solution(9778882509215433865)
XLA Ops:
  1.5 4.3 %collective-permute-start = (f32[4,16,1280]{2,1,0:T(8,128)S(1)}, f32[4,16,1280]{2,1,0:T(8,128)S(1)}, u32[]{:S(2)}, u32[]{:S(2)}) collective-permute-start(f32[4,16,1280]{2,1,0:T(8,128)S(1)} %get-tuple-element.40), channel_id=1, source_target_pairs={{0,704},{1,65},{2,706},{3,67},{4,708},{5,69},{6,710},{7,71},{8,712... | collective-permute-start | bytes 983048 | tf_op jit(solution)/shard_map/ppermute | solution.py:332
  5.8 1.9 %collective-permute-start.1 = (f32[4,16,1280]{2,1,0:T(8,128)S(1)}, f32[4,16,1280]{2,1,0:T(8,128)S(1)}, u32[]{:S(2)}, u32[]{:S(2)}) collective-permute-start(f32[4,16,1280]{2,1,0:T(8,128)S(1)} %get-tuple-element.41), channel_id=1, source_target_pairs={{0,1},{1,0},{2,3},{3,2},{4,5},{5,4},{6,7},{7,6},{8,9},{9,8},{10,11... | collective-permute-start | bytes 983048 | tf_op jit(solution)/shard_map/ppermute | solution.py:332
  7.7 7.7 %collective-permute-start.2 = (f32[4,16,1280]{2,1,0:T(8,128)S(1)}, f32[4,16,1280]{2,1,0:T(8,128)S(1)}, u32[]{:S(2)}, u32[]{:S(2)}) collective-permute-start(f32[4,16,1280]{2,1,0:T(8,128)S(1)} %get-tuple-element.42), channel_id=1, source_target_pairs={{0,63},{1,2},{2,1},{3,4},{4,3},{5,6},{6,5},{7,8},{8,7},{9,10},{10,... | collective-permute-start | bytes 983048 | tf_op jit(solution)/shard_map/ppermute | solution.py:332
  15.4 11.9 %collective-permute-start.3 = (f32[4,16,1280]{2,1,0:T(8,128)S(1)}, f32[4,16,1280]{2,1,0:T(8,128)S(1)}, u32[]{:S(2)}, u32[]{:S(2)}) collective-permute-start(f32[4,16,1280]{2,1,0:T(8,128)S(1)} %get-tuple-element.47), channel_id=1, source_target_pairs={{0,64},{1,705},{2,66},{3,707},{4,68},{5,709},{6,70},{7,711},{8,72}... | collective-permute-start | bytes 983048 | tf_op jit(solution)/shard_map/ppermute | solution.py:332
  27.6 1.7 %shard_map.57 = (f32[16,16,1280]{2,1,0:T(8,128)S(1)}, bf16[4,16,48]{2,1,0:T(8,128)(2,1)S(1)}, f32[64,128]{1,0:T(8,128)S(1)}) custom-call(s32[2,4,4]{2,1,0:T(4,128)S(1)} %copy-done.1, s32[2,4,4]{2,1,0:T(4,128)S(1)} %copy-done.2, f32[16,16,1280]{2,1,0:T(8,128)S(1)} %get-tuple-element.39.field, f32[4,16,1280]{2,1,0:T(8,128)S(1)} %collective-permute-done.early_a, ...), custom_call_target="tpu_custom_call" | custom-call | bytes 5242880 | tf_op jit(solution)/shard_map/pallas_call | solution.py:23
  29.3 2.9 %collective-permute-done.3.arrived = f32[4,16,1280]{2,1,0:T(8,128)S(1)} collective-permute-done((f32[4,16,1280]{2,1,0:T(8,128)S(1)}, f32[4,16,1280]{2,1,0:T(8,128)S(1)}, u32[]{:S(2)}, u32[]{:S(2)}) %collective-permute-start.3) | collective-permute-done | bytes 327712 | tf_op jit(solution)/shard_map/ppermute | solution.py:332
  32.7 3.9 %collective-permute-start.4 = (f32[16,1280]{1,0:T(8,128)S(1)}, f32[16,1280]{1,0:T(8,128)S(1)}, u32[]{:S(2)}, u32[]{:S(2)}) collective-permute-start(f32[16,1280]{1,0:T(8,128)S(1)} %get-tuple-element.52), channel_id=1, source_target_pairs={{0,64},{1,65},{2,66},{3,67},{4,68},{5,69},{6,70},{7,71},{8,72},{9,... | collective-permute-start | bytes 245768 | tf_op jit(solution)/shard_map/ppermute | solution.py:332
  36.6 1.9 %collective-permute-start.5 = (f32[16,1280]{1,0:T(8,128)S(1)}, f32[16,1280]{1,0:T(8,128)S(1)}, u32[]{:S(2)}, u32[]{:S(2)}) collective-permute-start(f32[16,1280]{1,0:T(8,128)S(1)} %get-tuple-element.53), channel_id=1, source_target_pairs={{0,704},{1,705},{2,706},{3,707},{4,708},{5,709},{6,710},{7,711},{8... | collective-permute-start | bytes 245768 | tf_op jit(solution)/shard_map/ppermute | solution.py:332
  39.4 3.5 %collective-permute-done.5.face_second = f32[16,1280]{1,0:T(8,128)S(1)} collective-permute-done((f32[16,1280]{1,0:T(8,128)S(1)}, f32[16,1280]{1,0:T(8,128)S(1)}, u32[]{:S(2)}, u32[]{:S(2)}) %collective-permute-start.5) | collective-permute-done | bytes 81952 | tf_op jit(solution)/shard_map/ppermute | solution.py:332
  43.0 1.9 %collective-permute-start.6 = (f32[16,1280]{1,0:T(8,128)S(1)}, f32[16,1280]{1,0:T(8,128)S(1)}, u32[]{:S(2)}, u32[]{:S(2)}) collective-permute-start(f32[16,1280]{1,0:T(8,128)S(1)} %get-tuple-element.56), channel_id=1, source_target_pairs={{0,1},{1,0},{2,3},{3,2},{4,5},{5,4},{6,7},{7,6},{8,9},{9,8},{10,11... | collective-permute-start | bytes 245768 | tf_op jit(solution)/shard_map/ppermute | solution.py:332
  44.9 3.9 %collective-permute-start.7 = (f32[16,1280]{1,0:T(8,128)S(1)}, f32[16,1280]{1,0:T(8,128)S(1)}, u32[]{:S(2)}, u32[]{:S(2)}) collective-permute-start(f32[16,1280]{1,0:T(8,128)S(1)} %get-tuple-element.57), channel_id=1, source_target_pairs={{0,63},{1,2},{2,1},{3,4},{4,3},{5,6},{6,5},{7,8},{8,7},{9,10},{10,... | collective-permute-start | bytes 245768 | tf_op jit(solution)/shard_map/ppermute | solution.py:332
  49.7 4.3 %collective-permute-done.7.tile_second = f32[16,1280]{1,0:T(8,128)S(1)} collective-permute-done((f32[16,1280]{1,0:T(8,128)S(1)}, f32[16,1280]{1,0:T(8,128)S(1)}, u32[]{:S(2)}, u32[]{:S(2)}) %collective-permute-start.7) | collective-permute-done | bytes 81952 | tf_op jit(solution)/shard_map/ppermute | solution.py:332
  54.3 1.9 %collective-permute-start.8 = (f32[4,16,1280]{2,1,0:T(8,128)S(1)}, f32[4,16,1280]{2,1,0:T(8,128)S(1)}, u32[]{:S(2)}, u32[]{:S(2)}) collective-permute-start(f32[4,16,1280]{2,1,0:T(8,128)S(1)} %get-tuple-element.58), channel_id=1, source_target_pairs={{0,704},{1,65},{2,706},{3,67},{4,708},{5,69},{6,710},{7,71},{8,712... | collective-permute-start | bytes 983048 | tf_op jit(solution)/shard_map/ppermute | solution.py:332
  56.2 1.9 %collective-permute-start.9 = (f32[4,16,1280]{2,1,0:T(8,128)S(1)}, f32[4,16,1280]{2,1,0:T(8,128)S(1)}, u32[]{:S(2)}, u32[]{:S(2)}) collective-permute-start(f32[4,16,1280]{2,1,0:T(8,128)S(1)} %get-tuple-element.59), channel_id=1, source_target_pairs={{0,1},{1,0},{2,3},{3,2},{4,5},{5,4},{6,7},{7,6},{8,9},{9,8},{10,11... | collective-permute-start | bytes 983048 | tf_op jit(solution)/shard_map/ppermute | solution.py:332
  58.1 4.5 %collective-permute-start.10 = (f32[4,16,1280]{2,1,0:T(8,128)S(1)}, f32[4,16,1280]{2,1,0:T(8,128)S(1)}, u32[]{:S(2)}, u32[]{:S(2)}) collective-permute-start(f32[4,16,1280]{2,1,0:T(8,128)S(1)} %get-tuple-element.60), channel_id=1, source_target_pairs={{0,63},{1,2},{2,1},{3,4},{4,3},{5,6},{6,5},{7,8},{8,7},{9,10},{10,... | collective-permute-start | bytes 983048 | tf_op jit(solution)/shard_map/ppermute | solution.py:332
  62.6 3.0 %collective-permute-start.11 = (f32[4,16,1280]{2,1,0:T(8,128)S(1)}, f32[4,16,1280]{2,1,0:T(8,128)S(1)}, u32[]{:S(2)}, u32[]{:S(2)}) collective-permute-start(f32[4,16,1280]{2,1,0:T(8,128)S(1)} %get-tuple-element.62), channel_id=1, source_target_pairs={{0,64},{1,705},{2,66},{3,707},{4,68},{5,709},{6,70},{7,711},{8,72}... | collective-permute-start | bytes 983048 | tf_op jit(solution)/shard_map/ppermute | solution.py:332
  65.8 4.0 %collective-permute-done.10.early_c = f32[4,16,1280]{2,1,0:T(8,128)S(1)} collective-permute-done((f32[4,16,1280]{2,1,0:T(8,128)S(1)}, f32[4,16,1280]{2,1,0:T(8,128)S(1)}, u32[]{:S(2)}, u32[]{:S(2)}) %collective-permute-start.10) | collective-permute-done | bytes 327712 | tf_op jit(solution)/shard_map/ppermute | solution.py:332
  69.8 1.7 %shard_map.65 = (f32[16,16,1280]{2,1,0:T(8,128)S(1)}, bf16[4,16,48]{2,1,0:T(8,128)(2,1)S(1)}, f32[64,128]{1,0:T(8,128)S(1)}) custom-call(s32[2,4,4]{2,1,0:T(4,128)S(1)} %copy-done.1, s32[2,4,4]{2,1,0:T(4,128)S(1)} %copy-done.2, f32[16,16,1280]{2,1,0:T(8,128)S(1)} %shard_map.62.field, f32[4,16,1280]{2,1,0:T(8,128)S(1)} %collective-permute-done.8.early_a, ...), custom_call_target="tpu_custom_call" | custom-call | bytes 5242880 | tf_op jit(solution)/shard_map/pallas_call | solution.py:23
  72.0 4.1 %collective-permute-start.12 = (f32[16,1280]{1,0:T(8,128)S(1)}, f32[16,1280]{1,0:T(8,128)S(1)}, u32[]{:S(2)}, u32[]{:S(2)}) collective-permute-start(f32[16,1280]{1,0:T(8,128)S(1)} %get-tuple-element.67), channel_id=1, source_target_pairs={{0,64},{1,65},{2,66},{3,67},{4,68},{5,69},{6,70},{7,71},{8,72},{9,... | collective-permute-start | bytes 245768 | tf_op jit(solution)/shard_map/ppermute | solution.py:332
  76.2 1.9 %collective-permute-start.13 = (f32[16,1280]{1,0:T(8,128)S(1)}, f32[16,1280]{1,0:T(8,128)S(1)}, u32[]{:S(2)}, u32[]{:S(2)}) collective-permute-start(f32[16,1280]{1,0:T(8,128)S(1)} %get-tuple-element.68), channel_id=1, source_target_pairs={{0,704},{1,705},{2,706},{3,707},{4,708},{5,709},{6,710},{7,711},{8... | collective-permute-start | bytes 245768 | tf_op jit(solution)/shard_map/ppermute | solution.py:332
  79.0 3.5 %collective-permute-done.13.face_second = f32[16,1280]{1,0:T(8,128)S(1)} collective-permute-done((f32[16,1280]{1,0:T(8,128)S(1)}, f32[16,1280]{1,0:T(8,128)S(1)}, u32[]{:S(2)}, u32[]{:S(2)}) %collective-permute-start.13) | collective-permute-done | bytes 81952 | tf_op jit(solution)/shard_map/ppermute | solution.py:332
  82.5 1.9 %collective-permute-start.14 = (f32[16,1280]{1,0:T(8,128)S(1)}, f32[16,1280]{1,0:T(8,128)S(1)}, u32[]{:S(2)}, u32[]{:S(2)}) collective-permute-start(f32[16,1280]{1,0:T(8,128)S(1)} %get-tuple-element.71), channel_id=1, source_target_pairs={{0,1},{1,0},{2,3},{3,2},{4,5},{5,4},{6,7},{7,6},{8,9},{9,8},{10,11... | collective-permute-start | bytes 245768 | tf_op jit(solution)/shard_map/ppermute | solution.py:332
  84.5 3.1 %collective-permute-start.15 = (f32[16,1280]{1,0:T(8,128)S(1)}, f32[16,1280]{1,0:T(8,128)S(1)}, u32[]{:S(2)}, u32[]{:S(2)}) collective-permute-start(f32[16,1280]{1,0:T(8,128)S(1)} %get-tuple-element.72), channel_id=1, source_target_pairs={{0,63},{1,2},{2,1},{3,4},{4,3},{5,6},{6,5},{7,8},{8,7},{9,10},{10,... | collective-permute-start | bytes 245768 | tf_op jit(solution)/shard_map/ppermute | solution.py:332
  87.7 5.9 %collective-permute-done.15.tile_second = f32[16,1280]{1,0:T(8,128)S(1)} collective-permute-done((f32[16,1280]{1,0:T(8,128)S(1)}, f32[16,1280]{1,0:T(8,128)S(1)}, u32[]{:S(2)}, u32[]{:S(2)}) %collective-permute-start.15) | collective-permute-done | bytes 81952 | tf_op jit(solution)/shard_map/ppermute | solution.py:332
  (30 shorter events, 7.0 us)
Async XLA Ops:
  0.0 27.3 %copy-start = (f32[2,4,4,16,16]{4,3,2,1,0:T(8,128)S(1)}, f32[2,4,4,16,16]{4,3,2,1,0:T(8,128)}, u32[]{:S(2)}) copy-start(f32[2,4,4,16,16]{4,3,2,1,0:T(8,128)} %param.6) | copy-start | bytes 98308
  0.0 27.6 %copy-start.2 = (s32[2,4,4]{2,1,0:T(4,128)S(1)}, s32[2,4,4]{2,1,0:T(4,128)}, u32[]{:S(2)}) copy-start(s32[2,4,4]{2,1,0:T(4,128)} %slot.3) | copy-start | bytes 388
  0.0 27.6 %copy-start.1 = (s32[2,4,4]{2,1,0:T(4,128)S(1)}, s32[2,4,4]{2,1,0:T(4,128)}, u32[]{:S(2)}) copy-start(s32[2,4,4]{2,1,0:T(4,128)} %owner.3) | copy-start | bytes 388
  1.5 26.1 %collective-permute-start = (f32[4,16,1280]{2,1,0:T(8,128)S(1)}, f32[4,16,1280]{2,1,0:T(8,128)S(1)}, u32[]{:S(2)}, u32[]{:S(2)}) collective-permute-start(f32[4,16,1280]{2,1,0:T(8,128)S(1)} %get-tuple-element.40), channel_id=1, source_target_pairs={{0,704},{1,65},{2,706},{3,67},{4,708},{5,69},{6,710},{7,71},{8,712... | collective-permute-start | bytes 983048 | tf_op jit(solution)/shard_map/ppermute | solution.py:332
  5.8 21.8 %collective-permute-start.1 = (f32[4,16,1280]{2,1,0:T(8,128)S(1)}, f32[4,16,1280]{2,1,0:T(8,128)S(1)}, u32[]{:S(2)}, u32[]{:S(2)}) collective-permute-start(f32[4,16,1280]{2,1,0:T(8,128)S(1)} %get-tuple-element.41), channel_id=1, source_target_pairs={{0,1},{1,0},{2,3},{3,2},{4,5},{5,4},{6,7},{7,6},{8,9},{9,8},{10,11... | collective-permute-start | bytes 983048 | tf_op jit(solution)/shard_map/ppermute | solution.py:332
  7.7 19.9 %collective-permute-start.2 = (f32[4,16,1280]{2,1,0:T(8,128)S(1)}, f32[4,16,1280]{2,1,0:T(8,128)S(1)}, u32[]{:S(2)}, u32[]{:S(2)}) collective-permute-start(f32[4,16,1280]{2,1,0:T(8,128)S(1)} %get-tuple-element.42), channel_id=1, source_target_pairs={{0,63},{1,2},{2,1},{3,4},{4,3},{5,6},{6,5},{7,8},{8,7},{9,10},{10,... | collective-permute-start | bytes 983048 | tf_op jit(solution)/shard_map/ppermute | solution.py:332
  15.4 16.9 %collective-permute-start.3 = (f32[4,16,1280]{2,1,0:T(8,128)S(1)}, f32[4,16,1280]{2,1,0:T(8,128)S(1)}, u32[]{:S(2)}, u32[]{:S(2)}) collective-permute-start(f32[4,16,1280]{2,1,0:T(8,128)S(1)} %get-tuple-element.47), channel_id=1, source_target_pairs={{0,64},{1,705},{2,66},{3,707},{4,68},{5,709},{6,70},{7,711},{8,72}... | collective-permute-start | bytes 983048 | tf_op jit(solution)/shard_map/ppermute | solution.py:332
  32.7 6.7 %collective-permute-start.4 = (f32[16,1280]{1,0:T(8,128)S(1)}, f32[16,1280]{1,0:T(8,128)S(1)}, u32[]{:S(2)}, u32[]{:S(2)}) collective-permute-start(f32[16,1280]{1,0:T(8,128)S(1)} %get-tuple-element.52), channel_id=1, source_target_pairs={{0,64},{1,65},{2,66},{3,67},{4,68},{5,69},{6,70},{7,71},{8,72},{9,... | collective-permute-start | bytes 245768 | tf_op jit(solution)/shard_map/ppermute | solution.py:332
  36.6 6.3 %collective-permute-start.5 = (f32[16,1280]{1,0:T(8,128)S(1)}, f32[16,1280]{1,0:T(8,128)S(1)}, u32[]{:S(2)}, u32[]{:S(2)}) collective-permute-start(f32[16,1280]{1,0:T(8,128)S(1)} %get-tuple-element.53), channel_id=1, source_target_pairs={{0,704},{1,705},{2,706},{3,707},{4,708},{5,709},{6,710},{7,711},{8... | collective-permute-start | bytes 245768 | tf_op jit(solution)/shard_map/ppermute | solution.py:332
  43.0 6.7 %collective-permute-start.6 = (f32[16,1280]{1,0:T(8,128)S(1)}, f32[16,1280]{1,0:T(8,128)S(1)}, u32[]{:S(2)}, u32[]{:S(2)}) collective-permute-start(f32[16,1280]{1,0:T(8,128)S(1)} %get-tuple-element.56), channel_id=1, source_target_pairs={{0,1},{1,0},{2,3},{3,2},{4,5},{5,4},{6,7},{7,6},{8,9},{9,8},{10,11... | collective-permute-start | bytes 245768 | tf_op jit(solution)/shard_map/ppermute | solution.py:332
  44.9 9.1 %collective-permute-start.7 = (f32[16,1280]{1,0:T(8,128)S(1)}, f32[16,1280]{1,0:T(8,128)S(1)}, u32[]{:S(2)}, u32[]{:S(2)}) collective-permute-start(f32[16,1280]{1,0:T(8,128)S(1)} %get-tuple-element.57), channel_id=1, source_target_pairs={{0,63},{1,2},{2,1},{3,4},{4,3},{5,6},{6,5},{7,8},{8,7},{9,10},{10,... | collective-permute-start | bytes 245768 | tf_op jit(solution)/shard_map/ppermute | solution.py:332
  54.3 11.5 %collective-permute-start.8 = (f32[4,16,1280]{2,1,0:T(8,128)S(1)}, f32[4,16,1280]{2,1,0:T(8,128)S(1)}, u32[]{:S(2)}, u32[]{:S(2)}) collective-permute-start(f32[4,16,1280]{2,1,0:T(8,128)S(1)} %get-tuple-element.58), channel_id=1, source_target_pairs={{0,704},{1,65},{2,706},{3,67},{4,708},{5,69},{6,710},{7,71},{8,712... | collective-permute-start | bytes 983048 | tf_op jit(solution)/shard_map/ppermute | solution.py:332
  56.2 9.6 %collective-permute-start.9 = (f32[4,16,1280]{2,1,0:T(8,128)S(1)}, f32[4,16,1280]{2,1,0:T(8,128)S(1)}, u32[]{:S(2)}, u32[]{:S(2)}) collective-permute-start(f32[4,16,1280]{2,1,0:T(8,128)S(1)} %get-tuple-element.59), channel_id=1, source_target_pairs={{0,1},{1,0},{2,3},{3,2},{4,5},{5,4},{6,7},{7,6},{8,9},{9,8},{10,11... | collective-permute-start | bytes 983048 | tf_op jit(solution)/shard_map/ppermute | solution.py:332
  58.1 11.7 %collective-permute-start.10 = (f32[4,16,1280]{2,1,0:T(8,128)S(1)}, f32[4,16,1280]{2,1,0:T(8,128)S(1)}, u32[]{:S(2)}, u32[]{:S(2)}) collective-permute-start(f32[4,16,1280]{2,1,0:T(8,128)S(1)} %get-tuple-element.60), channel_id=1, source_target_pairs={{0,63},{1,2},{2,1},{3,4},{4,3},{5,6},{6,5},{7,8},{8,7},{9,10},{10,... | collective-permute-start | bytes 983048 | tf_op jit(solution)/shard_map/ppermute | solution.py:332
  62.6 9.0 %collective-permute-start.11 = (f32[4,16,1280]{2,1,0:T(8,128)S(1)}, f32[4,16,1280]{2,1,0:T(8,128)S(1)}, u32[]{:S(2)}, u32[]{:S(2)}) collective-permute-start(f32[4,16,1280]{2,1,0:T(8,128)S(1)} %get-tuple-element.62), channel_id=1, source_target_pairs={{0,64},{1,705},{2,66},{3,707},{4,68},{5,709},{6,70},{7,711},{8,72}... | collective-permute-start | bytes 983048 | tf_op jit(solution)/shard_map/ppermute | solution.py:332
  72.0 6.9 %collective-permute-start.12 = (f32[16,1280]{1,0:T(8,128)S(1)}, f32[16,1280]{1,0:T(8,128)S(1)}, u32[]{:S(2)}, u32[]{:S(2)}) collective-permute-start(f32[16,1280]{1,0:T(8,128)S(1)} %get-tuple-element.67), channel_id=1, source_target_pairs={{0,64},{1,65},{2,66},{3,67},{4,68},{5,69},{6,70},{7,71},{8,72},{9,... | collective-permute-start | bytes 245768 | tf_op jit(solution)/shard_map/ppermute | solution.py:332
  76.2 6.3 %collective-permute-start.13 = (f32[16,1280]{1,0:T(8,128)S(1)}, f32[16,1280]{1,0:T(8,128)S(1)}, u32[]{:S(2)}, u32[]{:S(2)}) collective-permute-start(f32[16,1280]{1,0:T(8,128)S(1)} %get-tuple-element.68), channel_id=1, source_target_pairs={{0,704},{1,705},{2,706},{3,707},{4,708},{5,709},{6,710},{7,711},{8... | collective-permute-start | bytes 245768 | tf_op jit(solution)/shard_map/ppermute | solution.py:332
  82.5 5.1 %collective-permute-start.14 = (f32[16,1280]{1,0:T(8,128)S(1)}, f32[16,1280]{1,0:T(8,128)S(1)}, u32[]{:S(2)}, u32[]{:S(2)}) collective-permute-start(f32[16,1280]{1,0:T(8,128)S(1)} %get-tuple-element.71), channel_id=1, source_target_pairs={{0,1},{1,0},{2,3},{3,2},{4,5},{5,4},{6,7},{7,6},{8,9},{9,8},{10,11... | collective-permute-start | bytes 245768 | tf_op jit(solution)/shard_map/ppermute | solution.py:332
  84.5 9.1 %collective-permute-start.15 = (f32[16,1280]{1,0:T(8,128)S(1)}, f32[16,1280]{1,0:T(8,128)S(1)}, u32[]{:S(2)}, u32[]{:S(2)}) collective-permute-start(f32[16,1280]{1,0:T(8,128)S(1)} %get-tuple-element.72), channel_id=1, source_target_pairs={{0,63},{1,2},{2,1},{3,4},{4,3},{5,6},{6,5},{7,8},{8,7},{9,10},{10,... | collective-permute-start | bytes 245768 | tf_op jit(solution)/shard_map/ppermute | solution.py:332

commit v5 on v4

--- a/solution.py
+++ b/solution.py
@@ -45,7 +45,7 @@
 
 
 def directions():
-    return odd("mixed"), 1 - odd("mixed"), 2 + odd("tile"), 3 - odd("tile")
+    return odd("face"), 1 - odd("face"), 2 + odd("tile"), 3 - odd("tile")
 
 
 def first_gather(lists, field, face_first, face_second, tile_first, tile_second, held, table, list_sem, sem):
@@ -100,7 +100,7 @@
 
 def move_most(step, owner, slot, field, early_a, early_b, early_c, high, low, joined,
               moved, far_weights, is_far, source, split_high, split_low):
-    owners = [2 - odd("mixed"), 1 + odd("mixed"), 4 - odd("tile"), 3 + odd("tile")]
+    owners = [2 - odd("face"), 1 + odd("face"), 4 - odd("tile"), 3 + odd("tile")]
     far = owners.pop(LAST)
     target = [jnp.int32(-1)] * CAP
     for e in range(ELEMS):
@@ -325,9 +325,12 @@
     pairs = []
     for f in range(faces):
         for t in range(tiles):
-            parity = {"face": f, "mixed": f + t, "tile": t}[axis]
-            step = 1 if (parity + slot) % 2 == 0 else -1
-            target = f * tiles + (t + step) % tiles if axis == "tile" else (f + step) % faces * tiles + t
+            if axis == "face":
+                step = 1 if (f + t + slot) % 2 == 0 else -1
+                target = (f + step) % faces * tiles + t
+            else:
+                step = 1 if (t + slot) % 2 == 0 else -1
+                target = f * tiles + (t + step) % tiles
             pairs.append((f * tiles + t, target))
     return lax.ppermute(x, ("face", "tile"), pairs)
 
@@ -337,8 +340,8 @@
 
 
 def odd(axis):
-    place = lax.axis_index("face" if axis == "face" else "tile")
-    if axis == "mixed":
+    place = lax.axis_index("tile")
+    if axis == "face":
         place += lax.axis_index("face")
     return lax.rem(place, 2)
 
@@ -369,7 +372,7 @@
     *sends, field = run(first_gather, [HBM, HBM], [listed] * 4 + [block], 1, [table, dma, dma], lists_hbm, field_hbm)
     high, low, joined = run(spread_weights, [VMEM], [mats, mats, own], 1, [], weights)
     for step in range(steps):
-        face = swaps("mixed", sends[0], sends[1])
+        face = swaps("face", sends[0], sends[1])
         tile = swaps("tile", sends[2], sends[3])
         if step < steps - 1:
             upcoming = run(functools.partial(read_lists, step + 1), [HBM], own_lists, 1, [table, dma], lists_hbm)

time: 95.3 us -> 95.3 us (level)
  transfers between devices with their start and end apart: 16 -> 16, of which waited for: 7 -> 6; matrix products, arithmetic and copies ran while one was open for 0% -> 0% of each run, Pallas kernels for 7% -> 7%
where the time goes in v5:
time: 95.3 us; the launch traced here: 94.7 us
  starting transfers between devices  59.3 us (62%)
  waiting for transfers between devices  24.8 us (26%)
  Pallas kernels  10.3 us (11%)
    ppermute x16, starting transfers between devices, swap(): return lax.ppermute(x, ('face', 'tile'), pairs)  59.3 us
    ppermute x16, waiting for transfers between devices, swap(): return lax.ppermute(x, ('face', 'tile'), pairs)  24.8 us
    pallas_call x16, Pallas kernels, run(): pl.pallas_call(kernel, out_shape=out, in_specs=in_specs, out_specs=out_sp...  10.3 us
  transfers between devices with their start and end apart: 16, of which 6 were waited for; matrix products, arithmetic and copies ran while one was open for 0% of the time, Pallas kernels for 7%

profile of v5, /device:TPU:64, one launch (start us, length us, event | category | flops | bytes accessed | tf_op | source)
XLA Modules:
  0.0 94.7 jit_solution(14553617436296985040)
XLA Ops:
  1.5 4.3 %collective-permute-start = (f32[4,16,1280]{2,1,0:T(8,128)S(1)}, f32[4,16,1280]{2,1,0:T(8,128)S(1)}, u32[]{:S(2)}, u32[]{:S(2)}) collective-permute-start(f32[4,16,1280]{2,1,0:T(8,128)S(1)} %get-tuple-element.40), channel_id=1, source_target_pairs={{0,704},{1,65},{2,706},{3,67},{4,708},{5,69},{6,710},{7,71},{8,712... | collective-permute-start | bytes 983048 | tf_op jit(solution)/shard_map/ppermute | solution.py:335
  5.8 1.9 %collective-permute-start.1 = (f32[4,16,1280]{2,1,0:T(8,128)S(1)}, f32[4,16,1280]{2,1,0:T(8,128)S(1)}, u32[]{:S(2)}, u32[]{:S(2)}) collective-permute-start(f32[4,16,1280]{2,1,0:T(8,128)S(1)} %get-tuple-element.41), channel_id=1, source_target_pairs={{0,1},{1,0},{2,3},{3,2},{4,5},{5,4},{6,7},{7,6},{8,9},{9,8},{10,11... | collective-permute-start | bytes 983048 | tf_op jit(solution)/shard_map/ppermute | solution.py:335
  7.7 7.7 %collective-permute-start.2 = (f32[4,16,1280]{2,1,0:T(8,128)S(1)}, f32[4,16,1280]{2,1,0:T(8,128)S(1)}, u32[]{:S(2)}, u32[]{:S(2)}) collective-permute-start(f32[4,16,1280]{2,1,0:T(8,128)S(1)} %get-tuple-element.42), channel_id=1, source_target_pairs={{0,63},{1,2},{2,1},{3,4},{4,3},{5,6},{6,5},{7,8},{8,7},{9,10},{10,... | collective-permute-start | bytes 983048 | tf_op jit(solution)/shard_map/ppermute | solution.py:335
  15.4 11.9 %collective-permute-start.3 = (f32[4,16,1280]{2,1,0:T(8,128)S(1)}, f32[4,16,1280]{2,1,0:T(8,128)S(1)}, u32[]{:S(2)}, u32[]{:S(2)}) collective-permute-start(f32[4,16,1280]{2,1,0:T(8,128)S(1)} %get-tuple-element.47), channel_id=1, source_target_pairs={{0,64},{1,705},{2,66},{3,707},{4,68},{5,709},{6,70},{7,711},{8,72}... | collective-permute-start | bytes 983048 | tf_op jit(solution)/shard_map/ppermute | solution.py:335
  27.6 1.7 %shard_map.57 = (f32[16,16,1280]{2,1,0:T(8,128)S(1)}, bf16[4,16,48]{2,1,0:T(8,128)(2,1)S(1)}, f32[64,128]{1,0:T(8,128)S(1)}) custom-call(s32[2,4,4]{2,1,0:T(4,128)S(1)} %copy-done.1, s32[2,4,4]{2,1,0:T(4,128)S(1)} %copy-done.2, f32[16,16,1280]{2,1,0:T(8,128)S(1)} %get-tuple-element.39.field, f32[4,16,1280]{2,1,0:T(8,128)S(1)} %collective-permute-done.early_a, ...), custom_call_target="tpu_custom_call" | custom-call | bytes 5242880 | tf_op jit(solution)/shard_map/pallas_call | solution.py:23
  29.3 2.9 %collective-permute-done.3.arrived = f32[4,16,1280]{2,1,0:T(8,128)S(1)} collective-permute-done((f32[4,16,1280]{2,1,0:T(8,128)S(1)}, f32[4,16,1280]{2,1,0:T(8,128)S(1)}, u32[]{:S(2)}, u32[]{:S(2)}) %collective-permute-start.3) | collective-permute-done | bytes 327712 | tf_op jit(solution)/shard_map/ppermute | solution.py:335
  32.7 3.9 %collective-permute-start.4 = (f32[16,1280]{1,0:T(8,128)S(1)}, f32[16,1280]{1,0:T(8,128)S(1)}, u32[]{:S(2)}, u32[]{:S(2)}) collective-permute-start(f32[16,1280]{1,0:T(8,128)S(1)} %get-tuple-element.52), channel_id=1, source_target_pairs={{0,64},{1,705},{2,66},{3,707},{4,68},{5,709},{6,70},{7,711},{8,72}... | collective-permute-start | bytes 245768 | tf_op jit(solution)/shard_map/ppermute | solution.py:335
  36.6 1.9 %collective-permute-start.5 = (f32[16,1280]{1,0:T(8,128)S(1)}, f32[16,1280]{1,0:T(8,128)S(1)}, u32[]{:S(2)}, u32[]{:S(2)}) collective-permute-start(f32[16,1280]{1,0:T(8,128)S(1)} %get-tuple-element.53), channel_id=1, source_target_pairs={{0,704},{1,65},{2,706},{3,67},{4,708},{5,69},{6,710},{7,71},{8,712... | collective-permute-start | bytes 245768 | tf_op jit(solution)/shard_map/ppermute | solution.py:335
  39.4 3.5 %collective-permute-done.5.face_second = f32[16,1280]{1,0:T(8,128)S(1)} collective-permute-done((f32[16,1280]{1,0:T(8,128)S(1)}, f32[16,1280]{1,0:T(8,128)S(1)}, u32[]{:S(2)}, u32[]{:S(2)}) %collective-permute-start.5) | collective-permute-done | bytes 81952 | tf_op jit(solution)/shard_map/ppermute | solution.py:335
  43.0 1.9 %collective-permute-start.6 = (f32[16,1280]{1,0:T(8,128)S(1)}, f32[16,1280]{1,0:T(8,128)S(1)}, u32[]{:S(2)}, u32[]{:S(2)}) collective-permute-start(f32[16,1280]{1,0:T(8,128)S(1)} %get-tuple-element.56), channel_id=1, source_target_pairs={{0,1},{1,0},{2,3},{3,2},{4,5},{5,4},{6,7},{7,6},{8,9},{9,8},{10,11... | collective-permute-start | bytes 245768 | tf_op jit(solution)/shard_map/ppermute | solution.py:335
  44.9 3.4 %collective-permute-start.7 = (f32[16,1280]{1,0:T(8,128)S(1)}, f32[16,1280]{1,0:T(8,128)S(1)}, u32[]{:S(2)}, u32[]{:S(2)}) collective-permute-start(f32[16,1280]{1,0:T(8,128)S(1)} %get-tuple-element.57), channel_id=1, source_target_pairs={{0,63},{1,2},{2,1},{3,4},{4,3},{5,6},{6,5},{7,8},{8,7},{9,10},{10,... | collective-permute-start | bytes 245768 | tf_op jit(solution)/shard_map/ppermute | solution.py:335
  49.2 4.8 %collective-permute-done.7.tile_second = f32[16,1280]{1,0:T(8,128)S(1)} collective-permute-done((f32[16,1280]{1,0:T(8,128)S(1)}, f32[16,1280]{1,0:T(8,128)S(1)}, u32[]{:S(2)}, u32[]{:S(2)}) %collective-permute-start.7) | collective-permute-done | bytes 81952 | tf_op jit(solution)/shard_map/ppermute | solution.py:335
  54.3 1.9 %collective-permute-start.8 = (f32[4,16,1280]{2,1,0:T(8,128)S(1)}, f32[4,16,1280]{2,1,0:T(8,128)S(1)}, u32[]{:S(2)}, u32[]{:S(2)}) collective-permute-start(f32[4,16,1280]{2,1,0:T(8,128)S(1)} %get-tuple-element.58), channel_id=1, source_target_pairs={{0,704},{1,65},{2,706},{3,67},{4,708},{5,69},{6,710},{7,71},{8,712... | collective-permute-start | bytes 983048 | tf_op jit(solution)/shard_map/ppermute | solution.py:335
  56.2 1.9 %collective-permute-start.9 = (f32[4,16,1280]{2,1,0:T(8,128)S(1)}, f32[4,16,1280]{2,1,0:T(8,128)S(1)}, u32[]{:S(2)}, u32[]{:S(2)}) collective-permute-start(f32[4,16,1280]{2,1,0:T(8,128)S(1)} %get-tuple-element.59), channel_id=1, source_target_pairs={{0,1},{1,0},{2,3},{3,2},{4,5},{5,4},{6,7},{7,6},{8,9},{9,8},{10,11... | collective-permute-start | bytes 983048 | tf_op jit(solution)/shard_map/ppermute | solution.py:335
  58.1 4.3 %collective-permute-start.10 = (f32[4,16,1280]{2,1,0:T(8,128)S(1)}, f32[4,16,1280]{2,1,0:T(8,128)S(1)}, u32[]{:S(2)}, u32[]{:S(2)}) collective-permute-start(f32[4,16,1280]{2,1,0:T(8,128)S(1)} %get-tuple-element.60), channel_id=1, source_target_pairs={{0,63},{1,2},{2,1},{3,4},{4,3},{5,6},{6,5},{7,8},{8,7},{9,10},{10,... | collective-permute-start | bytes 983048 | tf_op jit(solution)/shard_map/ppermute | solution.py:335
  62.4 2.7 %collective-permute-start.11 = (f32[4,16,1280]{2,1,0:T(8,128)S(1)}, f32[4,16,1280]{2,1,0:T(8,128)S(1)}, u32[]{:S(2)}, u32[]{:S(2)}) collective-permute-start(f32[4,16,1280]{2,1,0:T(8,128)S(1)} %get-tuple-element.62), channel_id=1, source_target_pairs={{0,64},{1,705},{2,66},{3,707},{4,68},{5,709},{6,70},{7,711},{8,72}... | collective-permute-start | bytes 983048 | tf_op jit(solution)/shard_map/ppermute | solution.py:335
  65.3 4.5 %collective-permute-done.10.early_c = f32[4,16,1280]{2,1,0:T(8,128)S(1)} collective-permute-done((f32[4,16,1280]{2,1,0:T(8,128)S(1)}, f32[4,16,1280]{2,1,0:T(8,128)S(1)}, u32[]{:S(2)}, u32[]{:S(2)}) %collective-permute-start.10) | collective-permute-done | bytes 327712 | tf_op jit(solution)/shard_map/ppermute | solution.py:335
  69.8 1.7 %shard_map.65 = (f32[16,16,1280]{2,1,0:T(8,128)S(1)}, bf16[4,16,48]{2,1,0:T(8,128)(2,1)S(1)}, f32[64,128]{1,0:T(8,128)S(1)}) custom-call(s32[2,4,4]{2,1,0:T(4,128)S(1)} %copy-done.1, s32[2,4,4]{2,1,0:T(4,128)S(1)} %copy-done.2, f32[16,16,1280]{2,1,0:T(8,128)S(1)} %shard_map.62.field, f32[4,16,1280]{2,1,0:T(8,128)S(1)} %collective-permute-done.8.early_a, ...), custom_call_target="tpu_custom_call" | custom-call | bytes 5242880 | tf_op jit(solution)/shard_map/pallas_call | solution.py:23
  71.9 4.2 %collective-permute-start.12 = (f32[16,1280]{1,0:T(8,128)S(1)}, f32[16,1280]{1,0:T(8,128)S(1)}, u32[]{:S(2)}, u32[]{:S(2)}) collective-permute-start(f32[16,1280]{1,0:T(8,128)S(1)} %get-tuple-element.67), channel_id=1, source_target_pairs={{0,64},{1,705},{2,66},{3,707},{4,68},{5,709},{6,70},{7,711},{8,72}... | collective-permute-start | bytes 245768 | tf_op jit(solution)/shard_map/ppermute | solution.py:335
  76.2 1.9 %collective-permute-start.13 = (f32[16,1280]{1,0:T(8,128)S(1)}, f32[16,1280]{1,0:T(8,128)S(1)}, u32[]{:S(2)}, u32[]{:S(2)}) collective-permute-start(f32[16,1280]{1,0:T(8,128)S(1)} %get-tuple-element.68), channel_id=1, source_target_pairs={{0,704},{1,65},{2,706},{3,67},{4,708},{5,69},{6,710},{7,71},{8,712... | collective-permute-start | bytes 245768 | tf_op jit(solution)/shard_map/ppermute | solution.py:335
  79.0 3.5 %collective-permute-done.13.face_second = f32[16,1280]{1,0:T(8,128)S(1)} collective-permute-done((f32[16,1280]{1,0:T(8,128)S(1)}, f32[16,1280]{1,0:T(8,128)S(1)}, u32[]{:S(2)}, u32[]{:S(2)}) %collective-permute-start.13) | collective-permute-done | bytes 81952 | tf_op jit(solution)/shard_map/ppermute | solution.py:335
  82.5 1.9 %collective-permute-start.14 = (f32[16,1280]{1,0:T(8,128)S(1)}, f32[16,1280]{1,0:T(8,128)S(1)}, u32[]{:S(2)}, u32[]{:S(2)}) collective-permute-start(f32[16,1280]{1,0:T(8,128)S(1)} %get-tuple-element.71), channel_id=1, source_target_pairs={{0,1},{1,0},{2,3},{3,2},{4,5},{5,4},{6,7},{7,6},{8,9},{9,8},{10,11... | collective-permute-start | bytes 245768 | tf_op jit(solution)/shard_map/ppermute | solution.py:335
  84.5 3.5 %collective-permute-start.15 = (f32[16,1280]{1,0:T(8,128)S(1)}, f32[16,1280]{1,0:T(8,128)S(1)}, u32[]{:S(2)}, u32[]{:S(2)}) collective-permute-start(f32[16,1280]{1,0:T(8,128)S(1)} %get-tuple-element.72), channel_id=1, source_target_pairs={{0,63},{1,2},{2,1},{3,4},{4,3},{5,6},{6,5},{7,8},{8,7},{9,10},{10,... | collective-permute-start | bytes 245768 | tf_op jit(solution)/shard_map/ppermute | solution.py:335
  88.1 5.5 %collective-permute-done.15.tile_second = f32[16,1280]{1,0:T(8,128)S(1)} collective-permute-done((f32[16,1280]{1,0:T(8,128)S(1)}, f32[16,1280]{1,0:T(8,128)S(1)}, u32[]{:S(2)}, u32[]{:S(2)}) %collective-permute-start.15) | collective-permute-done | bytes 81952 | tf_op jit(solution)/shard_map/ppermute | solution.py:335
  (30 shorter events, 6.9 us)
Async XLA Ops:
  0.0 27.3 %copy-start = (f32[2,4,4,16,16]{4,3,2,1,0:T(8,128)S(1)}, f32[2,4,4,16,16]{4,3,2,1,0:T(8,128)}, u32[]{:S(2)}) copy-start(f32[2,4,4,16,16]{4,3,2,1,0:T(8,128)} %param.6) | copy-start | bytes 98308
  0.0 27.6 %copy-start.2 = (s32[2,4,4]{2,1,0:T(4,128)S(1)}, s32[2,4,4]{2,1,0:T(4,128)}, u32[]{:S(2)}) copy-start(s32[2,4,4]{2,1,0:T(4,128)} %slot.3) | copy-start | bytes 388
  0.0 27.6 %copy-start.1 = (s32[2,4,4]{2,1,0:T(4,128)S(1)}, s32[2,4,4]{2,1,0:T(4,128)}, u32[]{:S(2)}) copy-start(s32[2,4,4]{2,1,0:T(4,128)} %owner.3) | copy-start | bytes 388
  1.5 26.1 %collective-permute-start = (f32[4,16,1280]{2,1,0:T(8,128)S(1)}, f32[4,16,1280]{2,1,0:T(8,128)S(1)}, u32[]{:S(2)}, u32[]{:S(2)}) collective-permute-start(f32[4,16,1280]{2,1,0:T(8,128)S(1)} %get-tuple-element.40), channel_id=1, source_target_pairs={{0,704},{1,65},{2,706},{3,67},{4,708},{5,69},{6,710},{7,71},{8,712... | collective-permute-start | bytes 983048 | tf_op jit(solution)/shard_map/ppermute | solution.py:335
  5.8 21.8 %collective-permute-start.1 = (f32[4,16,1280]{2,1,0:T(8,128)S(1)}, f32[4,16,1280]{2,1,0:T(8,128)S(1)}, u32[]{:S(2)}, u32[]{:S(2)}) collective-permute-start(f32[4,16,1280]{2,1,0:T(8,128)S(1)} %get-tuple-element.41), channel_id=1, source_target_pairs={{0,1},{1,0},{2,3},{3,2},{4,5},{5,4},{6,7},{7,6},{8,9},{9,8},{10,11... | collective-permute-start | bytes 983048 | tf_op jit(solution)/shard_map/ppermute | solution.py:335
  7.7 19.9 %collective-permute-start.2 = (f32[4,16,1280]{2,1,0:T(8,128)S(1)}, f32[4,16,1280]{2,1,0:T(8,128)S(1)}, u32[]{:S(2)}, u32[]{:S(2)}) collective-permute-start(f32[4,16,1280]{2,1,0:T(8,128)S(1)} %get-tuple-element.42), channel_id=1, source_target_pairs={{0,63},{1,2},{2,1},{3,4},{4,3},{5,6},{6,5},{7,8},{8,7},{9,10},{10,... | collective-permute-start | bytes 983048 | tf_op jit(solution)/shard_map/ppermute | solution.py:335
  15.4 16.9 %collective-permute-start.3 = (f32[4,16,1280]{2,1,0:T(8,128)S(1)}, f32[4,16,1280]{2,1,0:T(8,128)S(1)}, u32[]{:S(2)}, u32[]{:S(2)}) collective-permute-start(f32[4,16,1280]{2,1,0:T(8,128)S(1)} %get-tuple-element.47), channel_id=1, source_target_pairs={{0,64},{1,705},{2,66},{3,707},{4,68},{5,709},{6,70},{7,711},{8,72}... | collective-permute-start | bytes 983048 | tf_op jit(solution)/shard_map/ppermute | solution.py:335
  32.7 6.7 %collective-permute-start.4 = (f32[16,1280]{1,0:T(8,128)S(1)}, f32[16,1280]{1,0:T(8,128)S(1)}, u32[]{:S(2)}, u32[]{:S(2)}) collective-permute-start(f32[16,1280]{1,0:T(8,128)S(1)} %get-tuple-element.52), channel_id=1, source_target_pairs={{0,64},{1,705},{2,66},{3,707},{4,68},{5,709},{6,70},{7,711},{8,72}... | collective-permute-start | bytes 245768 | tf_op jit(solution)/shard_map/ppermute | solution.py:335
  36.6 6.3 %collective-permute-start.5 = (f32[16,1280]{1,0:T(8,128)S(1)}, f32[16,1280]{1,0:T(8,128)S(1)}, u32[]{:S(2)}, u32[]{:S(2)}) collective-permute-start(f32[16,1280]{1,0:T(8,128)S(1)} %get-tuple-element.53), channel_id=1, source_target_pairs={{0,704},{1,65},{2,706},{3,67},{4,708},{5,69},{6,710},{7,71},{8,712... | collective-permute-start | bytes 245768 | tf_op jit(solution)/shard_map/ppermute | solution.py:335
  43.0 6.2 %collective-permute-start.6 = (f32[16,1280]{1,0:T(8,128)S(1)}, f32[16,1280]{1,0:T(8,128)S(1)}, u32[]{:S(2)}, u32[]{:S(2)}) collective-permute-start(f32[16,1280]{1,0:T(8,128)S(1)} %get-tuple-element.56), channel_id=1, source_target_pairs={{0,1},{1,0},{2,3},{3,2},{4,5},{5,4},{6,7},{7,6},{8,9},{9,8},{10,11... | collective-permute-start | bytes 245768 | tf_op jit(solution)/shard_map/ppermute | solution.py:335
  44.9 9.1 %collective-permute-start.7 = (f32[16,1280]{1,0:T(8,128)S(1)}, f32[16,1280]{1,0:T(8,128)S(1)}, u32[]{:S(2)}, u32[]{:S(2)}) collective-permute-start(f32[16,1280]{1,0:T(8,128)S(1)} %get-tuple-element.57), channel_id=1, source_target_pairs={{0,63},{1,2},{2,1},{3,4},{4,3},{5,6},{6,5},{7,8},{8,7},{9,10},{10,... | collective-permute-start | bytes 245768 | tf_op jit(solution)/shard_map/ppermute | solution.py:335
  54.3 11.0 %collective-permute-start.8 = (f32[4,16,1280]{2,1,0:T(8,128)S(1)}, f32[4,16,1280]{2,1,0:T(8,128)S(1)}, u32[]{:S(2)}, u32[]{:S(2)}) collective-permute-start(f32[4,16,1280]{2,1,0:T(8,128)S(1)} %get-tuple-element.58), channel_id=1, source_target_pairs={{0,704},{1,65},{2,706},{3,67},{4,708},{5,69},{6,710},{7,71},{8,712... | collective-permute-start | bytes 983048 | tf_op jit(solution)/shard_map/ppermute | solution.py:335
  56.2 9.1 %collective-permute-start.9 = (f32[4,16,1280]{2,1,0:T(8,128)S(1)}, f32[4,16,1280]{2,1,0:T(8,128)S(1)}, u32[]{:S(2)}, u32[]{:S(2)}) collective-permute-start(f32[4,16,1280]{2,1,0:T(8,128)S(1)} %get-tuple-element.59), channel_id=1, source_target_pairs={{0,1},{1,0},{2,3},{3,2},{4,5},{5,4},{6,7},{7,6},{8,9},{9,8},{10,11... | collective-permute-start | bytes 983048 | tf_op jit(solution)/shard_map/ppermute | solution.py:335
  58.1 11.7 %collective-permute-start.10 = (f32[4,16,1280]{2,1,0:T(8,128)S(1)}, f32[4,16,1280]{2,1,0:T(8,128)S(1)}, u32[]{:S(2)}, u32[]{:S(2)}) collective-permute-start(f32[4,16,1280]{2,1,0:T(8,128)S(1)} %get-tuple-element.60), channel_id=1, source_target_pairs={{0,63},{1,2},{2,1},{3,4},{4,3},{5,6},{6,5},{7,8},{8,7},{9,10},{10,... | collective-permute-start | bytes 983048 | tf_op jit(solution)/shard_map/ppermute | solution.py:335
  62.4 9.1 %collective-permute-start.11 = (f32[4,16,1280]{2,1,0:T(8,128)S(1)}, f32[4,16,1280]{2,1,0:T(8,128)S(1)}, u32[]{:S(2)}, u32[]{:S(2)}) collective-permute-start(f32[4,16,1280]{2,1,0:T(8,128)S(1)} %get-tuple-element.62), channel_id=1, source_target_pairs={{0,64},{1,705},{2,66},{3,707},{4,68},{5,709},{6,70},{7,711},{8,72}... | collective-permute-start | bytes 983048 | tf_op jit(solution)/shard_map/ppermute | solution.py:335
  71.9 7.0 %collective-permute-start.12 = (f32[16,1280]{1,0:T(8,128)S(1)}, f32[16,1280]{1,0:T(8,128)S(1)}, u32[]{:S(2)}, u32[]{:S(2)}) collective-permute-start(f32[16,1280]{1,0:T(8,128)S(1)} %get-tuple-element.67), channel_id=1, source_target_pairs={{0,64},{1,705},{2,66},{3,707},{4,68},{5,709},{6,70},{7,711},{8,72}... | collective-permute-start | bytes 245768 | tf_op jit(solution)/shard_map/ppermute | solution.py:335
  76.2 6.3 %collective-permute-start.13 = (f32[16,1280]{1,0:T(8,128)S(1)}, f32[16,1280]{1,0:T(8,128)S(1)}, u32[]{:S(2)}, u32[]{:S(2)}) collective-permute-start(f32[16,1280]{1,0:T(8,128)S(1)} %get-tuple-element.68), channel_id=1, source_target_pairs={{0,704},{1,65},{2,706},{3,67},{4,708},{5,69},{6,710},{7,71},{8,712... | collective-permute-start | bytes 245768 | tf_op jit(solution)/shard_map/ppermute | solution.py:335
  82.5 5.5 %collective-permute-start.14 = (f32[16,1280]{1,0:T(8,128)S(1)}, f32[16,1280]{1,0:T(8,128)S(1)}, u32[]{:S(2)}, u32[]{:S(2)}) collective-permute-start(f32[16,1280]{1,0:T(8,128)S(1)} %get-tuple-element.71), channel_id=1, source_target_pairs={{0,1},{1,0},{2,3},{3,2},{4,5},{5,4},{6,7},{7,6},{8,9},{9,8},{10,11... | collective-permute-start | bytes 245768 | tf_op jit(solution)/shard_map/ppermute | solution.py:335
  84.5 9.1 %collective-permute-start.15 = (f32[16,1280]{1,0:T(8,128)S(1)}, f32[16,1280]{1,0:T(8,128)S(1)}, u32[]{:S(2)}, u32[]{:S(2)}) collective-permute-start(f32[16,1280]{1,0:T(8,128)S(1)} %get-tuple-element.72), channel_id=1, source_target_pairs={{0,63},{1,2},{2,1},{3,4},{4,3},{5,6},{6,5},{7,8},{8,7},{9,10},{10,... | collective-permute-start | bytes 245768 | tf_op jit(solution)/shard_map/ppermute | solution.py:335
